TPU v7x, 256 devices: a whole 4x4x8 slice. The times are simulated.
256 devices in a mesh: dp: 8 (over x, core), rows: 32 (over y, z).
Axes of the slice: x: 4, y: 4, z: 8, core: 2. Of those that a mesh axis runs over, the one named last changes fastest.
Arguments:
- grads: bfloat16 [2, 4096, 14336], P(None, 'rows', 'dp'), may hold values from -64 to 64
- basis: bfloat16 [2, 4096, 512], P(None, 'rows'), may hold values from -0.09375 to 0.09375
- moment1: float32 [2, 512, 14336], P(None, 'rows', 'dp'), may hold values from -0.3 to 0.3
- moment2: float32 [2, 512, 14336], P(None, 'rows', 'dp'), may hold values from 0.001 to 0.03
- weights: bfloat16 [2, 4096, 14336], P(None, 'rows', 'dp'), may hold values from -0.09375 to 0.09375
Outputs:
- new_weights: bfloat16 [2, 4096, 14336], P(None, 'rows')
- new_moment1: float32 [2, 512, 14336], P(None, 'rows', 'dp')
- new_moment2: float32 [2, 512, 14336], P(None, 'rows', 'dp')
All inputs are finite; a program needn't handle non-finite values.
Results may differ from a plain program's by a relative error of at most 0.00115.
The roundings to bfloat16 on the way count: a program that leaves them out, or rounds other values in their place, can miss the bound.
Values may be sent and summed in bfloat16 or wider, within the bound.
No kernel may reach another device: no remote copies, remote signals or barrier semaphores. Data moves between devices by JAX's collectives and lax.ppermute only.
A program may use at most 64 MiB of HBM per device.

v0:
```python
import functools
import math

import jax
import jax.numpy as jnp
from jax import lax
from jax.experimental import pallas as pl
from jax.experimental.pallas import tpu as pltpu
from jax.sharding import Mesh
from jax.sharding import PartitionSpec as P


D = 4096
FF = 14336
MATS = 2
STEP = 10
F32 = jnp.float32
BF16 = jnp.bfloat16
VMEM = pl.BlockSpec(memory_space=pltpu.VMEM)
SMEM = pl.BlockSpec(memory_space=pltpu.SMEM)
ANY = pl.BlockSpec(memory_space=pl.ANY)
PARAMS = pltpu.CompilerParams(vmem_limit_bytes=20 * 2**20)


def shift(v, axis, k):
    n = lax.axis_size(axis)
    return lax.ppermute(v, axis, [(i, (i + k) % n) for i in range(n)])


def exchange(v, axis):
    return lax.all_to_all(v, axis, split_axis=0, concat_axis=0, tiled=True)


def cost(flops, size):
    return pl.CostEstimate(flops=int(flops), bytes_accessed=int(size), transcendentals=0)


def before(first, second):
    return lax.optimization_barrier((first, second))[1]


def project_kernel(at_ref, g_ref, own_ref, peer_ref, tile_ref, *refs):
    outs, basis_ref, total_ref = refs[:-2], refs[-2], refs[-1]
    x, core, y, z = (at_ref[i] for i in range(4))
    nx, nz, _, part, _ = own_ref.shape
    cols = g_ref.shape[2]
    ny = len(outs)
    width = outs[0].shape[-1]

    def gather(zz, _):
        e = lax.rem(z - zz + nz, nz)
        for m in range(MATS):
            for xa in range(nx):
                d = lax.rem(x - xa + nx, nx)
                ours, theirs = own_ref[d, e, m], peer_ref[d, e, m]
                basis_ref[m, zz, 2 * xa * part : (2 * xa + 1) * part] = jnp.where(
                    core == 0, ours, theirs
                )
                basis_ref[m, zz, (2 * xa + 1) * part : (2 * xa + 2) * part] = jnp.where(
                    core == 0, theirs, ours
                )
        return 0

    lax.fori_loop(0, nz, gather, 0)

    def multiply(m, _):
        left = jnp.concatenate([g_ref[zz, m] for zz in range(nz)], axis=1)
        right = basis_ref[m].reshape(left.shape[1], -1)
        total_ref[m] = jnp.dot(left, right, preferred_element_type=F32)
        return 0

    lax.fori_loop(0, MATS, multiply, 0)
    for m in range(MATS):
        for d in range(ny):
            start = pl.multiple_of(lax.rem(y + d, ny) * width, width)
            outs[d][m, :cols] = total_ref[m, :, pl.ds(start, width)]
            outs[d][m, cols:] = tile_ref[...]


def project(at, g, own, peer, tile, parts):
    nz, mats, cols, rows = g.shape
    rank = own.shape[-1]
    size = (mats, cols + tile.shape[0], rank // parts)
    return pl.pallas_call(
        project_kernel,
        out_shape=[jax.ShapeDtypeStruct(size, F32)] * parts,
        in_specs=[SMEM] + [VMEM] * 4,
        out_specs=[VMEM] * parts,
        scratch_shapes=[
            pltpu.VMEM((mats, nz, rows, rank), BF16),
            pltpu.VMEM((mats, cols, rank), F32),
        ],
        compiler_params=PARAMS,
        cost_estimate=cost(2 * mats * nz * cols * rows * rank, 4 * 2**20),
        name="project",
    )(at, g, own, peer, tile)


def moments_kernel(moments_ref, p0, p1, p2, p3, new_ref, *update_refs):
    nz, _, ranks, cols = moments_ref.shape
    limit = 1.0 * math.sqrt(MATS * D * FF)
    first_bias_correction = 1.0 - 0.9**STEP
    second_fix = 1.0 - 0.999**STEP
    spare = 256 - cols
    for m in range(MATS):
        summed = (p0[m] + p1[m]) + (p2[m] + p3[m])
        scale = limit / jnp.maximum(jnp.sqrt(summed[cols : cols + 1, 0:1]), limit)
        padded = jnp.concatenate([summed[:cols], jnp.zeros((spare, summed.shape[1]), F32)], axis=0)
        scaled = scale * jnp.transpose(padded)[:, :cols]
        first = 0.9 * moments_ref[:, m].reshape(nz * ranks, cols) + 0.1 * scaled
        second = 0.999 * moments_ref[:, MATS + m].reshape(nz * ranks, cols) + 0.001 * scaled * scaled
        new_ref[:, m] = first.reshape(nz, ranks, cols)
        new_ref[:, MATS + m] = second.reshape(nz, ranks, cols)
        update = first / first_bias_correction / (jnp.sqrt(second / second_fix) + 1e-08)
        wide = jnp.concatenate([update, jnp.zeros((update.shape[0], spare), F32)], axis=1)
        turned = jnp.transpose(wide)[:cols].astype(BF16)
        for z in range(nz):
            update_refs[m][z] = turned


def moments(held, parts):
    nz, _, ranks, cols = held.shape
    return pl.pallas_call(
        moments_kernel,
        out_shape=[jax.ShapeDtypeStruct(held.shape, F32)]
        + [jax.ShapeDtypeStruct((nz, cols, nz * ranks), BF16)] * MATS,
        in_specs=[VMEM] * 5,
        out_specs=[VMEM] * (1 + MATS),
        compiler_params=PARAMS,
        cost_estimate=cost(2e9, 2 * 2**20),
        name="moments",
    )(held, *parts)


def back_kernel(m, at_ref, basis_ref, w_ref, u0, u1, u2, u3, out_ref):
    y = at_ref[2]
    width = u0.shape[1]
    blocks = (u0, u1, u2, u3)
    n = len(blocks)
    total = None
    for d in range(0, n, 2):
        left = jnp.concatenate(
            [
                basis_ref[m, :, pl.ds(pl.multiple_of(lax.rem(y - e + n, n) * width, width), width)]
                for e in (d, d + 1)
            ],
            axis=1,
        )
        right = jnp.concatenate([blocks[d][...], blocks[d + 1][...]], axis=1)
        term = lax.dot_general(
            left, right, (((1,), (1,)), ((), ())), preferred_element_type=F32
        )
        total = term if total is None else total + term
    out_ref[...] = (w_ref[m].astype(F32) - 0.5 * total).astype(BF16)


def back(m, at, basis, w, blocks):
    _, rows, cols = w.shape
    return pl.pallas_call(
        functools.partial(back_kernel, m),
        out_shape=jax.ShapeDtypeStruct((rows, cols), BF16),
        in_specs=[SMEM] + [VMEM] * 6,
        out_specs=VMEM,
        compiler_params=PARAMS,
        cost_estimate=cost(2 * rows * cols * basis.shape[2], 3 * 2**20),
        name="back",
    )(at, basis, w, *blocks)


def place_kernel(m, spots, at_ref, *refs):
    n = len(spots)
    blocks, out_ref, sems = refs[:n], refs[-2], refs[-1]
    x, core = at_ref[0], at_ref[1]
    copies = []
    for i, (dx, across, row) in enumerate(spots):
        rows, width = blocks[i].shape
        owner = lax.rem(x + dx, 4) * 2 + (1 - core if across else core)
        start = pl.multiple_of(owner * width, 128)
        copies.append(
            pltpu.make_async_copy(
                blocks[i], out_ref.at[m, pl.ds(row, rows), pl.ds(start, width)], sems.at[i]
            )
        )
    for copy in copies:
        copy.start()
    for copy in copies:
        copy.wait()


def place(whole, shape, m, at, items):
    spots = [item[1:] for item in items]
    blocks = [item[0] for item in items]
    n = len(blocks)
    given = () if whole is None else (whole,)
    size = sum(2 * 2 * b.size for b in blocks)
    return pl.pallas_call(
        functools.partial(place_kernel, m, spots),
        out_shape=jax.ShapeDtypeStruct(shape, BF16),
        in_specs=[SMEM] + [VMEM] * n + [ANY] * len(given),
        out_specs=ANY,
        scratch_shapes=[pltpu.SemaphoreType.DMA((n,))],
        input_output_aliases={} if whole is None else {n + 1: 0},
        compiler_params=PARAMS,
        cost_estimate=cost(2e9, size),
        name="place",
    )(at, *blocks, *given)


def sum_over(tile, axis):
    n = lax.axis_size(axis)
    step = 1
    while step < n:
        tile = tile + lax.ppermute(tile, axis, [(i, i ^ step) for i in range(n)])
        step *= 2
    return tile


def step(grads, basis, moment1, moment2, weights):
    x, core = lax.axis_index("x"), lax.axis_index("core")
    y, z = lax.axis_index("y"), lax.axis_index("z")
    nx, nc, ny, nz = (lax.axis_size(a) for a in ("x", "core", "y", "z"))
    mats, rows, cols = grads.shape
    rank = basis.shape[2]
    part = rows // (nx * nc)
    ranks = rank // (ny * nz)
    at = jnp.stack([x, core, y, z])

    turned = jnp.swapaxes(grads, 1, 2).reshape(mats, nz, cols // nz, rows)
    mine = exchange(jnp.swapaxes(turned, 0, 1), "z")

    piece = lax.dynamic_slice_in_dim(basis, (x * nc + core) * part, part, axis=1)
    grad_wide = turned.astype(F32)
    tile = jnp.full((8, 128), jnp.sum(grad_wide * grad_wide), F32)
    tile = sum_over(sum_over(tile, "z"), "core")
    held = jnp.stack([piece] + [shift(piece, "z", k) for k in range(1, nz)])
    tile, held = lax.optimization_barrier((tile, held))
    tile = sum_over(tile, "x")
    own = jnp.stack([held] + [shift(held, "x", k) for k in range(1, nx)])
    tile, own = lax.optimization_barrier((tile, own))
    peer = shift(own, "core", 1)

    state = jnp.concatenate([moment1, moment2], axis=0).reshape(2 * mats, ranks, nz, cols // nz)
    state = exchange(before(mine, state.transpose(2, 0, 1, 3)), "z")

    parts = project(at, mine, own, peer, tile, ny)
    parts = [parts[0]] + [shift(parts[k], "y", k) for k in range(1, ny)]
    news, *updates = moments(state, parts)
    blocks = []
    for update in updates:
        block = exchange(update, "z").reshape(cols, nz * ranks)
        blocks.append([block] + [shift(block, "y", k) for k in range(1, ny)])

    news = before(blocks[-1][0], news)
    news = exchange(news, "z").transpose(1, 2, 0, 3).reshape(2, mats, ranks, cols)

    half = rows // 2
    shape = (mats, rows, cols * nx * nc)

    def put(whole, m, items):
        there = [(shift(b, "core", 1), dx, True, row) for b, dx, row in items]
        here = [(b, dx, False, row) for b, dx, row in items]
        return place(whole, shape, m, at, here + there)

    fresh = [back(m, at, basis, weights, blocks[m]) for m in range(mats)]
    near = [(shift(f, "x", 1), shift(f, "x", -1)) for f in fresh]
    whole = put(None, 0, [(fresh[0], 0, 0)])
    whole = put(whole, 0, [(near[0][0], 3, 0), (near[0][1], 1, 0)])
    for m in range(mats):
        left, right = near[m]
        if m:
            whole, left, right = lax.optimization_barrier((whole, left, right))
            whole = put(whole, m, [(fresh[m], 0, 0)])
            whole = put(whole, m, [(left, 3, 0), (right, 1, 0)])
        top, low = shift(left[:half], "x", 1), shift(right[half:], "x", -1)
        if m:
            whole, top, low = lax.optimization_barrier((whole, top, low))
        whole = put(whole, m, [(top, 2, 0), (low, 2, half)])
    return (whole, news[0], news[1])


def solution(mesh):
    finer = Mesh(mesh.devices.reshape(4, 2, 4, 8), ("x", "core", "y", "z"))
    dp, rows = ("x", "core"), ("y", "z")
    in_specs = (
        P(None, rows, dp),
        P(None, rows, None),
        P(None, rows, dp),
        P(None, rows, dp),
        P(None, rows, dp),
    )
    out_specs = (P(None, rows, None), P(None, rows, dp), P(None, rows, dp))
    return jax.shard_map(step, mesh=finer, in_specs=in_specs, out_specs=out_specs, check_vma=False)
```

profile of v0, /device:TPU:1, one launch (start us, length us, event | category | flops | bytes accessed | tf_op | source)
XLA Modules:
  0.0 230.3 jit_solution(1071391264014503783)
XLA Ops:
  0.7 1.6 copy.13
  4.0 2.5 %collective-permute-start = (f32[8,128]{1,0:T(8,128)S(1)}, f32[8,128]{1,0:T(8,128)S(1)}, u32[]{:S(2)}, u32[]{:S(2)}) collective-permute-start(f32[8,128]{1,0:T(8,128)S(1)} %broadcast_in_dim.3), channel_id=1, source_target_pairs={{0,1},{1,0},{2,3},{3,2},{4,5},{5,4},{6,7},{7,6},{8,9},{9,8},{10,11... | collective-permute-start | bytes 12296 | tf_op jit(solution)/shard_map/ppermute | solution.py:213
  8.2 3.1 %collective-permute-start.1 = (f32[8,128]{1,0:T(8,128)S(1)}, f32[8,128]{1,0:T(8,128)S(1)}, u32[]{:S(2)}, u32[]{:S(2)}) collective-permute-start(f32[8,128]{1,0:T(8,128)S(1)} %broadcast_add_fusion), channel_id=1, source_target_pairs={{0,2},{1,3},{2,0},{3,1},{4,6},{5,7},{6,4},{7,5},{8,10},{9,11},{10,... | collective-permute-start | bytes 12296 | tf_op jit(solution)/shard_map/ppermute | solution.py:213
  14.1 5.0 %collective-permute-start.2 = (f32[8,128]{1,0:T(8,128)S(1)}, f32[8,128]{1,0:T(8,128)S(1)}, u32[]{:S(2)}, u32[]{:S(2)}) collective-permute-start(f32[8,128]{1,0:T(8,128)S(1)} %fusion.1), channel_id=1, source_target_pairs={{0,4},{1,5},{2,6},{3,7},{4,0},{5,1},{6,2},{7,3},{8,12},{9,13},{10,... | collective-permute-start | bytes 12296 | tf_op jit(solution)/shard_map/ppermute | solution.py:213
  19.1 1.6 collective-permute-done.2
  20.7 3.7 %collective-permute-start.3 = (f32[8,128]{1,0:T(8,128)S(1)}, f32[8,128]{1,0:T(8,128)S(1)}, u32[]{:S(2)}, u32[]{:S(2)}) collective-permute-start(f32[8,128]{1,0:T(8,128)S(1)} %add.26), channel_id=1, source_target_pairs={{0,32},{32,0},{1,33},{33,1},{2,34},{34,2},{3,35},{35,3},{4,36},{36... | collective-permute-start | bytes 12296 | tf_op jit(solution)/shard_map/ppermute | solution.py:213
  25.7 4.7 %collective-permute-start.6 = (bf16[2,16,512]{2,1,0:T(8,128)(2,1)S(1)}, bf16[2,16,512]{2,1,0:T(8,128)(2,1)S(1)}, u32[]{:S(2)}, u32[]{:S(2)}) collective-permute-start(bf16[2,16,512]{2,1,0:T(8,128)(2,1)S(1)} %get-tuple-element.42), channel_id=1, source_target_pairs={{0,3},{1,4},{2,5},{3,6},{4,7},{5,0},{6,1},{7,2},{8,11},{9,12},{10,... | collective-permute-start | bytes 98312 | tf_op jit(solution)/shard_map/ppermute | solution.py:27
  32.2 5.7 %all-to-all-start = ((bf16[8,2,224,128]{3,2,1,0:T(8,128)(2,1)}), bf16[8,2,224,128]{3,2,1,0:T(8,128)(2,1)S(1)}, u32[]{:S(2)}, u32[]{:S(2)}) async-start(bf16[8,2,224,128]{3,2,1,0:T(8,128)(2,1)} %bitcast.39), calls=%async_computation | async-start | bytes 1835008 | tf_op jit(solution)/shard_map/all_to_all | solution.py:31
  38.0 4.5 %collective-permute-start.8 = (bf16[2,16,512]{2,1,0:T(8,128)(2,1)S(1)}, bf16[2,16,512]{2,1,0:T(8,128)(2,1)S(1)}, u32[]{:S(2)}, u32[]{:S(2)}) collective-permute-start(bf16[2,16,512]{2,1,0:T(8,128)(2,1)S(1)} %get-tuple-element.42), channel_id=1, source_target_pairs={{0,5},{1,6},{2,7},{3,0},{4,1},{5,2},{6,3},{7,4},{8,13},{9,14},{10,... | collective-permute-start | bytes 98312 | tf_op jit(solution)/shard_map/ppermute | solution.py:27
  44.0 14.3 %collective-permute-done.8 = bf16[2,16,512]{2,1,0:T(8,128)(2,1)S(1)} collective-permute-done((bf16[2,16,512]{2,1,0:T(8,128)(2,1)S(1)}, bf16[2,16,512]{2,1,0:T(8,128)(2,1)S(1)}, u32[]{:S(2)}, u32[]{:S(2)}) %collective-permute-start.8) | collective-permute-done | bytes 32800 | tf_op jit(solution)/shard_map/ppermute | solution.py:27
  58.3 4.0 %collective-permute-done.10 = bf16[2,16,512]{2,1,0:T(8,128)(2,1)S(1)} collective-permute-done((bf16[2,16,512]{2,1,0:T(8,128)(2,1)S(1)}, bf16[2,16,512]{2,1,0:T(8,128)(2,1)S(1)}, u32[]{:S(2)}, u32[]{:S(2)}) %collective-permute-start.10) | collective-permute-done | bytes 32800 | tf_op jit(solution)/shard_map/ppermute | solution.py:27
  62.3 2.5 %collective-permute-start.15 = (bf16[8,2,16,512]{3,2,1,0:T(8,128)(2,1)S(1)}, bf16[8,2,16,512]{3,2,1,0:T(8,128)(2,1)S(1)}, u32[]{:S(2)}, u32[]{:S(2)}) collective-permute-start(bf16[8,2,16,512]{3,2,1,0:T(8,128)(2,1)S(1)} %bitcast_dynamic-update-slice_fusion), channel_id=1, source_target_pairs={{0,192},{64,0},{128,64},{192,128},{1,193},{65,1},{129,65},{193,129... | collective-permute-start | bytes 786440 | tf_op jit(solution)/shard_map/ppermute | solution.py:27
  65.9 1.5 collective-permute-start.11
  67.4 6.2 %collective-permute-done.11 = f32[8,128]{1,0:T(8,128)S(1)} collective-permute-done((f32[8,128]{1,0:T(8,128)S(1)}, f32[8,128]{1,0:T(8,128)S(1)}, u32[]{:S(2)}, u32[]{:S(2)}) %collective-permute-start.11) | collective-permute-done | bytes 4128 | tf_op jit(solution)/shard_map/ppermute | solution.py:213
  73.5 2.5 %collective-permute-start.12 = (f32[8,128]{1,0:T(8,128)S(1)}, f32[8,128]{1,0:T(8,128)S(1)}, u32[]{:S(2)}, u32[]{:S(2)}) collective-permute-start(f32[8,128]{1,0:T(8,128)S(1)} %add.30), channel_id=1, source_target_pairs={{0,128},{64,192},{128,0},{192,64},{1,129},{65,193},{129,1},{193,65... | collective-permute-start | bytes 12296 | tf_op jit(solution)/shard_map/ppermute | solution.py:213
  76.0 1.6 collective-permute-done.12
  77.6 1.6 collective-permute-done.13
  79.3 3.8 %collective-permute-start.16 = (bf16[4,8,2,16,512]{4,3,2,1,0:T(8,128)(2,1)S(1)}, bf16[4,8,2,16,512]{4,3,2,1,0:T(8,128)(2,1)}, u32[]{:S(2)}, u32[]{:S(2)}) collective-permute-start(bf16[4,8,2,16,512]{4,3,2,1,0:T(8,128)(2,1)S(1)} %pad_maximum_fusion.own_ref), channel_id=1, source_target_pairs={{0,32},{32,0},{1,33},{33,1},{2,34},{34,2},{3,35},{35,3},{4,36},{36... | collective-permute-start | bytes 3145736 | tf_op jit(solution)/shard_map/ppermute | solution.py:27
  84.3 2.1 copy.21
  86.4 6.0 %all-to-all-start.1 = ((f32[8,4,16,224]{3,2,1,0:T(8,128)}), f32[8,4,16,224]{3,2,1,0:T(8,128)}, u32[]{:S(2)}, u32[]{:S(2)}) async-start(f32[8,4,16,224]{3,2,1,0:T(8,128)} %bitcast.50), calls=%async_computation.1 | async-start | bytes 1048576 | tf_op jit(solution)/shard_map/all_to_all | solution.py:31
  92.5 2.4 %project.1 = (f32[2,232,128]{2,1,0:T(8,128)S(1)}, f32[2,232,128]{2,1,0:T(8,128)S(1)}, f32[2,232,128]{2,1,0:T(8,128)S(1)}, f32[2,232,128]{2,1,0:T(8,128)S(1)}) custom-call(s32[4]{0:T(128)S(1)} %pad_add_fusion.at_ref, bf16[8,2,224,128]{3,2,1,0:T(8,128)(2,1)S(1)} %all-to-all-done.g_ref, bf16[4,8,2,16,512]{4,3,2,1,0:T(8,128)(2,1)S(1)} %pad_maximum_fusion.own_ref, ...), custom_call_target="tpu_custom_call" | custom-call | flops 469762048 | bytes 4194304 | tf_op jit(solution)/shard_map/project/pallas_call | solution.py:84
  96.3 2.6 %collective-permute-start.18 = (f32[2,232,128]{2,1,0:T(8,128)S(1)}, f32[2,232,128]{2,1,0:T(8,128)S(1)}, u32[]{:S(2)}, u32[]{:S(2)}) collective-permute-start(f32[2,232,128]{2,1,0:T(8,128)S(1)} %get-tuple-element.29), channel_id=1, source_target_pairs={{0,16},{8,24},{16,0},{24,8},{1,17},{9,25},{17,1},{25,9},{2,18},{10... | collective-permute-start | bytes 712712 | tf_op jit(solution)/shard_map/ppermute | solution.py:27
  100.0 3.5 %collective-permute-done.17.p1 = f32[2,232,128]{2,1,0:T(8,128)S(1)} collective-permute-done((f32[2,232,128]{2,1,0:T(8,128)S(1)}, f32[2,232,128]{2,1,0:T(8,128)S(1)}, u32[]{:S(2)}, u32[]{:S(2)}) %collective-permute-start.17) | collective-permute-done | bytes 237600 | tf_op jit(solution)/shard_map/ppermute | solution.py:27
  103.5 6.2 %collective-permute-done.18.p2 = f32[2,232,128]{2,1,0:T(8,128)S(1)} collective-permute-done((f32[2,232,128]{2,1,0:T(8,128)S(1)}, f32[2,232,128]{2,1,0:T(8,128)S(1)}, u32[]{:S(2)}, u32[]{:S(2)}) %collective-permute-start.18) | collective-permute-done | bytes 237600 | tf_op jit(solution)/shard_map/ppermute | solution.py:27
  110.6 2.2 moments.1
  112.8 19.4 %all_to_all.25 = bf16[8,224,128]{2,1,0:T(8,128)(2,1)S(1)} all-to-all(bf16[8,224,128]{2,1,0:T(8,128)(2,1)S(1)} %get-tuple-element.31), channel_id=1, replica_groups=mesh['x'=4,'core'=2,'y'=4,'z'=8] {'z'}, dimensions={0} | all-to-all | bytes 917504 | tf_op jit(solution)/shard_map/all_to_all | solution.py:31
  132.2 3.5 %all-to-all-start.3 = ((bf16[8,224,128]{2,1,0:T(8,128)(2,1)}), bf16[8,224,128]{2,1,0:T(8,128)(2,1)S(1)}, u32[]{:S(2)}, u32[]{:S(2)}) async-start(bf16[8,224,128]{2,1,0:T(8,128)(2,1)} %get-tuple-element.32), calls=%async_computation.3 | async-start | bytes 917504 | tf_op jit(solution)/shard_map/all_to_all | solution.py:31
  136.9 3.7 %collective-permute-start.21 = (bf16[1792,128]{1,0:T(8,128)(2,1)S(1)}, bf16[1792,128]{1,0:T(8,128)(2,1)S(1)}, u32[]{:S(2)}, u32[]{:S(2)}) collective-permute-start(bf16[1792,128]{1,0:T(8,128)(2,1)S(1)} %bitcast.46), channel_id=1, source_target_pairs={{0,16},{8,24},{16,0},{24,8},{1,17},{9,25},{17,1},{25,9},{2,18},{10... | collective-permute-start | bytes 1376264 | tf_op jit(solution)/shard_map/ppermute | solution.py:27
  140.7 7.9 %all-to-all-done.3 = bf16[8,224,128]{2,1,0:T(8,128)(2,1)S(1)} async-done(((bf16[8,224,128]{2,1,0:T(8,128)(2,1)}), bf16[8,224,128]{2,1,0:T(8,128)(2,1)S(1)}, u32[]{:S(2)}, u32[]{:S(2)}) %all-to-all-start.3) | async-done | bytes 458784 | tf_op jit(solution)/shard_map/all_to_all | solution.py:31
  149.6 9.5 %collective-permute-done.21.u2 = bf16[1792,128]{1,0:T(8,128)(2,1)S(1)} collective-permute-done((bf16[1792,128]{1,0:T(8,128)(2,1)S(1)}, bf16[1792,128]{1,0:T(8,128)(2,1)S(1)}, u32[]{:S(2)}, u32[]{:S(2)}) %collective-permute-start.21) | collective-permute-done | bytes 458784 | tf_op jit(solution)/shard_map/ppermute | solution.py:27
  161.0 1.8 back.2.refs_0_
  162.8 2.3 collective-permute-start.23
  167.0 2.9 %collective-permute-start.34 = (bf16[1792,128]{1,0:T(8,128)(2,1)S(1)}, bf16[1792,128]{1,0:T(8,128)(2,1)S(1)}, u32[]{:S(2)}, u32[]{:S(2)}) collective-permute-start(bf16[1792,128]{1,0:T(8,128)(2,1)S(1)} %bitcast.43), channel_id=1, source_target_pairs={{0,24},{8,0},{16,8},{24,16},{1,25},{9,1},{17,9},{25,17},{2,26},{10... | collective-permute-start | bytes 1376264 | tf_op jit(solution)/shard_map/ppermute | solution.py:27
  169.9 2.0 collective-permute-done.32.u1
  172.5 5.8 %collective-permute-start.29 = (bf16[128,1792]{1,0:T(8,128)(2,1)S(1)}, bf16[128,1792]{1,0:T(8,128)(2,1)S(1)}, u32[]{:S(2)}, u32[]{:S(2)}) collective-permute-start(bf16[128,1792]{1,0:T(8,128)(2,1)S(1)} %collective-permute-done.23.refs_0_), channel_id=1, source_target_pairs={{0,32},{32,0},{1,33},{33,1},{2,34},{34,2},{3,35},{35,3},{4,36},{36... | collective-permute-start | bytes 1376264 | tf_op jit(solution)/shard_map/ppermute | solution.py:27
  179.8 1.6 slice.27
  182.7 7.7 %collective-permute-done.34.u3 = bf16[1792,128]{1,0:T(8,128)(2,1)S(1)} collective-permute-done((bf16[1792,128]{1,0:T(8,128)(2,1)S(1)}, bf16[1792,128]{1,0:T(8,128)(2,1)S(1)}, u32[]{:S(2)}, u32[]{:S(2)}) %collective-permute-start.34) | collective-permute-done | bytes 458784 | tf_op jit(solution)/shard_map/ppermute | solution.py:27
  192.2 6.4 %all-to-all-start.4 = ((f32[8,4,16,224]{3,2,1,0:T(8,128)}), f32[8,4,16,224]{3,2,1,0:T(8,128)}, u32[]{:S(2)}, u32[]{:S(2)}) async-start(f32[8,4,16,224]{3,2,1,0:T(8,128)} %get-tuple-element.40), calls=%async_computation.4 | async-start | bytes 1048576 | tf_op jit(solution)/shard_map/all_to_all | solution.py:31
  202.4 2.3 %collective-permute-start.36 = (bf16[128,1792]{1,0:T(8,128)(2,1)S(1)}, bf16[128,1792]{1,0:T(8,128)(2,1)S(1)}, u32[]{:S(2)}, u32[]{:S(2)}) collective-permute-start(bf16[128,1792]{1,0:T(8,128)(2,1)S(1)} %back.3.refs_0_), channel_id=1, source_target_pairs={{0,192},{64,0},{128,64},{192,128},{1,193},{65,1},{129,65},{193,129... | collective-permute-start | bytes 1376264 | tf_op jit(solution)/shard_map/ppermute | solution.py:27
  204.7 2.9 %collective-permute-start.27 = (bf16[64,1792]{1,0:T(8,128)(2,1)}, bf16[64,1792]{1,0:T(8,128)(2,1)S(1)}, u32[]{:S(2)}, u32[]{:S(2)}) collective-permute-start(bf16[64,1792]{1,0:T(8,128)(2,1)} %collective-permute-done.24.refs_0_), channel_id=1, source_target_pairs={{0,32},{32,0},{1,33},{33,1},{2,34},{34,2},{3,35},{35,3},{4,36},{36... | collective-permute-start | bytes 688136 | tf_op jit(solution)/shard_map/ppermute | solution.py:27
  207.7 2.0 place.6.refs_4_
  210.2 2.4 %place.7.refs_4_ = bf16[2,128,14336]{2,1,0:T(8,128)(2,1)} custom-call(s32[4]{0:T(128)S(1)} %pad_add_fusion.at_ref, bf16[128,1792]{1,0:T(8,128)(2,1)S(1)} %collective-permute-done.23.refs_0_, bf16[128,1792]{1,0:T(8,128)(2,1)} %collective-permute-done.25.refs_1_, ...), custom_call_target="tpu_custom_call", output_to_operand_aliasing={{}: (5, {})} | custom-call | flops 2000000000 | bytes 3670016 | tf_op jit(solution)/shard_map/place/pallas_call | solution.py:196
  212.6 2.0 place.8.refs_2_
  214.7 1.5 collective-permute-start.37
  216.3 2.8 %collective-permute-start.41 = (bf16[64,1792]{1,0:T(8,128)(2,1)S(1)}, bf16[64,1792]{1,0:T(8,128)(2,1)S(1)}, u32[]{:S(2)}, u32[]{:S(2)}) collective-permute-start(bf16[64,1792]{1,0:T(8,128)(2,1)S(1)} %slice.23), channel_id=1, source_target_pairs={{0,192},{64,0},{128,64},{192,128},{1,193},{65,1},{129,65},{193,129... | collective-permute-start | bytes 688136 | tf_op jit(solution)/shard_map/ppermute | solution.py:27
  220.6 1.8 place.10.refs_4_
  222.4 1.8 collective-permute-done.40.refs_0_
  228.6 1.5 place.11
  (111 shorter events, 38.4 us)
Async XLA Ops:
  4.0 3.5 %collective-permute-start = (f32[8,128]{1,0:T(8,128)S(1)}, f32[8,128]{1,0:T(8,128)S(1)}, u32[]{:S(2)}, u32[]{:S(2)}) collective-permute-start(f32[8,128]{1,0:T(8,128)S(1)} %broadcast_in_dim.3), channel_id=1, source_target_pairs={{0,1},{1,0},{2,3},{3,2},{4,5},{5,4},{6,7},{7,6},{8,9},{9,8},{10,11... | collective-permute-start | bytes 12296 | tf_op jit(solution)/shard_map/ppermute | solution.py:213
  8.2 5.3 %collective-permute-start.1 = (f32[8,128]{1,0:T(8,128)S(1)}, f32[8,128]{1,0:T(8,128)S(1)}, u32[]{:S(2)}, u32[]{:S(2)}) collective-permute-start(f32[8,128]{1,0:T(8,128)S(1)} %broadcast_add_fusion), channel_id=1, source_target_pairs={{0,2},{1,3},{2,0},{3,1},{4,6},{5,7},{6,4},{7,5},{8,10},{9,11},{10,... | collective-permute-start | bytes 12296 | tf_op jit(solution)/shard_map/ppermute | solution.py:213
  12.0 30.4 %collective-permute-start.4 = (bf16[2,16,512]{2,1,0:T(8,128)(2,1)S(1)}, bf16[2,16,512]{2,1,0:T(8,128)(2,1)S(1)}, u32[]{:S(2)}, u32[]{:S(2)}) collective-permute-start(bf16[2,16,512]{2,1,0:T(8,128)(2,1)S(1)} %get-tuple-element.42), channel_id=1, source_target_pairs={{0,1},{1,2},{2,3},{3,4},{4,5},{5,6},{6,7},{7,0},{8,9},{9,10},{10,1... | collective-permute-start | bytes 98312 | tf_op jit(solution)/shard_map/ppermute | solution.py:27
  14.1 6.6 %collective-permute-start.2 = (f32[8,128]{1,0:T(8,128)S(1)}, f32[8,128]{1,0:T(8,128)S(1)}, u32[]{:S(2)}, u32[]{:S(2)}) collective-permute-start(f32[8,128]{1,0:T(8,128)S(1)} %fusion.1), channel_id=1, source_target_pairs={{0,4},{1,5},{2,6},{3,7},{4,0},{5,1},{6,2},{7,3},{8,12},{9,13},{10,... | collective-permute-start | bytes 12296 | tf_op jit(solution)/shard_map/ppermute | solution.py:213
  20.7 17.3 %collective-permute-start.3 = (f32[8,128]{1,0:T(8,128)S(1)}, f32[8,128]{1,0:T(8,128)S(1)}, u32[]{:S(2)}, u32[]{:S(2)}) collective-permute-start(f32[8,128]{1,0:T(8,128)S(1)} %add.26), channel_id=1, source_target_pairs={{0,32},{32,0},{1,33},{33,1},{2,34},{34,2},{3,35},{35,3},{4,36},{36... | collective-permute-start | bytes 12296 | tf_op jit(solution)/shard_map/ppermute | solution.py:213
  24.4 19.2 %collective-permute-start.5 = (bf16[2,16,512]{2,1,0:T(8,128)(2,1)S(1)}, bf16[2,16,512]{2,1,0:T(8,128)(2,1)S(1)}, u32[]{:S(2)}, u32[]{:S(2)}) collective-permute-start(bf16[2,16,512]{2,1,0:T(8,128)(2,1)S(1)} %get-tuple-element.42), channel_id=1, source_target_pairs={{0,2},{1,3},{2,4},{3,5},{4,6},{5,7},{6,0},{7,1},{8,10},{9,11},{10,... | collective-permute-start | bytes 98312 | tf_op jit(solution)/shard_map/ppermute | solution.py:27
  25.7 18.3 %collective-permute-start.6 = (bf16[2,16,512]{2,1,0:T(8,128)(2,1)S(1)}, bf16[2,16,512]{2,1,0:T(8,128)(2,1)S(1)}, u32[]{:S(2)}, u32[]{:S(2)}) collective-permute-start(bf16[2,16,512]{2,1,0:T(8,128)(2,1)S(1)} %get-tuple-element.42), channel_id=1, source_target_pairs={{0,3},{1,4},{2,5},{3,6},{4,7},{5,0},{6,1},{7,2},{8,11},{9,12},{10,... | collective-permute-start | bytes 98312 | tf_op jit(solution)/shard_map/ppermute | solution.py:27
  30.3 13.6 %collective-permute-start.7 = (bf16[2,16,512]{2,1,0:T(8,128)(2,1)S(1)}, bf16[2,16,512]{2,1,0:T(8,128)(2,1)S(1)}, u32[]{:S(2)}, u32[]{:S(2)}) collective-permute-start(bf16[2,16,512]{2,1,0:T(8,128)(2,1)S(1)} %get-tuple-element.42), channel_id=1, source_target_pairs={{0,4},{1,5},{2,6},{3,7},{4,0},{5,1},{6,2},{7,3},{8,12},{9,13},{10,... | collective-permute-start | bytes 98312 | tf_op jit(solution)/shard_map/ppermute | solution.py:27
  32.2 54.2 %all-to-all-start = ((bf16[8,2,224,128]{3,2,1,0:T(8,128)(2,1)}), bf16[8,2,224,128]{3,2,1,0:T(8,128)(2,1)S(1)}, u32[]{:S(2)}, u32[]{:S(2)}) async-start(bf16[8,2,224,128]{3,2,1,0:T(8,128)(2,1)} %bitcast.39), calls=%async_computation | async-start | bytes 1835008 | tf_op jit(solution)/shard_map/all_to_all | solution.py:31
  38.0 20.3 %collective-permute-start.8 = (bf16[2,16,512]{2,1,0:T(8,128)(2,1)S(1)}, bf16[2,16,512]{2,1,0:T(8,128)(2,1)S(1)}, u32[]{:S(2)}, u32[]{:S(2)}) collective-permute-start(bf16[2,16,512]{2,1,0:T(8,128)(2,1)S(1)} %get-tuple-element.42), channel_id=1, source_target_pairs={{0,5},{1,6},{2,7},{3,0},{4,1},{5,2},{6,3},{7,4},{8,13},{9,14},{10,... | collective-permute-start | bytes 98312 | tf_op jit(solution)/shard_map/ppermute | solution.py:27
  42.5 15.8 %collective-permute-start.9 = (bf16[2,16,512]{2,1,0:T(8,128)(2,1)S(1)}, bf16[2,16,512]{2,1,0:T(8,128)(2,1)S(1)}, u32[]{:S(2)}, u32[]{:S(2)}) collective-permute-start(bf16[2,16,512]{2,1,0:T(8,128)(2,1)S(1)} %get-tuple-element.42), channel_id=1, source_target_pairs={{0,6},{1,7},{2,0},{3,1},{4,2},{5,3},{6,4},{7,5},{8,14},{9,15},{10,... | collective-permute-start | bytes 98312 | tf_op jit(solution)/shard_map/ppermute | solution.py:27
  43.6 18.6 %collective-permute-start.10 = (bf16[2,16,512]{2,1,0:T(8,128)(2,1)S(1)}, bf16[2,16,512]{2,1,0:T(8,128)(2,1)S(1)}, u32[]{:S(2)}, u32[]{:S(2)}) collective-permute-start(bf16[2,16,512]{2,1,0:T(8,128)(2,1)S(1)} %get-tuple-element.42), channel_id=1, source_target_pairs={{0,7},{1,0},{2,1},{3,2},{4,3},{5,4},{6,5},{7,6},{8,15},{9,8},{10,9... | collective-permute-start | bytes 98312 | tf_op jit(solution)/shard_map/ppermute | solution.py:27
  62.3 15.3 %collective-permute-start.15 = (bf16[8,2,16,512]{3,2,1,0:T(8,128)(2,1)S(1)}, bf16[8,2,16,512]{3,2,1,0:T(8,128)(2,1)S(1)}, u32[]{:S(2)}, u32[]{:S(2)}) collective-permute-start(bf16[8,2,16,512]{3,2,1,0:T(8,128)(2,1)S(1)} %bitcast_dynamic-update-slice_fusion), channel_id=1, source_target_pairs={{0,192},{64,0},{128,64},{192,128},{1,193},{65,1},{129,65},{193,129... | collective-permute-start | bytes 786440 | tf_op jit(solution)/shard_map/ppermute | solution.py:27
  64.7 12.8 %collective-permute-start.14 = (bf16[8,2,16,512]{3,2,1,0:T(8,128)(2,1)S(1)}, bf16[8,2,16,512]{3,2,1,0:T(8,128)(2,1)S(1)}, u32[]{:S(2)}, u32[]{:S(2)}) collective-permute-start(bf16[8,2,16,512]{3,2,1,0:T(8,128)(2,1)S(1)} %bitcast_dynamic-update-slice_fusion), channel_id=1, source_target_pairs={{0,128},{64,192},{128,0},{192,64},{1,129},{65,193},{129,1},{193,65... | collective-permute-start | bytes 786440 | tf_op jit(solution)/shard_map/ppermute | solution.py:27
  65.3 13.9 %collective-permute-start.13 = (bf16[8,2,16,512]{3,2,1,0:T(8,128)(2,1)S(1)}, bf16[8,2,16,512]{3,2,1,0:T(8,128)(2,1)S(1)}, u32[]{:S(2)}, u32[]{:S(2)}) collective-permute-start(bf16[8,2,16,512]{3,2,1,0:T(8,128)(2,1)S(1)} %bitcast_dynamic-update-slice_fusion), channel_id=1, source_target_pairs={{0,64},{64,128},{128,192},{192,0},{1,65},{65,129},{129,193},{193,1... | collective-permute-start | bytes 786440 | tf_op jit(solution)/shard_map/ppermute | solution.py:27
  65.9 7.7 %collective-permute-start.11 = (f32[8,128]{1,0:T(8,128)S(1)}, f32[8,128]{1,0:T(8,128)S(1)}, u32[]{:S(2)}, u32[]{:S(2)}) collective-permute-start(f32[8,128]{1,0:T(8,128)S(1)} %add.27), channel_id=1, source_target_pairs={{0,64},{64,0},{128,192},{192,128},{1,65},{65,1},{129,193},{193,129... | collective-permute-start | bytes 12296 | tf_op jit(solution)/shard_map/ppermute | solution.py:213
  73.5 4.0 %collective-permute-start.12 = (f32[8,128]{1,0:T(8,128)S(1)}, f32[8,128]{1,0:T(8,128)S(1)}, u32[]{:S(2)}, u32[]{:S(2)}) collective-permute-start(f32[8,128]{1,0:T(8,128)S(1)} %add.30), channel_id=1, source_target_pairs={{0,128},{64,192},{128,0},{192,64},{1,129},{65,193},{129,1},{193,65... | collective-permute-start | bytes 12296 | tf_op jit(solution)/shard_map/ppermute | solution.py:213
  79.3 13.3 %collective-permute-start.16 = (bf16[4,8,2,16,512]{4,3,2,1,0:T(8,128)(2,1)S(1)}, bf16[4,8,2,16,512]{4,3,2,1,0:T(8,128)(2,1)}, u32[]{:S(2)}, u32[]{:S(2)}) collective-permute-start(bf16[4,8,2,16,512]{4,3,2,1,0:T(8,128)(2,1)S(1)} %pad_maximum_fusion.own_ref), channel_id=1, source_target_pairs={{0,32},{32,0},{1,33},{33,1},{2,34},{34,2},{3,35},{35,3},{4,36},{36... | collective-permute-start | bytes 3145736 | tf_op jit(solution)/shard_map/ppermute | solution.py:27
  86.4 24.2 %all-to-all-start.1 = ((f32[8,4,16,224]{3,2,1,0:T(8,128)}), f32[8,4,16,224]{3,2,1,0:T(8,128)}, u32[]{:S(2)}, u32[]{:S(2)}) async-start(f32[8,4,16,224]{3,2,1,0:T(8,128)} %bitcast.50), calls=%async_computation.1 | async-start | bytes 1048576 | tf_op jit(solution)/shard_map/all_to_all | solution.py:31
  94.9 8.6 %collective-permute-start.17 = (f32[2,232,128]{2,1,0:T(8,128)S(1)}, f32[2,232,128]{2,1,0:T(8,128)S(1)}, u32[]{:S(2)}, u32[]{:S(2)}) collective-permute-start(f32[2,232,128]{2,1,0:T(8,128)S(1)} %get-tuple-element.28), channel_id=1, source_target_pairs={{0,8},{8,16},{16,24},{24,0},{1,9},{9,17},{17,25},{25,1},{2,10},{10... | collective-permute-start | bytes 712712 | tf_op jit(solution)/shard_map/ppermute | solution.py:27
  96.3 13.4 %collective-permute-start.18 = (f32[2,232,128]{2,1,0:T(8,128)S(1)}, f32[2,232,128]{2,1,0:T(8,128)S(1)}, u32[]{:S(2)}, u32[]{:S(2)}) collective-permute-start(f32[2,232,128]{2,1,0:T(8,128)S(1)} %get-tuple-element.29), channel_id=1, source_target_pairs={{0,16},{8,24},{16,0},{24,8},{1,17},{9,25},{17,1},{25,9},{2,18},{10... | collective-permute-start | bytes 712712 | tf_op jit(solution)/shard_map/ppermute | solution.py:27
  98.9 10.8 %collective-permute-start.19 = (f32[2,232,128]{2,1,0:T(8,128)S(1)}, f32[2,232,128]{2,1,0:T(8,128)S(1)}, u32[]{:S(2)}, u32[]{:S(2)}) collective-permute-start(f32[2,232,128]{2,1,0:T(8,128)S(1)} %get-tuple-element.30), channel_id=1, source_target_pairs={{0,24},{8,0},{16,8},{24,16},{1,25},{9,1},{17,9},{25,17},{2,26},{10... | collective-permute-start | bytes 712712 | tf_op jit(solution)/shard_map/ppermute | solution.py:27
  132.2 16.4 %all-to-all-start.3 = ((bf16[8,224,128]{2,1,0:T(8,128)(2,1)}), bf16[8,224,128]{2,1,0:T(8,128)(2,1)S(1)}, u32[]{:S(2)}, u32[]{:S(2)}) async-start(bf16[8,224,128]{2,1,0:T(8,128)(2,1)} %get-tuple-element.32), calls=%async_computation.3 | async-start | bytes 917504 | tf_op jit(solution)/shard_map/all_to_all | solution.py:31
  135.7 14.0 %collective-permute-start.20 = (bf16[1792,128]{1,0:T(8,128)(2,1)S(1)}, bf16[1792,128]{1,0:T(8,128)(2,1)S(1)}, u32[]{:S(2)}, u32[]{:S(2)}) collective-permute-start(bf16[1792,128]{1,0:T(8,128)(2,1)S(1)} %bitcast.45), channel_id=1, source_target_pairs={{0,8},{8,16},{16,24},{24,0},{1,9},{9,17},{17,25},{25,1},{2,10},{10... | collective-permute-start | bytes 1376264 | tf_op jit(solution)/shard_map/ppermute | solution.py:27
  136.9 22.3 %collective-permute-start.21 = (bf16[1792,128]{1,0:T(8,128)(2,1)S(1)}, bf16[1792,128]{1,0:T(8,128)(2,1)S(1)}, u32[]{:S(2)}, u32[]{:S(2)}) collective-permute-start(bf16[1792,128]{1,0:T(8,128)(2,1)S(1)} %bitcast.46), channel_id=1, source_target_pairs={{0,16},{8,24},{16,0},{24,8},{1,17},{9,25},{17,1},{25,9},{2,18},{10... | collective-permute-start | bytes 1376264 | tf_op jit(solution)/shard_map/ppermute | solution.py:27
  140.7 19.3 %collective-permute-start.22 = (bf16[1792,128]{1,0:T(8,128)(2,1)S(1)}, bf16[1792,128]{1,0:T(8,128)(2,1)}, u32[]{:S(2)}, u32[]{:S(2)}) collective-permute-start(bf16[1792,128]{1,0:T(8,128)(2,1)S(1)} %bitcast.47), channel_id=1, source_target_pairs={{0,24},{8,0},{16,8},{24,16},{1,25},{9,1},{17,9},{25,17},{2,26},{10... | collective-permute-start | bytes 1376264 | tf_op jit(solution)/shard_map/ppermute | solution.py:27
  148.6 23.4 %collective-permute-start.32 = (bf16[1792,128]{1,0:T(8,128)(2,1)S(1)}, bf16[1792,128]{1,0:T(8,128)(2,1)S(1)}, u32[]{:S(2)}, u32[]{:S(2)}) collective-permute-start(bf16[1792,128]{1,0:T(8,128)(2,1)S(1)} %bitcast.41), channel_id=1, source_target_pairs={{0,8},{8,16},{16,24},{24,0},{1,9},{9,17},{17,25},{25,1},{2,10},{10... | collective-permute-start | bytes 1376264 | tf_op jit(solution)/shard_map/ppermute | solution.py:27
  162.8 9.8 %collective-permute-start.23 = (bf16[128,1792]{1,0:T(8,128)(2,1)S(1)}, bf16[128,1792]{1,0:T(8,128)(2,1)S(1)}, u32[]{:S(2)}, u32[]{:S(2)}) collective-permute-start(bf16[128,1792]{1,0:T(8,128)(2,1)S(1)} %back.2.refs_0_), channel_id=1, source_target_pairs={{0,64},{64,128},{128,192},{192,0},{1,65},{65,129},{129,193},{193,1... | collective-permute-start | bytes 1376264 | tf_op jit(solution)/shard_map/ppermute | solution.py:27
  165.0 13.3 %collective-permute-start.25 = (bf16[128,1792]{1,0:T(8,128)(2,1)S(1)}, bf16[128,1792]{1,0:T(8,128)(2,1)}, u32[]{:S(2)}, u32[]{:S(2)}) collective-permute-start(bf16[128,1792]{1,0:T(8,128)(2,1)S(1)} %back.2.refs_0_), channel_id=1, source_target_pairs={{0,192},{64,0},{128,64},{192,128},{1,193},{65,1},{129,65},{193,129... | collective-permute-start | bytes 1376264 | tf_op jit(solution)/shard_map/ppermute | solution.py:27
  166.4 15.0 %collective-permute-start.33 = (bf16[1792,128]{1,0:T(8,128)(2,1)S(1)}, bf16[1792,128]{1,0:T(8,128)(2,1)S(1)}, u32[]{:S(2)}, u32[]{:S(2)}) collective-permute-start(bf16[1792,128]{1,0:T(8,128)(2,1)S(1)} %bitcast.42), channel_id=1, source_target_pairs={{0,16},{8,24},{16,0},{24,8},{1,17},{9,25},{17,1},{25,9},{2,18},{10... | collective-permute-start | bytes 1376264 | tf_op jit(solution)/shard_map/ppermute | solution.py:27
  167.0 23.3 %collective-permute-start.34 = (bf16[1792,128]{1,0:T(8,128)(2,1)S(1)}, bf16[1792,128]{1,0:T(8,128)(2,1)S(1)}, u32[]{:S(2)}, u32[]{:S(2)}) collective-permute-start(bf16[1792,128]{1,0:T(8,128)(2,1)S(1)} %bitcast.43), channel_id=1, source_target_pairs={{0,24},{8,0},{16,8},{24,16},{1,25},{9,1},{17,9},{25,17},{2,26},{10... | collective-permute-start | bytes 1376264 | tf_op jit(solution)/shard_map/ppermute | solution.py:27
  171.9 30.0 %collective-permute-start.31 = (bf16[128,1792]{1,0:T(8,128)(2,1)S(1)}, bf16[128,1792]{1,0:T(8,128)(2,1)}, u32[]{:S(2)}, u32[]{:S(2)}) collective-permute-start(bf16[128,1792]{1,0:T(8,128)(2,1)S(1)} %back.2.refs_0_), channel_id=1, source_target_pairs={{0,32},{32,0},{1,33},{33,1},{2,34},{34,2},{3,35},{35,3},{4,36},{36... | collective-permute-start | bytes 1376264 | tf_op jit(solution)/shard_map/ppermute | solution.py:27
  172.5 35.1 %collective-permute-start.29 = (bf16[128,1792]{1,0:T(8,128)(2,1)S(1)}, bf16[128,1792]{1,0:T(8,128)(2,1)S(1)}, u32[]{:S(2)}, u32[]{:S(2)}) collective-permute-start(bf16[128,1792]{1,0:T(8,128)(2,1)S(1)} %collective-permute-done.23.refs_0_), channel_id=1, source_target_pairs={{0,32},{32,0},{1,33},{33,1},{2,34},{34,2},{3,35},{35,3},{4,36},{36... | collective-permute-start | bytes 1376264 | tf_op jit(solution)/shard_map/ppermute | solution.py:27
  178.3 31.4 %collective-permute-start.30 = (bf16[128,1792]{1,0:T(8,128)(2,1)}, bf16[128,1792]{1,0:T(8,128)(2,1)}, u32[]{:S(2)}, u32[]{:S(2)}) collective-permute-start(bf16[128,1792]{1,0:T(8,128)(2,1)} %collective-permute-done.25.refs_1_), channel_id=1, source_target_pairs={{0,32},{32,0},{1,33},{33,1},{2,34},{34,2},{3,35},{35,3},{4,36},{36... | collective-permute-start | bytes 1376264 | tf_op jit(solution)/shard_map/ppermute | solution.py:27
  182.2 20.2 %collective-permute-start.24 = (bf16[64,1792]{1,0:T(8,128)(2,1)}, bf16[64,1792]{1,0:T(8,128)(2,1)}, u32[]{:S(2)}, u32[]{:S(2)}) collective-permute-start(bf16[64,1792]{1,0:T(8,128)(2,1)} %slice.26), channel_id=1, source_target_pairs={{0,64},{64,128},{128,192},{192,0},{1,65},{65,129},{129,193},{193,1... | collective-permute-start | bytes 688136 | tf_op jit(solution)/shard_map/ppermute | solution.py:27
  191.1 13.6 %collective-permute-start.26 = (bf16[64,1792]{1,0:T(8,128)(2,1)}, bf16[64,1792]{1,0:T(8,128)(2,1)}, u32[]{:S(2)}, u32[]{:S(2)}) collective-permute-start(bf16[64,1792]{1,0:T(8,128)(2,1)} %slice.27), channel_id=1, source_target_pairs={{0,192},{64,0},{128,64},{192,128},{1,193},{65,1},{129,65},{193,129... | collective-permute-start | bytes 688136 | tf_op jit(solution)/shard_map/ppermute | solution.py:27
  192.2 33.3 %all-to-all-start.4 = ((f32[8,4,16,224]{3,2,1,0:T(8,128)}), f32[8,4,16,224]{3,2,1,0:T(8,128)}, u32[]{:S(2)}, u32[]{:S(2)}) async-start(f32[8,4,16,224]{3,2,1,0:T(8,128)} %get-tuple-element.40), calls=%async_computation.4 | async-start | bytes 1048576 | tf_op jit(solution)/shard_map/all_to_all | solution.py:31
  202.0 12.7 %collective-permute-start.35 = (bf16[128,1792]{1,0:T(8,128)(2,1)S(1)}, bf16[128,1792]{1,0:T(8,128)(2,1)S(1)}, u32[]{:S(2)}, u32[]{:S(2)}) collective-permute-start(bf16[128,1792]{1,0:T(8,128)(2,1)S(1)} %back.3.refs_0_), channel_id=1, source_target_pairs={{0,64},{64,128},{128,192},{192,0},{1,65},{65,129},{129,193},{193,1... | collective-permute-start | bytes 1376264 | tf_op jit(solution)/shard_map/ppermute | solution.py:27
  202.4 12.3 %collective-permute-start.36 = (bf16[128,1792]{1,0:T(8,128)(2,1)S(1)}, bf16[128,1792]{1,0:T(8,128)(2,1)S(1)}, u32[]{:S(2)}, u32[]{:S(2)}) collective-permute-start(bf16[128,1792]{1,0:T(8,128)(2,1)S(1)} %back.3.refs_0_), channel_id=1, source_target_pairs={{0,192},{64,0},{128,64},{192,128},{1,193},{65,1},{129,65},{193,129... | collective-permute-start | bytes 1376264 | tf_op jit(solution)/shard_map/ppermute | solution.py:27
  204.7 7.9 %collective-permute-start.27 = (bf16[64,1792]{1,0:T(8,128)(2,1)}, bf16[64,1792]{1,0:T(8,128)(2,1)S(1)}, u32[]{:S(2)}, u32[]{:S(2)}) collective-permute-start(bf16[64,1792]{1,0:T(8,128)(2,1)} %collective-permute-done.24.refs_0_), channel_id=1, source_target_pairs={{0,32},{32,0},{1,33},{33,1},{2,34},{34,2},{3,35},{35,3},{4,36},{36... | collective-permute-start | bytes 688136 | tf_op jit(solution)/shard_map/ppermute | solution.py:27
  207.6 5.0 %collective-permute-start.28 = (bf16[64,1792]{1,0:T(8,128)(2,1)}, bf16[64,1792]{1,0:T(8,128)(2,1)S(1)}, u32[]{:S(2)}, u32[]{:S(2)}) collective-permute-start(bf16[64,1792]{1,0:T(8,128)(2,1)} %collective-permute-done.26.refs_1_), channel_id=1, source_target_pairs={{0,32},{32,0},{1,33},{33,1},{2,34},{34,2},{3,35},{35,3},{4,36},{36... | collective-permute-start | bytes 688136 | tf_op jit(solution)/shard_map/ppermute | solution.py:27
  209.7 9.4 %collective-permute-start.39 = (bf16[128,1792]{1,0:T(8,128)(2,1)S(1)}, bf16[128,1792]{1,0:T(8,128)(2,1)S(1)}, u32[]{:S(2)}, u32[]{:S(2)}) collective-permute-start(bf16[128,1792]{1,0:T(8,128)(2,1)S(1)} %back.3.refs_0_), channel_id=1, source_target_pairs={{0,32},{32,0},{1,33},{33,1},{2,34},{34,2},{3,35},{35,3},{4,36},{36... | collective-permute-start | bytes 1376264 | tf_op jit(solution)/shard_map/ppermute | solution.py:27
  214.7 5.9 %collective-permute-start.37 = (bf16[128,1792]{1,0:T(8,128)(2,1)S(1)}, bf16[128,1792]{1,0:T(8,128)(2,1)S(1)}, u32[]{:S(2)}, u32[]{:S(2)}) collective-permute-start(bf16[128,1792]{1,0:T(8,128)(2,1)S(1)} %collective-permute-done.35.refs_0_), channel_id=1, source_target_pairs={{0,32},{32,0},{1,33},{33,1},{2,34},{34,2},{3,35},{35,3},{4,36},{36... | collective-permute-start | bytes 1376264 | tf_op jit(solution)/shard_map/ppermute | solution.py:27
  216.2 4.4 %collective-permute-start.38 = (bf16[128,1792]{1,0:T(8,128)(2,1)S(1)}, bf16[128,1792]{1,0:T(8,128)(2,1)S(1)}, u32[]{:S(2)}, u32[]{:S(2)}) collective-permute-start(bf16[128,1792]{1,0:T(8,128)(2,1)S(1)} %collective-permute-done.36.refs_1_), channel_id=1, source_target_pairs={{0,32},{32,0},{1,33},{33,1},{2,34},{34,2},{3,35},{35,3},{4,36},{36... | collective-permute-start | bytes 1376264 | tf_op jit(solution)/shard_map/ppermute | solution.py:27
  216.2 8.0 %collective-permute-start.40 = (bf16[64,1792]{1,0:T(8,128)(2,1)S(1)}, bf16[64,1792]{1,0:T(8,128)(2,1)S(1)}, u32[]{:S(2)}, u32[]{:S(2)}) collective-permute-start(bf16[64,1792]{1,0:T(8,128)(2,1)S(1)} %slice.22), channel_id=1, source_target_pairs={{0,64},{64,128},{128,192},{192,0},{1,65},{65,129},{129,193},{193,1... | collective-permute-start | bytes 688136 | tf_op jit(solution)/shard_map/ppermute | solution.py:27
  216.3 7.9 %collective-permute-start.41 = (bf16[64,1792]{1,0:T(8,128)(2,1)S(1)}, bf16[64,1792]{1,0:T(8,128)(2,1)S(1)}, u32[]{:S(2)}, u32[]{:S(2)}) collective-permute-start(bf16[64,1792]{1,0:T(8,128)(2,1)S(1)} %slice.23), channel_id=1, source_target_pairs={{0,192},{64,0},{128,64},{192,128},{1,193},{65,1},{129,65},{193,129... | collective-permute-start | bytes 688136 | tf_op jit(solution)/shard_map/ppermute | solution.py:27
  224.2 4.4 %collective-permute-start.42 = (bf16[64,1792]{1,0:T(8,128)(2,1)S(1)}, bf16[64,1792]{1,0:T(8,128)(2,1)S(1)}, u32[]{:S(2)}, u32[]{:S(2)}) collective-permute-start(bf16[64,1792]{1,0:T(8,128)(2,1)S(1)} %collective-permute-done.40.refs_0_), channel_id=1, source_target_pairs={{0,32},{32,0},{1,33},{33,1},{2,34},{34,2},{3,35},{35,3},{4,36},{36... | collective-permute-start | bytes 688136 | tf_op jit(solution)/shard_map/ppermute | solution.py:27
  225.5 3.1 %collective-permute-start.43 = (bf16[64,1792]{1,0:T(8,128)(2,1)S(1)}, bf16[64,1792]{1,0:T(8,128)(2,1)S(1)}, u32[]{:S(2)}, u32[]{:S(2)}) collective-permute-start(bf16[64,1792]{1,0:T(8,128)(2,1)S(1)} %collective-permute-done.41.refs_1_), channel_id=1, source_target_pairs={{0,32},{32,0},{1,33},{33,1},{2,34},{34,2},{3,35},{35,3},{4,36},{36... | collective-permute-start | bytes 688136 | tf_op jit(solution)/shard_map/ppermute | solution.py:27
  (10 other events, 321.7 us)
where the time goes:
time: 231 us; the launch traced here: 230 us
  starting transfers between devices  100 us (43%)
  waiting for transfers between devices  69.8 us (30%)
  blocking collectives  19.4 us (8%)
  Pallas kernels  18.9 us (8%)
  local copies, waits for them, and re-layouts  18 us (8%)
  other arithmetic  2.63 us (1%)
    ppermute x38, starting transfers between devices, shift(): return lax.ppermute(v, axis, [(i, (i + k) % n) for i in range(n)])  60.6 us
    ppermute x38, waiting for transfers between devices, shift(): return lax.ppermute(v, axis, [(i, (i + k) % n) for i in range(n)])  50.7 us
    all_to_all x4, starting transfers between devices, exchange(): return lax.all_to_all(v, axis, split_axis=0, concat_axis=0, tiled=True)  21.7 us
    all_to_all x1, blocking collectives, exchange(): return lax.all_to_all(v, axis, split_axis=0, concat_axis=0, tiled=True)  19.4 us
    ppermute x6, starting transfers between devices, sum_over(): tile = tile + lax.ppermute(tile, axis, [(i, i ^ step) for i in range(n)])  18.3 us
    pallas_call x6, Pallas kernels, place(): pl.pallas_call(functools.partial(place_kernel, m, spots), out_shape=jax.S...  11.2 us
    ppermute x6, waiting for transfers between devices, sum_over(): tile = tile + lax.ppermute(tile, axis, [(i, i ^ step) for i in range(n)])  10.3 us
    all_to_all x4, waiting for transfers between devices, exchange(): return lax.all_to_all(v, axis, split_axis=0, concat_axis=0, tiled=True)  8.8 us
  transfers between devices with their start and end apart: 48, of which 15 were waited for; matrix products, arithmetic and copies ran while one was open for 5% of the time, Pallas kernels for 7%

commit v1 on v0

--- a/solution.py
+++ b/solution.py
@@ -39,11 +39,10 @@
     return lax.optimization_barrier((first, second))[1]
 
 
-def project_kernel(at_ref, g_ref, own_ref, peer_ref, tile_ref, *refs):
-    outs, basis_ref, total_ref = refs[:-2], refs[-2], refs[-1]
+def project_kernel(at_ref, g_ref, own_ref, peer_ref, basis_ref, *refs):
+    outs, total_ref = refs[:-1], refs[-1]
     x, core, y, z = (at_ref[i] for i in range(4))
     nx, nz, _, part, _ = own_ref.shape
-    cols = g_ref.shape[2]
     ny = len(outs)
     width = outs[0].shape[-1]
 
@@ -70,99 +69,98 @@
         return 0
 
     lax.fori_loop(0, MATS, multiply, 0)
-    for m in range(MATS):
-        for d in range(ny):
-            start = pl.multiple_of(lax.rem(y + d, ny) * width, width)
-            outs[d][m, :cols] = total_ref[m, :, pl.ds(start, width)]
-            outs[d][m, cols:] = tile_ref[...]
-
-
-def project(at, g, own, peer, tile, parts):
+    for d in range(ny):
+        start = pl.multiple_of(lax.rem(y + d, ny) * width, width)
+        outs[d][...] = total_ref[:, :, pl.ds(start, width)]
+
+
+def project(at, g, own, peer, parts):
     nz, mats, cols, rows = g.shape
     rank = own.shape[-1]
-    size = (mats, cols + tile.shape[0], rank // parts)
-    return pl.pallas_call(
+    basis, *out = pl.pallas_call(
         project_kernel,
-        out_shape=[jax.ShapeDtypeStruct(size, F32)] * parts,
-        in_specs=[SMEM] + [VMEM] * 4,
-        out_specs=[VMEM] * parts,
-        scratch_shapes=[
-            pltpu.VMEM((mats, nz, rows, rank), BF16),
-            pltpu.VMEM((mats, cols, rank), F32),
-        ],
+        out_shape=[jax.ShapeDtypeStruct((mats, nz, rows, rank), BF16)]
+        + [jax.ShapeDtypeStruct((mats, cols, rank // parts), F32)] * parts,
+        in_specs=[SMEM] + [VMEM] * 3,
+        out_specs=[VMEM] * (1 + parts),
+        scratch_shapes=[pltpu.VMEM((mats, cols, rank), F32)],
         compiler_params=PARAMS,
         cost_estimate=cost(2 * mats * nz * cols * rows * rank, 4 * 2**20),
         name="project",
-    )(at, g, own, peer, tile)
-
-
-def moments_kernel(moments_ref, p0, p1, p2, p3, new_ref, *update_refs):
-    nz, _, ranks, cols = moments_ref.shape
+    )(at, g, own, peer)
+    return basis, out
+
+
+def moments_kernel(moments_ref, sum_ref, new_ref, update_ref):
+    nz, _, cols = moments_ref.shape
+    kinds = 2 * MATS
+    ranks = new_ref.shape[1] // kinds
     limit = 1.0 * math.sqrt(MATS * D * FF)
+    total = jnp.sum(moments_ref[:, kinds * ranks :], axis=0)
+    scale = limit / jnp.maximum(jnp.sqrt(total[0:1, 0:1]), limit)
     first_bias_correction = 1.0 - 0.9**STEP
     second_fix = 1.0 - 0.999**STEP
     spare = 256 - cols
     for m in range(MATS):
-        summed = (p0[m] + p1[m]) + (p2[m] + p3[m])
-        scale = limit / jnp.maximum(jnp.sqrt(summed[cols : cols + 1, 0:1]), limit)
-        padded = jnp.concatenate([summed[:cols], jnp.zeros((spare, summed.shape[1]), F32)], axis=0)
+        one, two = (slice(k * ranks, (k + 1) * ranks) for k in (m, MATS + m))
+        summed = sum_ref[m]
+        padded = jnp.concatenate([summed, jnp.zeros((spare, summed.shape[1]), F32)], axis=0)
         scaled = scale * jnp.transpose(padded)[:, :cols]
-        first = 0.9 * moments_ref[:, m].reshape(nz * ranks, cols) + 0.1 * scaled
-        second = 0.999 * moments_ref[:, MATS + m].reshape(nz * ranks, cols) + 0.001 * scaled * scaled
-        new_ref[:, m] = first.reshape(nz, ranks, cols)
-        new_ref[:, MATS + m] = second.reshape(nz, ranks, cols)
+        first = 0.9 * moments_ref[:, one].reshape(nz * ranks, cols) + 0.1 * scaled
+        second = 0.999 * moments_ref[:, two].reshape(nz * ranks, cols) + 0.001 * scaled * scaled
+        new_ref[:, one] = first.reshape(nz, ranks, cols)
+        new_ref[:, two] = second.reshape(nz, ranks, cols)
         update = first / first_bias_correction / (jnp.sqrt(second / second_fix) + 1e-08)
         wide = jnp.concatenate([update, jnp.zeros((update.shape[0], spare), F32)], axis=1)
-        turned = jnp.transpose(wide)[:cols].astype(BF16)
-        for z in range(nz):
-            update_refs[m][z] = turned
-
-
-def moments(held, parts):
-    nz, _, ranks, cols = held.shape
+        update_ref[m] = jnp.transpose(wide)[:cols].astype(BF16)
+
+
+def moments(held, ranks, summed):
+    nz, _, cols = held.shape
     return pl.pallas_call(
         moments_kernel,
-        out_shape=[jax.ShapeDtypeStruct(held.shape, F32)]
-        + [jax.ShapeDtypeStruct((nz, cols, nz * ranks), BF16)] * MATS,
-        in_specs=[VMEM] * 5,
-        out_specs=[VMEM] * (1 + MATS),
+        out_shape=[
+            jax.ShapeDtypeStruct((nz, 2 * MATS * ranks, cols), F32),
+            jax.ShapeDtypeStruct((MATS, cols, nz * ranks), BF16),
+        ],
+        in_specs=[VMEM] * 2,
+        out_specs=[VMEM] * 2,
         compiler_params=PARAMS,
         cost_estimate=cost(2e9, 2 * 2**20),
         name="moments",
-    )(held, *parts)
-
-
-def back_kernel(m, at_ref, basis_ref, w_ref, u0, u1, u2, u3, out_ref):
+    )(held, summed)
+
+
+def back_kernel(m, at_ref, basis_ref, w_ref, u0, u1, u2, u3, out_ref, whole_ref):
     y = at_ref[2]
-    width = u0.shape[1]
+    width = u0.shape[2]
     blocks = (u0, u1, u2, u3)
     n = len(blocks)
-    total = None
-    for d in range(0, n, 2):
-        left = jnp.concatenate(
-            [
-                basis_ref[m, :, pl.ds(pl.multiple_of(lax.rem(y - e + n, n) * width, width), width)]
-                for e in (d, d + 1)
-            ],
-            axis=1,
+    for d in range(n):
+        start = pl.multiple_of(lax.rem(y - d + n, n) * width, width)
+        whole_ref[:, pl.ds(start, width)] = blocks[d][m]
+
+    def rows(z, _):
+        product = lax.dot_general(
+            whole_ref[...], basis_ref[m, z], (((1,), (1,)), ((), ())), preferred_element_type=F32
         )
-        right = jnp.concatenate([blocks[d][...], blocks[d + 1][...]], axis=1)
-        term = lax.dot_general(
-            left, right, (((1,), (1,)), ((), ())), preferred_element_type=F32
-        )
-        total = term if total is None else total + term
-    out_ref[...] = (w_ref[m].astype(F32) - 0.5 * total).astype(BF16)
+        out_ref[z] = (w_ref[z, m].astype(F32) - 0.5 * product).astype(BF16)
+        return 0
+
+    lax.fori_loop(0, basis_ref.shape[1], rows, 0)
 
 
 def back(m, at, basis, w, blocks):
-    _, rows, cols = w.shape
+    nz, _, cols, rows = w.shape
+    rank = basis.shape[3]
     return pl.pallas_call(
         functools.partial(back_kernel, m),
-        out_shape=jax.ShapeDtypeStruct((rows, cols), BF16),
+        out_shape=jax.ShapeDtypeStruct((nz, cols, rows), BF16),
         in_specs=[SMEM] + [VMEM] * 6,
         out_specs=VMEM,
-        compiler_params=PARAMS,
-        cost_estimate=cost(2 * rows * cols * basis.shape[2], 3 * 2**20),
+        scratch_shapes=[pltpu.VMEM((cols, rank), BF16)],
+        compiler_params=PARAMS,
+        cost_estimate=cost(2 * nz * rows * cols * rank, 3 * 2**20),
         name="back",
     )(at, basis, w, *blocks)
 
@@ -225,33 +223,41 @@
     ranks = rank // (ny * nz)
     at = jnp.stack([x, core, y, z])
 
-    turned = jnp.swapaxes(grads, 1, 2).reshape(mats, nz, cols // nz, rows)
-    mine = exchange(jnp.swapaxes(turned, 0, 1), "z")
+    def by_block(v):
+        blocks = jnp.swapaxes(v, 1, 2).reshape(mats, nz, cols // nz, rows)
+        return blocks, jnp.swapaxes(blocks, 0, 1)
 
     piece = lax.dynamic_slice_in_dim(basis, (x * nc + core) * part, part, axis=1)
+    held = jnp.stack([piece] + [shift(piece, "z", k) for k in range(1, nz)])
+    turned, sent = by_block(grads)
+    mine = exchange(sent, "z")
     grad_wide = turned.astype(F32)
-    tile = jnp.full((8, 128), jnp.sum(grad_wide * grad_wide), F32)
-    tile = sum_over(sum_over(tile, "z"), "core")
-    held = jnp.stack([piece] + [shift(piece, "z", k) for k in range(1, nz)])
+    tile = jnp.full((8, cols // nz), jnp.sum(grad_wide * grad_wide), F32)
+    tile = sum_over(tile, "x")
     tile, held = lax.optimization_barrier((tile, held))
-    tile = sum_over(tile, "x")
+    tile = sum_over(tile, "y")
     own = jnp.stack([held] + [shift(held, "x", k) for k in range(1, nx)])
     tile, own = lax.optimization_barrier((tile, own))
+    tile = sum_over(tile, "core")
     peer = shift(own, "core", 1)
 
-    state = jnp.concatenate([moment1, moment2], axis=0).reshape(2 * mats, ranks, nz, cols // nz)
-    state = exchange(before(mine, state.transpose(2, 0, 1, 3)), "z")
-
-    parts = project(at, mine, own, peer, tile, ny)
+    state = jnp.concatenate([moment1, moment2], axis=0).reshape(2 * mats * ranks, nz, cols // nz)
+    state = jnp.concatenate([jnp.swapaxes(state, 0, 1), jnp.stack([tile] * nz)], axis=1)
+    w = by_block(weights)[1]
+    mine, peer, state, w = lax.optimization_barrier((mine, peer, state, w))
+    state = exchange(state, "z")
+
+    gathered, parts = project(at, mine, own, peer, ny)
+    gathered, w = lax.optimization_barrier((gathered, w))
+    w = exchange(before(state, w), "z")
     parts = [parts[0]] + [shift(parts[k], "y", k) for k in range(1, ny)]
-    news, *updates = moments(state, parts)
-    blocks = []
-    for update in updates:
-        block = exchange(update, "z").reshape(cols, nz * ranks)
-        blocks.append([block] + [shift(block, "y", k) for k in range(1, ny)])
-
-    news = before(blocks[-1][0], news)
-    news = exchange(news, "z").transpose(1, 2, 0, 3).reshape(2, mats, ranks, cols)
+    summed = (parts[0] + parts[1]) + (parts[2] + parts[3])
+    news, update = moments(state, ranks, summed)
+    updates = [update] + [shift(update, "y", k) for k in range(1, ny)]
+    fresh = [exchange(back(m, at, gathered, w, updates), "z") for m in range(mats)]
+    news = exchange(before(fresh[-1], news), "z")
+    news = jnp.swapaxes(news, 0, 1).reshape(2, mats, ranks, cols)
+    fresh = [jnp.swapaxes(f.reshape(cols, rows), 0, 1) for f in fresh]
 
     half = rows // 2
     shape = (mats, rows, cols * nx * nc)
@@ -261,7 +267,6 @@
         here = [(b, dx, False, row) for b, dx, row in items]
         return place(whole, shape, m, at, here + there)
 
-    fresh = [back(m, at, basis, weights, blocks[m]) for m in range(mats)]
     near = [(shift(f, "x", 1), shift(f, "x", -1)) for f in fresh]
     whole = put(None, 0, [(fresh[0], 0, 0)])
     whole = put(whole, 0, [(near[0][0], 3, 0), (near[0][1], 1, 0)])

time: 231 us -> 223 us (0.965)
  waiting for transfers between devices: 69.8 us -> 53.1 us
  local copies, waits for them, and re-layouts: 18 us -> 28.6 us
  starting transfers between devices: 100 us -> 95.5 us
  other arithmetic: 2.63 us -> 6.32 us
    ppermute x38 -> x35, waiting for transfers between devices: 50.7 us -> 35 us  [shift(): return lax.ppermute(v, axis, [(i, (i + k) % n) for i in range(n)])]
    ppermute x6 -> x5, starting transfers between devices: 18.3 us -> 9.69 us  [sum_over(): tile = tile + lax.ppermute(tile, axis, [(i, i ^ step) for i in range(n)])]
    ppermute x6 -> x5, waiting for transfers between devices: 10.3 us -> 3.64 us  [sum_over(): tile = tile + lax.ppermute(tile, axis, [(i, i ^ step) for i in range(n)])]
    unnamed x28 -> x45, local copies, waits for them, and re-layouts: 7.76 us -> 14.4 us
    all_to_all x4 -> x5, waiting for transfers between devices: 8.8 us -> 14.5 us  [exchange(): return lax.all_to_all(v, axis, split_axis=0, concat_axis=0, tiled=True)]
    reshape x1 -> x4, local copies, waits for them, and re-layouts: 0.98 us -> 4.66 us  [the longest x2 3.22 us: by_block(): blocks = jnp.swapaxes(v, 1, 2).reshape(mats, nz, cols // nz, rows)]
    all_to_all x4 -> x5, starting transfers between devices: 21.7 us -> 25.2 us  [exchange(): return lax.all_to_all(v, axis, split_axis=0, concat_axis=0, tiled=True)]
    ppermute x38 -> x35, starting transfers between devices: 60.6 us -> 60.6 us  [shift(): return lax.ppermute(v, axis, [(i, (i + k) % n) for i in range(n)])]
  transfers between devices with their start and end apart: 48 -> 45, of which waited for: 15 -> 16; matrix products, arithmetic and copies ran while one was open for 5% -> 9% of each run, Pallas kernels for 7% -> 7%
where the time goes in v1:
time: 223 us; the launch traced here: 222 us
  starting transfers between devices  95.5 us (43%)
  waiting for transfers between devices  53.1 us (24%)
  local copies, waits for them, and re-layouts  28.6 us (13%)
  blocking collectives  18.9 us (8%)
  Pallas kernels  18.5 us (8%)
  other arithmetic  6.32 us (3%)
    ppermute x35, starting transfers between devices, shift(): return lax.ppermute(v, axis, [(i, (i + k) % n) for i in range(n)])  60.6 us
    ppermute x35, waiting for transfers between devices, shift(): return lax.ppermute(v, axis, [(i, (i + k) % n) for i in range(n)])  35 us
    all_to_all x5, starting transfers between devices, exchange(): return lax.all_to_all(v, axis, split_axis=0, concat_axis=0, tiled=True)  25.2 us
    all_to_all x1, blocking collectives, exchange(): return lax.all_to_all(v, axis, split_axis=0, concat_axis=0, tiled=True)  18.9 us
    all_to_all x5, waiting for transfers between devices, exchange(): return lax.all_to_all(v, axis, split_axis=0, concat_axis=0, tiled=True)  14.5 us
    unnamed x45, local copies, waits for them, and re-layouts  14.4 us
    pallas_call x6, Pallas kernels, place(): pl.pallas_call(functools.partial(place_kernel, m, spots), out_shape=jax.S...  10.6 us
    ppermute x5, starting transfers between devices, sum_over(): tile = tile + lax.ppermute(tile, axis, [(i, i ^ step) for i in range(n)])  9.69 us
  transfers between devices with their start and end apart: 45, of which 16 were waited for; matrix products, arithmetic and copies ran while one was open for 9% of the time, Pallas kernels for 7%

profile of v1, /device:TPU:1, one launch (start us, length us, event | category | flops | bytes accessed | tf_op | source)
XLA Modules:
  0.0 222.1 jit_solution(17065522317738302484)
XLA Ops:
  0.6 1.6 copy.15
  4.0 2.1 collective-permute-start
  7.8 3.1 %collective-permute-start.1 = (f32[8,224]{1,0:T(8,128)S(1)}, f32[8,224]{1,0:T(8,128)S(1)}, u32[]{:S(2)}, u32[]{:S(2)}) collective-permute-start(f32[8,224]{1,0:T(8,128)S(1)} %broadcast_add_fusion), channel_id=1, source_target_pairs={{0,128},{64,192},{128,0},{192,64},{1,129},{65,193},{129,1},{193,65... | collective-permute-start | bytes 21512 | tf_op jit(solution)/shard_map/ppermute | solution.py:211
  11.6 1.6 collective-permute-start.2
  13.3 3.0 %collective-permute-start.3 = (bf16[2,16,512]{2,1,0:T(8,128)(2,1)S(1)}, bf16[2,16,512]{2,1,0:T(8,128)(2,1)S(1)}, u32[]{:S(2)}, u32[]{:S(2)}) collective-permute-start(bf16[2,16,512]{2,1,0:T(8,128)(2,1)S(1)} %get-tuple-element.54), channel_id=1, source_target_pairs={{0,2},{1,3},{2,4},{3,5},{4,6},{5,7},{6,0},{7,1},{8,10},{9,11},{10,... | collective-permute-start | bytes 98312 | tf_op jit(solution)/shard_map/ppermute | solution.py:27
  16.3 3.8 %collective-permute-start.4 = (bf16[2,16,512]{2,1,0:T(8,128)(2,1)S(1)}, bf16[2,16,512]{2,1,0:T(8,128)(2,1)S(1)}, u32[]{:S(2)}, u32[]{:S(2)}) collective-permute-start(bf16[2,16,512]{2,1,0:T(8,128)(2,1)S(1)} %get-tuple-element.54), channel_id=1, source_target_pairs={{0,3},{1,4},{2,5},{3,6},{4,7},{5,0},{6,1},{7,2},{8,11},{9,12},{10,... | collective-permute-start | bytes 98312 | tf_op jit(solution)/shard_map/ppermute | solution.py:27
  21.5 6.2 %all-to-all-start = ((bf16[8,2,224,128]{3,2,1,0:T(8,128)(2,1)}), bf16[8,2,224,128]{3,2,1,0:T(8,128)(2,1)S(1)}, u32[]{:S(2)}, u32[]{:S(2)}) async-start(bf16[8,2,224,128]{3,2,1,0:T(8,128)(2,1)} %bitcast.43), calls=%async_computation | async-start | bytes 1835008 | tf_op jit(solution)/shard_map/all_to_all | solution.py:31
  27.7 4.5 %collective-permute-start.6 = (bf16[2,16,512]{2,1,0:T(8,128)(2,1)S(1)}, bf16[2,16,512]{2,1,0:T(8,128)(2,1)S(1)}, u32[]{:S(2)}, u32[]{:S(2)}) collective-permute-start(bf16[2,16,512]{2,1,0:T(8,128)(2,1)S(1)} %get-tuple-element.54), channel_id=1, source_target_pairs={{0,5},{1,6},{2,7},{3,0},{4,1},{5,2},{6,3},{7,4},{8,13},{9,14},{10,... | collective-permute-start | bytes 98312 | tf_op jit(solution)/shard_map/ppermute | solution.py:27
  34.4 9.0 %collective-permute-done.6 = bf16[2,16,512]{2,1,0:T(8,128)(2,1)S(1)} collective-permute-done((bf16[2,16,512]{2,1,0:T(8,128)(2,1)S(1)}, bf16[2,16,512]{2,1,0:T(8,128)(2,1)S(1)}, u32[]{:S(2)}, u32[]{:S(2)}) %collective-permute-start.6) | collective-permute-done | bytes 32800 | tf_op jit(solution)/shard_map/ppermute | solution.py:27
  43.4 3.7 %collective-permute-done.7 = bf16[2,16,512]{2,1,0:T(8,128)(2,1)S(1)} collective-permute-done((bf16[2,16,512]{2,1,0:T(8,128)(2,1)S(1)}, bf16[2,16,512]{2,1,0:T(8,128)(2,1)S(1)}, u32[]{:S(2)}, u32[]{:S(2)}) %collective-permute-start.7) | collective-permute-done | bytes 32800 | tf_op jit(solution)/shard_map/ppermute | solution.py:27
  47.8 1.7 collective-permute-start.12
  51.5 1.5 collective-permute-done.9
  53.0 2.9 %collective-permute-start.10 = (f32[8,224]{1,0:T(8,128)S(1)}, f32[8,224]{1,0:T(8,128)S(1)}, u32[]{:S(2)}, u32[]{:S(2)}) collective-permute-start(f32[8,224]{1,0:T(8,128)S(1)} %add.34), channel_id=1, source_target_pairs={{0,16},{8,24},{16,0},{24,8},{1,17},{9,25},{17,1},{25,9},{2,18},{10... | collective-permute-start | bytes 21512 | tf_op jit(solution)/shard_map/ppermute | solution.py:211
  57.4 9.7 %collective-permute-start.14 = (bf16[4,8,2,16,512]{4,3,2,1,0:T(8,128)(2,1)S(1)}, bf16[4,8,2,16,512]{4,3,2,1,0:T(8,128)(2,1)S(1)}, u32[]{:S(2)}, u32[]{:S(2)}) collective-permute-start(bf16[4,8,2,16,512]{4,3,2,1,0:T(8,128)(2,1)S(1)} %pad_maximum_fusion.own_ref), channel_id=1, source_target_pairs={{0,32},{32,0},{1,33},{33,1},{2,34},{34,2},{3,35},{35,3},{4,36},{36... | collective-permute-start | bytes 3145736 | tf_op jit(solution)/shard_map/ppermute | solution.py:27
  67.5 1.8 pad_maximum_fusion.2
  69.2 2.2 reshape.29
  71.4 2.0 copy.29
  73.4 2.2 copy.18
  75.6 2.2 %copy.27 = bf16[2,8,224,128]{3,2,0,1:T(8,128)(2,1)} copy(bf16[2,8,224,128]{3,2,1,0:T(8,128)(2,1)} %bitcast.55) | data formatting | bytes 1835008 | tf_op jit(solution)/shard_map/reshape | solution.py:227
  77.8 1.9 pad_maximum_fusion.1
  80.7 5.5 %all-to-all-start.1 = ((f32[8,72,224]{2,1,0:T(8,128)}), f32[8,72,224]{2,1,0:T(8,128)}, u32[]{:S(2)}, u32[]{:S(2)}) async-start(f32[8,72,224]{2,1,0:T(8,128)} %pad_maximum_fusion.1), calls=%async_computation.1 | async-start | bytes 1179648 | tf_op jit(solution)/shard_map/all_to_all | solution.py:31
  88.7 1.7 project.1
  92.4 13.2 %all-to-all-done.1.moments_ref = f32[8,72,224]{2,1,0:T(8,128)} async-done(((f32[8,72,224]{2,1,0:T(8,128)}), f32[8,72,224]{2,1,0:T(8,128)}, u32[]{:S(2)}, u32[]{:S(2)}) %all-to-all-start.1) | async-done | bytes 516128 | tf_op jit(solution)/shard_map/all_to_all | solution.py:31
  105.7 3.6 %all-to-all-start.2 = ((bf16[8,2,224,128]{3,2,1,0:T(8,128)(2,1)}), bf16[8,2,224,128]{3,2,1,0:T(8,128)(2,1)S(1)}, u32[]{:S(2)}, u32[]{:S(2)}) async-start(bf16[8,2,224,128]{3,2,1,0:T(8,128)(2,1)} %bitcast.54), calls=%async_computation.2 | async-start | bytes 1835008 | tf_op jit(solution)/shard_map/all_to_all | solution.py:31
  110.6 2.6 %collective-permute-start.17 = (f32[2,224,128]{2,1,0:T(8,128)}, f32[2,224,128]{2,1,0:T(8,128)S(1)}, u32[]{:S(2)}, u32[]{:S(2)}) collective-permute-start(f32[2,224,128]{2,1,0:T(8,128)} %copy-done.15), channel_id=1, source_target_pairs={{0,16},{8,24},{16,0},{24,8},{1,17},{9,25},{17,1},{25,9},{2,18},{10... | collective-permute-start | bytes 688136 | tf_op jit(solution)/shard_map/ppermute | solution.py:27
  114.3 3.2 %collective-permute-done.16 = f32[2,224,128]{2,1,0:T(8,128)S(1)} collective-permute-done((f32[2,224,128]{2,1,0:T(8,128)}, f32[2,224,128]{2,1,0:T(8,128)S(1)}, u32[]{:S(2)}, u32[]{:S(2)}) %collective-permute-start.16) | collective-permute-done | bytes 229408 | tf_op jit(solution)/shard_map/ppermute | solution.py:27
  117.5 6.0 %collective-permute-done.17 = f32[2,224,128]{2,1,0:T(8,128)S(1)} collective-permute-done((f32[2,224,128]{2,1,0:T(8,128)}, f32[2,224,128]{2,1,0:T(8,128)S(1)}, u32[]{:S(2)}, u32[]{:S(2)}) %collective-permute-start.17) | collective-permute-done | bytes 229408 | tf_op jit(solution)/shard_map/ppermute | solution.py:27
  126.3 2.8 %collective-permute-start.20 = (bf16[2,224,128]{2,1,0:T(8,128)(2,1)S(1)}, bf16[2,224,128]{2,1,0:T(8,128)(2,1)S(1)}, u32[]{:S(2)}, u32[]{:S(2)}) collective-permute-start(bf16[2,224,128]{2,1,0:T(8,128)(2,1)S(1)} %get-tuple-element.44.u0), channel_id=1, source_target_pairs={{0,16},{8,24},{16,0},{24,8},{1,17},{9,25},{17,1},{25,9},{2,18},{10... | collective-permute-start | bytes 344072 | tf_op jit(solution)/shard_map/ppermute | solution.py:27
  130.1 4.2 %collective-permute-done.20.u2 = bf16[2,224,128]{2,1,0:T(8,128)(2,1)S(1)} collective-permute-done((bf16[2,224,128]{2,1,0:T(8,128)(2,1)S(1)}, bf16[2,224,128]{2,1,0:T(8,128)(2,1)S(1)}, u32[]{:S(2)}, u32[]{:S(2)}) %collective-permute-start.20) | collective-permute-done | bytes 114720 | tf_op jit(solution)/shard_map/ppermute | solution.py:27
  135.5 2.4 %back.2 = bf16[8,224,128]{2,1,0:T(8,128)(2,1)S(1)} custom-call(s32[4]{0:T(128)S(1)} %pad_add_fusion.at_ref, bf16[2,8,128,512]{3,2,1,0:T(8,128)(2,1)S(1)} %get-tuple-element.36.basis_ref, bf16[8,2,224,128]{3,2,1,0:T(8,128)(2,1)S(1)} %all-to-all-done.2.w_ref, bf16[2,224,128]{2,1,0:T(8,128)(2,1)S(1)} %get-tuple-element.44.u0, ...), custom_call_target="tpu_custom_call" | custom-call | flops 234881024 | bytes 3145728 | tf_op jit(solution)/shard_map/back/pallas_call | solution.py:156
  137.9 18.9 %all_to_all.30 = bf16[8,224,128]{2,1,0:T(8,128)(2,1)} all-to-all(bf16[8,224,128]{2,1,0:T(8,128)(2,1)S(1)} %back.2), channel_id=1, replica_groups=mesh['x'=4,'core'=2,'y'=4,'z'=8] {'z'}, dimensions={0} | all-to-all | bytes 917504 | tf_op jit(solution)/shard_map/all_to_all | solution.py:31
  162.8 2.4 %back.3 = bf16[8,224,128]{2,1,0:T(8,128)(2,1)S(1)} custom-call(s32[4]{0:T(128)S(1)} %pad_add_fusion.at_ref, bf16[2,8,128,512]{3,2,1,0:T(8,128)(2,1)S(1)} %get-tuple-element.36.basis_ref, bf16[8,2,224,128]{3,2,1,0:T(8,128)(2,1)S(1)} %all-to-all-done.2.w_ref, bf16[2,224,128]{2,1,0:T(8,128)(2,1)S(1)} %copy-done.7, bf16[2,224,128]{2,1,0:T(8,128)(2,1)S(1)} %copy-done.9, ...), custom_call_target="tpu_custom_call" | custom-call | flops 234881024 | bytes 3145728 | tf_op jit(solution)/shard_map/back/pallas_call | solution.py:156
  165.9 3.5 %all-to-all-start.4 = ((bf16[8,224,128]{2,1,0:T(8,128)(2,1)}), bf16[8,224,128]{2,1,0:T(8,128)(2,1)S(1)}, u32[]{:S(2)}, u32[]{:S(2)}) async-start(bf16[8,224,128]{2,1,0:T(8,128)(2,1)} %copy-done.2), calls=%async_computation.4 | async-start | bytes 917504 | tf_op jit(solution)/shard_map/all_to_all | solution.py:31
  169.4 1.7 collective-permute-start.24
  171.1 3.7 %collective-permute-start.30 = (bf16[128,1792]{1,0:T(8,128)(2,1)S(1)}, bf16[128,1792]{1,0:T(8,128)(2,1)S(1)}, u32[]{:S(2)}, u32[]{:S(2)}) collective-permute-start(bf16[128,1792]{1,0:T(8,128)(2,1)S(1)} %bitcast.47), channel_id=1, source_target_pairs={{0,32},{32,0},{1,33},{33,1},{2,34},{34,2},{3,35},{35,3},{4,36},{36... | collective-permute-start | bytes 1376264 | tf_op jit(solution)/shard_map/ppermute | solution.py:27
  174.9 3.2 %collective-permute-done.24.refs_1_ = bf16[128,1792]{1,0:T(8,128)(2,1)S(1)} collective-permute-done((bf16[128,1792]{1,0:T(8,128)(2,1)S(1)}, bf16[128,1792]{1,0:T(8,128)(2,1)S(1)}, u32[]{:S(2)}, u32[]{:S(2)}) %collective-permute-start.24) | collective-permute-done | bytes 458784 | tf_op jit(solution)/shard_map/ppermute | solution.py:27
  178.1 4.3 %collective-permute-start.29 = (bf16[128,1792]{1,0:T(8,128)(2,1)S(1)}, bf16[128,1792]{1,0:T(8,128)(2,1)}, u32[]{:S(2)}, u32[]{:S(2)}) collective-permute-start(bf16[128,1792]{1,0:T(8,128)(2,1)S(1)} %collective-permute-done.24.refs_1_), channel_id=1, source_target_pairs={{0,32},{32,0},{1,33},{33,1},{2,34},{34,2},{3,35},{35,3},{4,36},{36... | collective-permute-start | bytes 1376264 | tf_op jit(solution)/shard_map/ppermute | solution.py:27
  185.3 1.7 collective-permute-start.25
  187.2 6.5 %all-to-all-start.5 = ((f32[8,64,224]{2,1,0:T(8,128)}), f32[8,64,224]{2,1,0:T(8,128)}, u32[]{:S(2)}, u32[]{:S(2)}) async-start(f32[8,64,224]{2,1,0:T(8,128)} %copy-done.5), calls=%async_computation.5 | async-start | bytes 1048576 | tf_op jit(solution)/shard_map/all_to_all | solution.py:31
  193.8 2.7 %collective-permute-start.32 = (bf16[128,1792]{1,0:T(8,128)(2,1)S(1)}, bf16[128,1792]{1,0:T(8,128)(2,1)S(1)}, u32[]{:S(2)}, u32[]{:S(2)}) collective-permute-start(bf16[128,1792]{1,0:T(8,128)(2,1)S(1)} %bitcast.50), channel_id=1, source_target_pairs={{0,192},{64,0},{128,64},{192,128},{1,193},{65,1},{129,65},{193,129... | collective-permute-start | bytes 1376264 | tf_op jit(solution)/shard_map/ppermute | solution.py:27
  199.8 2.4 %place.7.refs_4_ = bf16[2,128,14336]{2,1,0:T(8,128)(2,1)} custom-call(s32[4]{0:T(128)S(1)} %pad_add_fusion.at_ref, bf16[128,1792]{1,0:T(8,128)(2,1)} %collective-permute-done.22.refs_0_, bf16[128,1792]{1,0:T(8,128)(2,1)S(1)} %collective-permute-done.24.refs_1_, ...), custom_call_target="tpu_custom_call", output_to_operand_aliasing={{}: (5, {})} | custom-call | flops 2000000000 | bytes 3670016 | tf_op jit(solution)/shard_map/place/pallas_call | solution.py:194
  202.3 1.9 place.8.refs_2_
  204.2 2.4 %collective-permute-done.31.refs_0_ = bf16[128,1792]{1,0:T(8,128)(2,1)S(1)} collective-permute-done((bf16[128,1792]{1,0:T(8,128)(2,1)S(1)}, bf16[128,1792]{1,0:T(8,128)(2,1)S(1)}, u32[]{:S(2)}, u32[]{:S(2)}) %collective-permute-start.31) | collective-permute-done | bytes 458784 | tf_op jit(solution)/shard_map/ppermute | solution.py:27
  208.1 2.8 %collective-permute-start.37 = (bf16[64,1792]{1,0:T(8,128)(2,1)S(1)}, bf16[64,1792]{1,0:T(8,128)(2,1)S(1)}, u32[]{:S(2)}, u32[]{:S(2)}) collective-permute-start(bf16[64,1792]{1,0:T(8,128)(2,1)S(1)} %slice.23), channel_id=1, source_target_pairs={{0,192},{64,0},{128,64},{192,128},{1,193},{65,1},{129,65},{193,129... | collective-permute-start | bytes 688136 | tf_op jit(solution)/shard_map/ppermute | solution.py:27
  210.9 1.5 place.9.refs_4_
  212.4 1.8 place.10.refs_4_
  214.2 1.8 collective-permute-done.36.refs_0_
  220.4 1.5 place.11
  (127 shorter events, 44.4 us)
Async XLA Ops:
  0.6 66.8 %copy-start.17 = (f32[2,16,1792]{2,1,0:T(8,128)S(1)}, f32[2,16,1792]{2,1,0:T(8,128)}, u32[]{:S(2)}) copy-start(f32[2,16,1792]{2,1,0:T(8,128)} %param.8) | copy-start | bytes 688132
  4.0 3.2 %collective-permute-start = (f32[8,224]{1,0:T(8,128)S(1)}, f32[8,224]{1,0:T(8,128)S(1)}, u32[]{:S(2)}, u32[]{:S(2)}) collective-permute-start(f32[8,224]{1,0:T(8,128)S(1)} %broadcast_in_dim.3), channel_id=1, source_target_pairs={{0,64},{64,0},{128,192},{192,128},{1,65},{65,1},{129,193},{193,129... | collective-permute-start | bytes 21512 | tf_op jit(solution)/shard_map/ppermute | solution.py:211
  7.8 19.9 %collective-permute-start.1 = (f32[8,224]{1,0:T(8,128)S(1)}, f32[8,224]{1,0:T(8,128)S(1)}, u32[]{:S(2)}, u32[]{:S(2)}) collective-permute-start(f32[8,224]{1,0:T(8,128)S(1)} %broadcast_add_fusion), channel_id=1, source_target_pairs={{0,128},{64,192},{128,0},{192,64},{1,129},{65,193},{129,1},{193,65... | collective-permute-start | bytes 21512 | tf_op jit(solution)/shard_map/ppermute | solution.py:211
  11.6 21.2 %collective-permute-start.2 = (bf16[2,16,512]{2,1,0:T(8,128)(2,1)S(1)}, bf16[2,16,512]{2,1,0:T(8,128)(2,1)S(1)}, u32[]{:S(2)}, u32[]{:S(2)}) collective-permute-start(bf16[2,16,512]{2,1,0:T(8,128)(2,1)S(1)} %get-tuple-element.54), channel_id=1, source_target_pairs={{0,1},{1,2},{2,3},{3,4},{4,5},{5,6},{6,7},{7,0},{8,9},{9,10},{10,1... | collective-permute-start | bytes 98312 | tf_op jit(solution)/shard_map/ppermute | solution.py:27
  13.3 20.8 %collective-permute-start.3 = (bf16[2,16,512]{2,1,0:T(8,128)(2,1)S(1)}, bf16[2,16,512]{2,1,0:T(8,128)(2,1)S(1)}, u32[]{:S(2)}, u32[]{:S(2)}) collective-permute-start(bf16[2,16,512]{2,1,0:T(8,128)(2,1)S(1)} %get-tuple-element.54), channel_id=1, source_target_pairs={{0,2},{1,3},{2,4},{3,5},{4,6},{5,7},{6,0},{7,1},{8,10},{9,11},{10,... | collective-permute-start | bytes 98312 | tf_op jit(solution)/shard_map/ppermute | solution.py:27
  16.3 18.1 %collective-permute-start.4 = (bf16[2,16,512]{2,1,0:T(8,128)(2,1)S(1)}, bf16[2,16,512]{2,1,0:T(8,128)(2,1)S(1)}, u32[]{:S(2)}, u32[]{:S(2)}) collective-permute-start(bf16[2,16,512]{2,1,0:T(8,128)(2,1)S(1)} %get-tuple-element.54), channel_id=1, source_target_pairs={{0,3},{1,4},{2,5},{3,6},{4,7},{5,0},{6,1},{7,2},{8,11},{9,12},{10,... | collective-permute-start | bytes 98312 | tf_op jit(solution)/shard_map/ppermute | solution.py:27
  20.0 14.4 %collective-permute-start.5 = (bf16[2,16,512]{2,1,0:T(8,128)(2,1)S(1)}, bf16[2,16,512]{2,1,0:T(8,128)(2,1)S(1)}, u32[]{:S(2)}, u32[]{:S(2)}) collective-permute-start(bf16[2,16,512]{2,1,0:T(8,128)(2,1)S(1)} %get-tuple-element.54), channel_id=1, source_target_pairs={{0,4},{1,5},{2,6},{3,7},{4,0},{5,1},{6,2},{7,3},{8,12},{9,13},{10,... | collective-permute-start | bytes 98312 | tf_op jit(solution)/shard_map/ppermute | solution.py:27
  21.5 59.2 %all-to-all-start = ((bf16[8,2,224,128]{3,2,1,0:T(8,128)(2,1)}), bf16[8,2,224,128]{3,2,1,0:T(8,128)(2,1)S(1)}, u32[]{:S(2)}, u32[]{:S(2)}) async-start(bf16[8,2,224,128]{3,2,1,0:T(8,128)(2,1)} %bitcast.43), calls=%async_computation | async-start | bytes 1835008 | tf_op jit(solution)/shard_map/all_to_all | solution.py:31
  27.7 15.8 %collective-permute-start.6 = (bf16[2,16,512]{2,1,0:T(8,128)(2,1)S(1)}, bf16[2,16,512]{2,1,0:T(8,128)(2,1)S(1)}, u32[]{:S(2)}, u32[]{:S(2)}) collective-permute-start(bf16[2,16,512]{2,1,0:T(8,128)(2,1)S(1)} %get-tuple-element.54), channel_id=1, source_target_pairs={{0,5},{1,6},{2,7},{3,0},{4,1},{5,2},{6,3},{7,4},{8,13},{9,14},{10,... | collective-permute-start | bytes 98312 | tf_op jit(solution)/shard_map/ppermute | solution.py:27
  32.8 14.3 %collective-permute-start.7 = (bf16[2,16,512]{2,1,0:T(8,128)(2,1)S(1)}, bf16[2,16,512]{2,1,0:T(8,128)(2,1)S(1)}, u32[]{:S(2)}, u32[]{:S(2)}) collective-permute-start(bf16[2,16,512]{2,1,0:T(8,128)(2,1)S(1)} %get-tuple-element.54), channel_id=1, source_target_pairs={{0,6},{1,7},{2,0},{3,1},{4,2},{5,3},{6,4},{7,5},{8,14},{9,15},{10,... | collective-permute-start | bytes 98312 | tf_op jit(solution)/shard_map/ppermute | solution.py:27
  34.1 13.4 %collective-permute-start.8 = (bf16[2,16,512]{2,1,0:T(8,128)(2,1)S(1)}, bf16[2,16,512]{2,1,0:T(8,128)(2,1)S(1)}, u32[]{:S(2)}, u32[]{:S(2)}) collective-permute-start(bf16[2,16,512]{2,1,0:T(8,128)(2,1)S(1)} %get-tuple-element.54), channel_id=1, source_target_pairs={{0,7},{1,0},{2,1},{3,2},{4,3},{5,4},{6,5},{7,6},{8,15},{9,8},{10,9... | collective-permute-start | bytes 98312 | tf_op jit(solution)/shard_map/ppermute | solution.py:27
  47.4 9.5 %collective-permute-start.11 = (bf16[8,2,16,512]{3,2,1,0:T(8,128)(2,1)S(1)}, bf16[8,2,16,512]{3,2,1,0:T(8,128)(2,1)S(1)}, u32[]{:S(2)}, u32[]{:S(2)}) collective-permute-start(bf16[8,2,16,512]{3,2,1,0:T(8,128)(2,1)S(1)} %bitcast_dynamic-update-slice_fusion), channel_id=1, source_target_pairs={{0,64},{64,128},{128,192},{192,0},{1,65},{65,129},{129,193},{193,1... | collective-permute-start | bytes 786440 | tf_op jit(solution)/shard_map/ppermute | solution.py:27
  47.8 9.2 %collective-permute-start.12 = (bf16[8,2,16,512]{3,2,1,0:T(8,128)(2,1)S(1)}, bf16[8,2,16,512]{3,2,1,0:T(8,128)(2,1)S(1)}, u32[]{:S(2)}, u32[]{:S(2)}) collective-permute-start(bf16[8,2,16,512]{3,2,1,0:T(8,128)(2,1)S(1)} %bitcast_dynamic-update-slice_fusion), channel_id=1, source_target_pairs={{0,128},{64,192},{128,0},{192,64},{1,129},{65,193},{129,1},{193,65... | collective-permute-start | bytes 786440 | tf_op jit(solution)/shard_map/ppermute | solution.py:27
  49.5 7.8 %collective-permute-start.13 = (bf16[8,2,16,512]{3,2,1,0:T(8,128)(2,1)S(1)}, bf16[8,2,16,512]{3,2,1,0:T(8,128)(2,1)S(1)}, u32[]{:S(2)}, u32[]{:S(2)}) collective-permute-start(bf16[8,2,16,512]{3,2,1,0:T(8,128)(2,1)S(1)} %bitcast_dynamic-update-slice_fusion), channel_id=1, source_target_pairs={{0,192},{64,0},{128,64},{192,128},{1,193},{65,1},{129,65},{193,129... | collective-permute-start | bytes 786440 | tf_op jit(solution)/shard_map/ppermute | solution.py:27
  50.2 2.8 %collective-permute-start.9 = (f32[8,224]{1,0:T(8,128)S(1)}, f32[8,224]{1,0:T(8,128)S(1)}, u32[]{:S(2)}, u32[]{:S(2)}) collective-permute-start(f32[8,224]{1,0:T(8,128)S(1)} %fusion.1), channel_id=1, source_target_pairs={{0,8},{8,0},{16,24},{24,16},{1,9},{9,1},{17,25},{25,17},{2,10},{10... | collective-permute-start | bytes 21512 | tf_op jit(solution)/shard_map/ppermute | solution.py:211
  53.0 4.0 %collective-permute-start.10 = (f32[8,224]{1,0:T(8,128)S(1)}, f32[8,224]{1,0:T(8,128)S(1)}, u32[]{:S(2)}, u32[]{:S(2)}) collective-permute-start(f32[8,224]{1,0:T(8,128)S(1)} %add.34), channel_id=1, source_target_pairs={{0,16},{8,24},{16,0},{24,8},{1,17},{9,25},{17,1},{25,9},{2,18},{10... | collective-permute-start | bytes 21512 | tf_op jit(solution)/shard_map/ppermute | solution.py:211
  57.4 22.3 %collective-permute-start.14 = (bf16[4,8,2,16,512]{4,3,2,1,0:T(8,128)(2,1)S(1)}, bf16[4,8,2,16,512]{4,3,2,1,0:T(8,128)(2,1)S(1)}, u32[]{:S(2)}, u32[]{:S(2)}) collective-permute-start(bf16[4,8,2,16,512]{4,3,2,1,0:T(8,128)(2,1)S(1)} %pad_maximum_fusion.own_ref), channel_id=1, source_target_pairs={{0,32},{32,0},{1,33},{33,1},{2,34},{34,2},{3,35},{35,3},{4,36},{36... | collective-permute-start | bytes 3145736 | tf_op jit(solution)/shard_map/ppermute | solution.py:27
  67.2 10.6 %collective-permute-start.15 = (f32[8,224]{1,0:T(8,128)S(1)}, f32[8,224]{1,0:T(8,128)S(1)}, u32[]{:S(2)}, u32[]{:S(2)}) collective-permute-start(f32[8,224]{1,0:T(8,128)S(1)} %add.35), channel_id=1, source_target_pairs={{0,32},{32,0},{1,33},{33,1},{2,34},{34,2},{3,35},{35,3},{4,36},{36... | collective-permute-start | bytes 21512 | tf_op jit(solution)/shard_map/ppermute | solution.py:211
  80.7 25.0 %all-to-all-start.1 = ((f32[8,72,224]{2,1,0:T(8,128)}), f32[8,72,224]{2,1,0:T(8,128)}, u32[]{:S(2)}, u32[]{:S(2)}) async-start(f32[8,72,224]{2,1,0:T(8,128)} %pad_maximum_fusion.1), calls=%async_computation.1 | async-start | bytes 1179648 | tf_op jit(solution)/shard_map/all_to_all | solution.py:31
  105.7 29.9 %all-to-all-start.2 = ((bf16[8,2,224,128]{3,2,1,0:T(8,128)(2,1)}), bf16[8,2,224,128]{3,2,1,0:T(8,128)(2,1)S(1)}, u32[]{:S(2)}, u32[]{:S(2)}) async-start(bf16[8,2,224,128]{3,2,1,0:T(8,128)(2,1)} %bitcast.54), calls=%async_computation.2 | async-start | bytes 1835008 | tf_op jit(solution)/shard_map/all_to_all | solution.py:31
  109.2 8.3 %collective-permute-start.16 = (f32[2,224,128]{2,1,0:T(8,128)}, f32[2,224,128]{2,1,0:T(8,128)S(1)}, u32[]{:S(2)}, u32[]{:S(2)}) collective-permute-start(f32[2,224,128]{2,1,0:T(8,128)} %copy-done.16), channel_id=1, source_target_pairs={{0,8},{8,16},{16,24},{24,0},{1,9},{9,17},{17,25},{25,1},{2,10},{10... | collective-permute-start | bytes 688136 | tf_op jit(solution)/shard_map/ppermute | solution.py:27
  110.6 13.0 %collective-permute-start.17 = (f32[2,224,128]{2,1,0:T(8,128)}, f32[2,224,128]{2,1,0:T(8,128)S(1)}, u32[]{:S(2)}, u32[]{:S(2)}) collective-permute-start(f32[2,224,128]{2,1,0:T(8,128)} %copy-done.15), channel_id=1, source_target_pairs={{0,16},{8,24},{16,0},{24,8},{1,17},{9,25},{17,1},{25,9},{2,18},{10... | collective-permute-start | bytes 688136 | tf_op jit(solution)/shard_map/ppermute | solution.py:27
  113.2 10.3 %collective-permute-start.18 = (f32[2,224,128]{2,1,0:T(8,128)}, f32[2,224,128]{2,1,0:T(8,128)S(1)}, u32[]{:S(2)}, u32[]{:S(2)}) collective-permute-start(f32[2,224,128]{2,1,0:T(8,128)} %copy-done.14), channel_id=1, source_target_pairs={{0,24},{8,0},{16,8},{24,16},{1,25},{9,1},{17,9},{25,17},{2,26},{10... | collective-permute-start | bytes 688136 | tf_op jit(solution)/shard_map/ppermute | solution.py:27
  125.1 31.7 %copy-start.6 = (bf16[2,224,128]{2,1,0:T(8,128)(2,1)}, bf16[2,224,128]{2,1,0:T(8,128)(2,1)S(1)}, u32[]{:S(2)}) copy-start(bf16[2,224,128]{2,1,0:T(8,128)(2,1)S(1)} %get-tuple-element.44.u0) | copy-start | bytes 344068
  125.1 5.0 %collective-permute-start.19 = (bf16[2,224,128]{2,1,0:T(8,128)(2,1)S(1)}, bf16[2,224,128]{2,1,0:T(8,128)(2,1)S(1)}, u32[]{:S(2)}, u32[]{:S(2)}) collective-permute-start(bf16[2,224,128]{2,1,0:T(8,128)(2,1)S(1)} %get-tuple-element.44.u0), channel_id=1, source_target_pairs={{0,8},{8,16},{16,24},{24,0},{1,9},{9,17},{17,25},{25,1},{2,10},{10... | collective-permute-start | bytes 344072 | tf_op jit(solution)/shard_map/ppermute | solution.py:27
  126.3 8.0 %collective-permute-start.20 = (bf16[2,224,128]{2,1,0:T(8,128)(2,1)S(1)}, bf16[2,224,128]{2,1,0:T(8,128)(2,1)S(1)}, u32[]{:S(2)}, u32[]{:S(2)}) collective-permute-start(bf16[2,224,128]{2,1,0:T(8,128)(2,1)S(1)} %get-tuple-element.44.u0), channel_id=1, source_target_pairs={{0,16},{8,24},{16,0},{24,8},{1,17},{9,25},{17,1},{25,9},{2,18},{10... | collective-permute-start | bytes 344072 | tf_op jit(solution)/shard_map/ppermute | solution.py:27
  129.1 5.2 %collective-permute-start.21 = (bf16[2,224,128]{2,1,0:T(8,128)(2,1)S(1)}, bf16[2,224,128]{2,1,0:T(8,128)(2,1)S(1)}, u32[]{:S(2)}, u32[]{:S(2)}) collective-permute-start(bf16[2,224,128]{2,1,0:T(8,128)(2,1)S(1)} %get-tuple-element.44.u0), channel_id=1, source_target_pairs={{0,24},{8,0},{16,8},{24,16},{1,25},{9,1},{17,9},{25,17},{2,26},{10... | collective-permute-start | bytes 344072 | tf_op jit(solution)/shard_map/ppermute | solution.py:27
  130.1 26.7 %copy-start.8 = (bf16[2,224,128]{2,1,0:T(8,128)(2,1)}, bf16[2,224,128]{2,1,0:T(8,128)(2,1)S(1)}, u32[]{:S(2)}) copy-start(bf16[2,224,128]{2,1,0:T(8,128)(2,1)S(1)} %collective-permute-done.19.u1) | copy-start | bytes 344068
  158.1 16.8 %collective-permute-start.22 = (bf16[128,1792]{1,0:T(8,128)(2,1)S(1)}, bf16[128,1792]{1,0:T(8,128)(2,1)}, u32[]{:S(2)}, u32[]{:S(2)}) collective-permute-start(bf16[128,1792]{1,0:T(8,128)(2,1)S(1)} %bitcast.45), channel_id=1, source_target_pairs={{0,64},{64,128},{128,192},{192,0},{1,65},{65,129},{129,193},{193,1... | collective-permute-start | bytes 1376264 | tf_op jit(solution)/shard_map/ppermute | solution.py:27
  165.9 21.1 %all-to-all-start.4 = ((bf16[8,224,128]{2,1,0:T(8,128)(2,1)}), bf16[8,224,128]{2,1,0:T(8,128)(2,1)S(1)}, u32[]{:S(2)}, u32[]{:S(2)}) async-start(bf16[8,224,128]{2,1,0:T(8,128)(2,1)} %copy-done.2), calls=%async_computation.4 | async-start | bytes 917504 | tf_op jit(solution)/shard_map/all_to_all | solution.py:31
  169.4 8.7 %collective-permute-start.24 = (bf16[128,1792]{1,0:T(8,128)(2,1)S(1)}, bf16[128,1792]{1,0:T(8,128)(2,1)S(1)}, u32[]{:S(2)}, u32[]{:S(2)}) collective-permute-start(bf16[128,1792]{1,0:T(8,128)(2,1)S(1)} %bitcast.46), channel_id=1, source_target_pairs={{0,192},{64,0},{128,64},{192,128},{1,193},{65,1},{129,65},{193,129... | collective-permute-start | bytes 1376264 | tf_op jit(solution)/shard_map/ppermute | solution.py:27
  171.1 22.6 %collective-permute-start.30 = (bf16[128,1792]{1,0:T(8,128)(2,1)S(1)}, bf16[128,1792]{1,0:T(8,128)(2,1)S(1)}, u32[]{:S(2)}, u32[]{:S(2)}) collective-permute-start(bf16[128,1792]{1,0:T(8,128)(2,1)S(1)} %bitcast.47), channel_id=1, source_target_pairs={{0,32},{32,0},{1,33},{33,1},{2,34},{34,2},{3,35},{35,3},{4,36},{36... | collective-permute-start | bytes 1376264 | tf_op jit(solution)/shard_map/ppermute | solution.py:27
  174.9 22.9 %collective-permute-start.28 = (bf16[128,1792]{1,0:T(8,128)(2,1)}, bf16[128,1792]{1,0:T(8,128)(2,1)S(1)}, u32[]{:S(2)}, u32[]{:S(2)}) collective-permute-start(bf16[128,1792]{1,0:T(8,128)(2,1)} %collective-permute-done.22.refs_0_), channel_id=1, source_target_pairs={{0,32},{32,0},{1,33},{33,1},{2,34},{34,2},{3,35},{35,3},{4,36},{36... | collective-permute-start | bytes 1376264 | tf_op jit(solution)/shard_map/ppermute | solution.py:27
  178.1 21.2 %collective-permute-start.29 = (bf16[128,1792]{1,0:T(8,128)(2,1)S(1)}, bf16[128,1792]{1,0:T(8,128)(2,1)}, u32[]{:S(2)}, u32[]{:S(2)}) collective-permute-start(bf16[128,1792]{1,0:T(8,128)(2,1)S(1)} %collective-permute-done.24.refs_1_), channel_id=1, source_target_pairs={{0,32},{32,0},{1,33},{33,1},{2,34},{34,2},{3,35},{35,3},{4,36},{36... | collective-permute-start | bytes 1376264 | tf_op jit(solution)/shard_map/ppermute | solution.py:27
  183.4 10.5 %collective-permute-start.23 = (bf16[64,1792]{1,0:T(8,128)(2,1)S(1)}, bf16[64,1792]{1,0:T(8,128)(2,1)S(1)}, u32[]{:S(2)}, u32[]{:S(2)}) collective-permute-start(bf16[64,1792]{1,0:T(8,128)(2,1)S(1)} %slice.26), channel_id=1, source_target_pairs={{0,64},{64,128},{128,192},{192,0},{1,65},{65,129},{129,193},{193,1... | collective-permute-start | bytes 688136 | tf_op jit(solution)/shard_map/ppermute | solution.py:27
  185.3 11.2 %collective-permute-start.25 = (bf16[64,1792]{1,0:T(8,128)(2,1)}, bf16[64,1792]{1,0:T(8,128)(2,1)}, u32[]{:S(2)}, u32[]{:S(2)}) collective-permute-start(bf16[64,1792]{1,0:T(8,128)(2,1)} %slice.27), channel_id=1, source_target_pairs={{0,192},{64,0},{128,64},{192,128},{1,193},{65,1},{129,65},{193,129... | collective-permute-start | bytes 688136 | tf_op jit(solution)/shard_map/ppermute | solution.py:27
  187.2 30.1 %all-to-all-start.5 = ((f32[8,64,224]{2,1,0:T(8,128)}), f32[8,64,224]{2,1,0:T(8,128)}, u32[]{:S(2)}, u32[]{:S(2)}) async-start(f32[8,64,224]{2,1,0:T(8,128)} %copy-done.5), calls=%async_computation.5 | async-start | bytes 1048576 | tf_op jit(solution)/shard_map/all_to_all | solution.py:31
  193.7 12.8 %collective-permute-start.31 = (bf16[128,1792]{1,0:T(8,128)(2,1)S(1)}, bf16[128,1792]{1,0:T(8,128)(2,1)S(1)}, u32[]{:S(2)}, u32[]{:S(2)}) collective-permute-start(bf16[128,1792]{1,0:T(8,128)(2,1)S(1)} %bitcast.49), channel_id=1, source_target_pairs={{0,64},{64,128},{128,192},{192,0},{1,65},{65,129},{129,193},{193,1... | collective-permute-start | bytes 1376264 | tf_op jit(solution)/shard_map/ppermute | solution.py:27
  193.8 12.7 %collective-permute-start.32 = (bf16[128,1792]{1,0:T(8,128)(2,1)S(1)}, bf16[128,1792]{1,0:T(8,128)(2,1)S(1)}, u32[]{:S(2)}, u32[]{:S(2)}) collective-permute-start(bf16[128,1792]{1,0:T(8,128)(2,1)S(1)} %bitcast.50), channel_id=1, source_target_pairs={{0,192},{64,0},{128,64},{192,128},{1,193},{65,1},{129,65},{193,129... | collective-permute-start | bytes 1376264 | tf_op jit(solution)/shard_map/ppermute | solution.py:27
  196.5 5.8 %collective-permute-start.26 = (bf16[64,1792]{1,0:T(8,128)(2,1)S(1)}, bf16[64,1792]{1,0:T(8,128)(2,1)S(1)}, u32[]{:S(2)}, u32[]{:S(2)}) collective-permute-start(bf16[64,1792]{1,0:T(8,128)(2,1)S(1)} %collective-permute-done.23.refs_0_), channel_id=1, source_target_pairs={{0,32},{32,0},{1,33},{33,1},{2,34},{34,2},{3,35},{35,3},{4,36},{36... | collective-permute-start | bytes 688136 | tf_op jit(solution)/shard_map/ppermute | solution.py:27
  197.7 4.5 %collective-permute-start.27 = (bf16[64,1792]{1,0:T(8,128)(2,1)}, bf16[64,1792]{1,0:T(8,128)(2,1)S(1)}, u32[]{:S(2)}, u32[]{:S(2)}) collective-permute-start(bf16[64,1792]{1,0:T(8,128)(2,1)} %collective-permute-done.25.refs_1_), channel_id=1, source_target_pairs={{0,32},{32,0},{1,33},{33,1},{2,34},{34,2},{3,35},{35,3},{4,36},{36... | collective-permute-start | bytes 688136 | tf_op jit(solution)/shard_map/ppermute | solution.py:27
  199.3 11.5 %collective-permute-start.35 = (bf16[128,1792]{1,0:T(8,128)(2,1)S(1)}, bf16[128,1792]{1,0:T(8,128)(2,1)S(1)}, u32[]{:S(2)}, u32[]{:S(2)}) collective-permute-start(bf16[128,1792]{1,0:T(8,128)(2,1)S(1)} %bitcast.51), channel_id=1, source_target_pairs={{0,32},{32,0},{1,33},{33,1},{2,34},{34,2},{3,35},{35,3},{4,36},{36... | collective-permute-start | bytes 1376264 | tf_op jit(solution)/shard_map/ppermute | solution.py:27
  206.6 5.8 %collective-permute-start.33 = (bf16[128,1792]{1,0:T(8,128)(2,1)S(1)}, bf16[128,1792]{1,0:T(8,128)(2,1)S(1)}, u32[]{:S(2)}, u32[]{:S(2)}) collective-permute-start(bf16[128,1792]{1,0:T(8,128)(2,1)S(1)} %collective-permute-done.31.refs_0_), channel_id=1, source_target_pairs={{0,32},{32,0},{1,33},{33,1},{2,34},{34,2},{3,35},{35,3},{4,36},{36... | collective-permute-start | bytes 1376264 | tf_op jit(solution)/shard_map/ppermute | solution.py:27
  208.0 4.4 %collective-permute-start.34 = (bf16[128,1792]{1,0:T(8,128)(2,1)S(1)}, bf16[128,1792]{1,0:T(8,128)(2,1)S(1)}, u32[]{:S(2)}, u32[]{:S(2)}) collective-permute-start(bf16[128,1792]{1,0:T(8,128)(2,1)S(1)} %collective-permute-done.32.refs_1_), channel_id=1, source_target_pairs={{0,32},{32,0},{1,33},{33,1},{2,34},{34,2},{3,35},{35,3},{4,36},{36... | collective-permute-start | bytes 1376264 | tf_op jit(solution)/shard_map/ppermute | solution.py:27
  208.0 8.0 %collective-permute-start.36 = (bf16[64,1792]{1,0:T(8,128)(2,1)S(1)}, bf16[64,1792]{1,0:T(8,128)(2,1)S(1)}, u32[]{:S(2)}, u32[]{:S(2)}) collective-permute-start(bf16[64,1792]{1,0:T(8,128)(2,1)S(1)} %slice.22), channel_id=1, source_target_pairs={{0,64},{64,128},{128,192},{192,0},{1,65},{65,129},{129,193},{193,1... | collective-permute-start | bytes 688136 | tf_op jit(solution)/shard_map/ppermute | solution.py:27
  208.1 7.9 %collective-permute-start.37 = (bf16[64,1792]{1,0:T(8,128)(2,1)S(1)}, bf16[64,1792]{1,0:T(8,128)(2,1)S(1)}, u32[]{:S(2)}, u32[]{:S(2)}) collective-permute-start(bf16[64,1792]{1,0:T(8,128)(2,1)S(1)} %slice.23), channel_id=1, source_target_pairs={{0,192},{64,0},{128,64},{192,128},{1,193},{65,1},{129,65},{193,129... | collective-permute-start | bytes 688136 | tf_op jit(solution)/shard_map/ppermute | solution.py:27
  216.0 4.4 %collective-permute-start.38 = (bf16[64,1792]{1,0:T(8,128)(2,1)S(1)}, bf16[64,1792]{1,0:T(8,128)(2,1)S(1)}, u32[]{:S(2)}, u32[]{:S(2)}) collective-permute-start(bf16[64,1792]{1,0:T(8,128)(2,1)S(1)} %collective-permute-done.36.refs_0_), channel_id=1, source_target_pairs={{0,32},{32,0},{1,33},{33,1},{2,34},{34,2},{3,35},{35,3},{4,36},{36... | collective-permute-start | bytes 688136 | tf_op jit(solution)/shard_map/ppermute | solution.py:27
  217.3 3.1 %collective-permute-start.39 = (bf16[64,1792]{1,0:T(8,128)(2,1)S(1)}, bf16[64,1792]{1,0:T(8,128)(2,1)S(1)}, u32[]{:S(2)}, u32[]{:S(2)}) collective-permute-start(bf16[64,1792]{1,0:T(8,128)(2,1)S(1)} %collective-permute-done.37.refs_1_), channel_id=1, source_target_pairs={{0,32},{32,0},{1,33},{33,1},{2,34},{34,2},{3,35},{35,3},{4,36},{36... | collective-permute-start | bytes 688136 | tf_op jit(solution)/shard_map/ppermute | solution.py:27
  (15 other events, 69.6 us)

commit v2 on v1

--- a/solution.py
+++ b/solution.py
@@ -39,31 +39,129 @@
     return lax.optimization_barrier((first, second))[1]
 
 
+def pack_kernel(extra, at_ref, v_ref, *refs):
+    out_ref = refs[-2] if extra else refs[-1]
+    nz = out_ref.shape[0]
+    cols = v_ref.shape[2] // nz
+    total = None
+    for m in range(MATS):
+        turned = jnp.transpose(v_ref[m])
+        for z in range(nz):
+            out_ref[z, m, :cols] = turned[z * cols : (z + 1) * cols]
+        if extra:
+            wide = v_ref[m].astype(F32)
+            squares = jnp.sum(wide * wide, axis=0, keepdims=True)
+            total = squares if total is None else total + squares
+    if extra:
+        basis_ref, tile_ref = refs[0], refs[-1]
+        tile_ref[...] = jnp.broadcast_to(jnp.sum(total, axis=1, keepdims=True), tile_ref.shape)
+        part = basis_ref.shape[1] // 8
+        start = pl.multiple_of((at_ref[0] * 2 + at_ref[1]) * part, part)
+        width = out_ref.shape[3]
+        for m in range(MATS):
+            piece = basis_ref[m, pl.ds(start, part)]
+            for k in range(piece.shape[1] // width):
+                low = cols + k * part
+                for z in range(nz):
+                    out_ref[z, m, low : low + part] = piece[:, k * width : (k + 1) * width]
+
+
+def pack(at, v, nz, basis=None):
+    mats, rows, cols = v.shape
+    cols //= nz
+    extra = basis is not None
+    more = basis.shape[1] // 8 * (basis.shape[2] // rows) if extra else 0
+    shapes = [jax.ShapeDtypeStruct((nz, mats, cols + more, rows), BF16)]
+    if extra:
+        shapes.append(jax.ShapeDtypeStruct((8, cols), F32))
+    given = (basis,) if extra else ()
+    out = pl.pallas_call(
+        functools.partial(pack_kernel, extra),
+        out_shape=shapes,
+        in_specs=[SMEM] + [VMEM] * (1 + len(given)),
+        out_specs=[VMEM] * len(shapes),
+        compiler_params=PARAMS,
+        cost_estimate=cost(2e9, 2 * 2**20),
+        name="pack",
+    )(at, v, *given)
+    return out if extra else out[0]
+
+
+def pack_state_kernel(one_ref, two_ref, tile_ref, out_ref):
+    nz, _, cols = out_ref.shape
+    ranks = one_ref.shape[1]
+    for k, ref in enumerate((one_ref, two_ref)):
+        for m in range(MATS):
+            low = (k * MATS + m) * ranks
+            for z in range(nz):
+                out_ref[z, low : low + ranks] = ref[m, :, z * cols : (z + 1) * cols]
+    for z in range(nz):
+        out_ref[z, 2 * MATS * ranks :] = tile_ref[...]
+
+
+def pack_state(one, two, tile, nz):
+    mats, ranks, cols = one.shape
+    return pl.pallas_call(
+        pack_state_kernel,
+        out_shape=jax.ShapeDtypeStruct((nz, 2 * mats * ranks + tile.shape[0], cols // nz), F32),
+        in_specs=[VMEM] * 3,
+        out_specs=VMEM,
+        compiler_params=PARAMS,
+        cost_estimate=cost(2e9, 2**20),
+        name="pack_state",
+    )(one, two, tile)
+
+
+def unpack_state_kernel(in_ref, one_ref, two_ref):
+    nz, _, _ = in_ref.shape
+    ranks = one_ref.shape[1]
+    for k, ref in enumerate((one_ref, two_ref)):
+        for m in range(MATS):
+            low = (k * MATS + m) * ranks
+            ref[m] = jnp.concatenate([in_ref[z, low : low + ranks] for z in range(nz)], axis=1)
+
+
+def unpack_state(held):
+    nz, kinds, cols = held.shape
+    shape = jax.ShapeDtypeStruct((MATS, kinds // (2 * MATS), nz * cols), F32)
+    return pl.pallas_call(
+        unpack_state_kernel,
+        out_shape=[shape, shape],
+        in_specs=[VMEM],
+        out_specs=[VMEM] * 2,
+        compiler_params=PARAMS,
+        cost_estimate=cost(2e9, 2**20),
+        name="unpack_state",
+    )(held)
+
+
 def project_kernel(at_ref, g_ref, own_ref, peer_ref, basis_ref, *refs):
     outs, total_ref = refs[:-1], refs[-1]
-    x, core, y, z = (at_ref[i] for i in range(4))
-    nx, nz, _, part, _ = own_ref.shape
+    x, core, y = (at_ref[i] for i in range(3))
+    nx, nz, _, size, width = own_ref.shape
+    rank = basis_ref.shape[3]
+    part = size * width // rank
+    cols = total_ref.shape[1]
     ny = len(outs)
-    width = outs[0].shape[-1]
-
-    def gather(zz, _):
-        e = lax.rem(z - zz + nz, nz)
+
+    def gather(z, _):
         for m in range(MATS):
             for xa in range(nx):
                 d = lax.rem(x - xa + nx, nx)
-                ours, theirs = own_ref[d, e, m], peer_ref[d, e, m]
-                basis_ref[m, zz, 2 * xa * part : (2 * xa + 1) * part] = jnp.where(
-                    core == 0, ours, theirs
-                )
-                basis_ref[m, zz, (2 * xa + 1) * part : (2 * xa + 2) * part] = jnp.where(
-                    core == 0, theirs, ours
-                )
+                ours, theirs = own_ref[d, z, m], peer_ref[d, z, m]
+                pair = (jnp.where(core == 0, ours, theirs), jnp.where(core == 0, theirs, ours))
+                for c in range(2):
+                    low = (2 * xa + c) * part
+                    for k in range(rank // width):
+                        basis_ref[m, z, low : low + part, k * width : (k + 1) * width] = pair[c][
+                            k * part : (k + 1) * part
+                        ]
         return 0
 
     lax.fori_loop(0, nz, gather, 0)
 
     def multiply(m, _):
-        left = jnp.concatenate([g_ref[zz, m] for zz in range(nz)], axis=1)
+        left = jnp.concatenate([g_ref[z, m, :cols] for z in range(nz)], axis=1)
         right = basis_ref[m].reshape(left.shape[1], -1)
         total_ref[m] = jnp.dot(left, right, preferred_element_type=F32)
         return 0
@@ -74,9 +172,8 @@
         outs[d][...] = total_ref[:, :, pl.ds(start, width)]
 
 
-def project(at, g, own, peer, parts):
-    nz, mats, cols, rows = g.shape
-    rank = own.shape[-1]
+def project(at, g, own, peer, cols, rank, parts):
+    nz, mats, _, rows = g.shape
     basis, *out = pl.pallas_call(
         project_kernel,
         out_shape=[jax.ShapeDtypeStruct((mats, nz, rows, rank), BF16)]
@@ -219,44 +316,29 @@
     nx, nc, ny, nz = (lax.axis_size(a) for a in ("x", "core", "y", "z"))
     mats, rows, cols = grads.shape
     rank = basis.shape[2]
-    part = rows // (nx * nc)
     ranks = rank // (ny * nz)
     at = jnp.stack([x, core, y, z])
 
-    def by_block(v):
-        blocks = jnp.swapaxes(v, 1, 2).reshape(mats, nz, cols // nz, rows)
-        return blocks, jnp.swapaxes(blocks, 0, 1)
-
-    piece = lax.dynamic_slice_in_dim(basis, (x * nc + core) * part, part, axis=1)
-    held = jnp.stack([piece] + [shift(piece, "z", k) for k in range(1, nz)])
-    turned, sent = by_block(grads)
+    sent, tile = pack(at, grads, nz, basis)
     mine = exchange(sent, "z")
-    grad_wide = turned.astype(F32)
-    tile = jnp.full((8, cols // nz), jnp.sum(grad_wide * grad_wide), F32)
-    tile = sum_over(tile, "x")
-    tile, held = lax.optimization_barrier((tile, held))
-    tile = sum_over(tile, "y")
+    for axis in ("x", "y", "core"):
+        tile = sum_over(tile, axis)
+    state = pack_state(moment1, moment2, tile, nz)
+    w = pack(at, weights, nz)
+
+    held = mine[:, :, cols // nz :]
     own = jnp.stack([held] + [shift(held, "x", k) for k in range(1, nx)])
-    tile, own = lax.optimization_barrier((tile, own))
-    tile = sum_over(tile, "core")
     peer = shift(own, "core", 1)
-
-    state = jnp.concatenate([moment1, moment2], axis=0).reshape(2 * mats * ranks, nz, cols // nz)
-    state = jnp.concatenate([jnp.swapaxes(state, 0, 1), jnp.stack([tile] * nz)], axis=1)
-    w = by_block(weights)[1]
-    mine, peer, state, w = lax.optimization_barrier((mine, peer, state, w))
-    state = exchange(state, "z")
-
-    gathered, parts = project(at, mine, own, peer, ny)
-    gathered, w = lax.optimization_barrier((gathered, w))
+    state = exchange(before(mine, state), "z")
     w = exchange(before(state, w), "z")
+
+    gathered, parts = project(at, mine, own, peer, cols // nz, rank, ny)
     parts = [parts[0]] + [shift(parts[k], "y", k) for k in range(1, ny)]
     summed = (parts[0] + parts[1]) + (parts[2] + parts[3])
     news, update = moments(state, ranks, summed)
     updates = [update] + [shift(update, "y", k) for k in range(1, ny)]
     fresh = [exchange(back(m, at, gathered, w, updates), "z") for m in range(mats)]
-    news = exchange(before(fresh[-1], news), "z")
-    news = jnp.swapaxes(news, 0, 1).reshape(2, mats, ranks, cols)
+    news = unpack_state(exchange(before(fresh[-1], news), "z"))
     fresh = [jnp.swapaxes(f.reshape(cols, rows), 0, 1) for f in fresh]
 
     half = rows // 2

time: 223 us -> 194 us (0.87)
  local copies, waits for them, and re-layouts: 28.6 us -> 14.6 us
  starting transfers between devices: 95.5 us -> 81.5 us
  Pallas kernels: 18.5 us -> 24.4 us
  other arithmetic: 6.32 us -> 1.29 us
  waiting for transfers between devices: 53.1 us -> 49.2 us
    ppermute x35 -> x28, starting transfers between devices: 60.6 us -> 39.2 us  [shift(): return lax.ppermute(v, axis, [(i, (i + k) % n) for i in range(n)])]
    reshape x4 -> x0, local copies, waits for them, and re-layouts: 7.37 us -> none  [the longest x2 4.15 us: step(): jnp.concatenate([moment1, moment2], axis=0)]
    pallas_call x0 -> x4, Pallas kernels: none -> 5.56 us  [the longest x2 3.67 us: pack(): pl.pallas_call(functools.partial(pack_kernel, extra), out_shape=shapes, i...]
    all_to_all x5, starting transfers between devices: 25.2 us -> 29.2 us  [exchange(): return lax.all_to_all(v, axis, split_axis=0, concat_axis=0, tiled=True)]
    unnamed x45 -> x42, local copies, waits for them, and re-layouts: 14.4 us -> 10.6 us
    concatenate x2 -> x0, other arithmetic: 3.67 us -> none  [the longest x1 1.92 us: step(): jnp.concatenate([jnp.swapaxes(state, 0, 1), jnp.stack([tile] * nz)], axis=1)]
    ppermute x35 -> x28, waiting for transfers between devices: 35 us -> 31.4 us  [shift(): return lax.ppermute(v, axis, [(i, (i + k) % n) for i in range(n)])]
    ppermute x5, starting transfers between devices: 9.69 us -> 13.1 us  [sum_over(): tile = tile + lax.ppermute(tile, axis, [(i, i ^ step) for i in range(n)])]
  transfers between devices with their start and end apart: 45 -> 38, of which waited for: 16 -> 18; matrix products, arithmetic and copies ran while one was open for 9% -> 2% of each run, Pallas kernels for 7% -> 10%
where the time goes in v2:
time: 194 us; the launch traced here: 193 us
  starting transfers between devices  81.5 us (42%)
  waiting for transfers between devices  49.2 us (25%)
  Pallas kernels  24.4 us (13%)
  blocking collectives  20.8 us (11%)
  local copies, waits for them, and re-layouts  14.6 us (8%)
    ppermute x28, starting transfers between devices, shift(): return lax.ppermute(v, axis, [(i, (i + k) % n) for i in range(n)])  39.2 us
    ppermute x28, waiting for transfers between devices, shift(): return lax.ppermute(v, axis, [(i, (i + k) % n) for i in range(n)])  31.4 us
    all_to_all x5, starting transfers between devices, exchange(): return lax.all_to_all(v, axis, split_axis=0, concat_axis=0, tiled=True)  29.2 us
    all_to_all x1, blocking collectives, exchange(): return lax.all_to_all(v, axis, split_axis=0, concat_axis=0, tiled=True)  20.8 us
    ppermute x5, starting transfers between devices, sum_over(): tile = tile + lax.ppermute(tile, axis, [(i, i ^ step) for i in range(n)])  13.1 us
    all_to_all x5, waiting for transfers between devices, exchange(): return lax.all_to_all(v, axis, split_axis=0, concat_axis=0, tiled=True)  11.6 us
    pallas_call x6, Pallas kernels, place(): pl.pallas_call(functools.partial(place_kernel, m, spots), out_shape=jax.S...  10.7 us
    unnamed x42, local copies, waits for them, and re-layouts  10.6 us
  transfers between devices with their start and end apart: 38, of which 18 were waited for; matrix products, arithmetic and copies ran while one was open for 2% of the time, Pallas kernels for 10%

profile of v2, /device:TPU:1, one launch (start us, length us, event | category | flops | bytes accessed | tf_op | source)
XLA Modules:
  0.0 192.9 jit_solution(16535879636781030029)
XLA Ops:
  2.9 1.9 pack.2
  4.8 9.1 %all-to-all-start = ((bf16[8,2,288,128]{3,2,1,0:T(8,128)(2,1)}), bf16[8,2,288,128]{3,2,1,0:T(8,128)(2,1)S(1)}, u32[]{:S(2)}, u32[]{:S(2)}) async-start(bf16[8,2,288,128]{3,2,1,0:T(8,128)(2,1)} %get-tuple-element.23), calls=%async_computation | async-start | bytes 2359296 | tf_op jit(solution)/shard_map/all_to_all | solution.py:31
  15.1 1.3 collective-permute-done.4
  16.4 2.7 %collective-permute-start.5 = (f32[8,224]{1,0:T(8,128)S(1)}, f32[8,224]{1,0:T(8,128)S(1)}, u32[]{:S(2)}, u32[]{:S(2)}) collective-permute-start(f32[8,224]{1,0:T(8,128)S(1)} %add.24), channel_id=1, source_target_pairs={{0,128},{64,192},{128,0},{192,64},{1,129},{65,193},{129,1},{193,65... | collective-permute-start | bytes 21512 | tf_op jit(solution)/shard_map/ppermute | solution.py:308
  20.4 1.3 collective-permute-start.6
  21.7 1.5 collective-permute-done.6
  23.2 2.9 %collective-permute-start.7 = (f32[8,224]{1,0:T(8,128)S(1)}, f32[8,224]{1,0:T(8,128)S(1)}, u32[]{:S(2)}, u32[]{:S(2)}) collective-permute-start(f32[8,224]{1,0:T(8,128)S(1)} %add.26), channel_id=1, source_target_pairs={{0,16},{8,24},{16,0},{24,8},{1,17},{9,25},{17,1},{25,9},{2,18},{10... | collective-permute-start | bytes 21512 | tf_op jit(solution)/shard_map/ppermute | solution.py:308
  26.1 1.4 collective-permute-done.7
  27.5 5.0 %collective-permute-start.8 = (f32[8,224]{1,0:T(8,128)S(1)}, f32[8,224]{1,0:T(8,128)S(1)}, u32[]{:S(2)}, u32[]{:S(2)}) collective-permute-start(f32[8,224]{1,0:T(8,128)S(1)} %add.27), channel_id=1, source_target_pairs={{0,32},{32,0},{1,33},{33,1},{2,34},{34,2},{3,35},{35,3},{4,36},{36... | collective-permute-start | bytes 21512 | tf_op jit(solution)/shard_map/ppermute | solution.py:308
  34.3 11.6 %all-to-all-done.g_ref = bf16[8,2,288,128]{3,2,1,0:T(8,128)(2,1)S(1)} async-done(((bf16[8,2,288,128]{3,2,1,0:T(8,128)(2,1)}), bf16[8,2,288,128]{3,2,1,0:T(8,128)(2,1)S(1)}, u32[]{:S(2)}, u32[]{:S(2)}) %all-to-all-start) | async-done | bytes 1179680 | tf_op jit(solution)/shard_map/all_to_all | solution.py:31
  45.9 3.5 %all-to-all-start.1 = ((f32[8,72,224]{2,1,0:T(8,128)}), f32[8,72,224]{2,1,0:T(8,128)S(1)}, u32[]{:S(2)}, u32[]{:S(2)}) async-start(f32[8,72,224]{2,1,0:T(8,128)} %pack_state.1), calls=%async_computation.1 | async-start | bytes 1179648 | tf_op jit(solution)/shard_map/all_to_all | solution.py:31
  49.6 1.3 collective-permute-start
  50.9 2.5 %collective-permute-start.1 = (bf16[8,2,64,128]{3,2,1,0:T(8,128)(2,1)S(1)}, bf16[8,2,64,128]{3,2,1,0:T(8,128)(2,1)S(1)}, u32[]{:S(2)}, u32[]{:S(2)}) collective-permute-start(bf16[8,2,64,128]{3,2,1,0:T(8,128)(2,1)S(1)} %get-tuple-element.44), channel_id=1, source_target_pairs={{0,128},{64,192},{128,0},{192,64},{1,129},{65,193},{129,1},{193,65... | collective-permute-start | bytes 786440 | tf_op jit(solution)/shard_map/ppermute | solution.py:27
  54.5 3.8 %collective-permute-done = bf16[8,2,64,128]{3,2,1,0:T(8,128)(2,1)S(1)} collective-permute-done((bf16[8,2,64,128]{3,2,1,0:T(8,128)(2,1)S(1)}, bf16[8,2,64,128]{3,2,1,0:T(8,128)(2,1)S(1)}, u32[]{:S(2)}, u32[]{:S(2)}) %collective-permute-start) | collective-permute-done | bytes 262176 | tf_op jit(solution)/shard_map/ppermute | solution.py:27
  58.3 6.6 %collective-permute-done.1 = bf16[8,2,64,128]{3,2,1,0:T(8,128)(2,1)S(1)} collective-permute-done((bf16[8,2,64,128]{3,2,1,0:T(8,128)(2,1)S(1)}, bf16[8,2,64,128]{3,2,1,0:T(8,128)(2,1)S(1)}, u32[]{:S(2)}, u32[]{:S(2)}) %collective-permute-start.1) | collective-permute-done | bytes 262176 | tf_op jit(solution)/shard_map/ppermute | solution.py:27
  66.0 1.3 collective-permute-start.3
  67.4 1.8 pack.3
  69.1 6.6 %all-to-all-start.2 = ((bf16[8,2,224,128]{3,2,1,0:T(8,128)(2,1)}), bf16[8,2,224,128]{3,2,1,0:T(8,128)(2,1)S(1)}, u32[]{:S(2)}, u32[]{:S(2)}) async-start(bf16[8,2,224,128]{3,2,1,0:T(8,128)(2,1)} %pack.3), calls=%async_computation.2 | async-start | bytes 1835008 | tf_op jit(solution)/shard_map/all_to_all | solution.py:31
  77.0 2.9 %project.1 = (bf16[2,8,128,512]{3,2,1,0:T(8,128)(2,1)S(1)}, f32[2,224,128]{2,1,0:T(8,128)S(1)}, f32[2,224,128]{2,1,0:T(8,128)S(1)}, f32[2,224,128]{2,1,0:T(8,128)S(1)}, f32[2,224,128]{2,1,0:T(8,128)S(1)}) custom-call(s32[4]{0:T(128)S(1)} %pad_add_fusion.at_ref, bf16[8,2,288,128]{3,2,1,0:T(8,128)(2,1)S(1)} %copy-done.1, ...), custom_call_target="tpu_custom_call" | custom-call | flops 469762048 | bytes 4194304 | tf_op jit(solution)/shard_map/project/pallas_call | solution.py:177
  79.9 3.0 %collective-permute-start.10 = (f32[2,224,128]{2,1,0:T(8,128)S(1)}, f32[2,224,128]{2,1,0:T(8,128)S(1)}, u32[]{:S(2)}, u32[]{:S(2)}) collective-permute-start(f32[2,224,128]{2,1,0:T(8,128)S(1)} %get-tuple-element.30), channel_id=1, source_target_pairs={{0,16},{8,24},{16,0},{24,8},{1,17},{9,25},{17,1},{25,9},{2,18},{10... | collective-permute-start | bytes 688136 | tf_op jit(solution)/shard_map/ppermute | solution.py:27
  84.4 4.0 %collective-permute-done.10 = f32[2,224,128]{2,1,0:T(8,128)S(1)} collective-permute-done((f32[2,224,128]{2,1,0:T(8,128)S(1)}, f32[2,224,128]{2,1,0:T(8,128)S(1)}, u32[]{:S(2)}, u32[]{:S(2)}) %collective-permute-start.10) | collective-permute-done | bytes 229408 | tf_op jit(solution)/shard_map/ppermute | solution.py:27
  88.4 5.3 %collective-permute-done.11 = f32[2,224,128]{2,1,0:T(8,128)S(1)} collective-permute-done((f32[2,224,128]{2,1,0:T(8,128)S(1)}, f32[2,224,128]{2,1,0:T(8,128)S(1)}, u32[]{:S(2)}, u32[]{:S(2)}) %collective-permute-start.11) | collective-permute-done | bytes 229408 | tf_op jit(solution)/shard_map/ppermute | solution.py:27
  95.3 1.6 collective-permute-start.12
  96.9 2.6 %collective-permute-start.13 = (bf16[2,224,128]{2,1,0:T(8,128)(2,1)S(1)}, bf16[2,224,128]{2,1,0:T(8,128)(2,1)S(1)}, u32[]{:S(2)}, u32[]{:S(2)}) collective-permute-start(bf16[2,224,128]{2,1,0:T(8,128)(2,1)S(1)} %get-tuple-element.32.u0), channel_id=1, source_target_pairs={{0,16},{8,24},{16,0},{24,8},{1,17},{9,25},{17,1},{25,9},{2,18},{10... | collective-permute-start | bytes 344072 | tf_op jit(solution)/shard_map/ppermute | solution.py:27
  100.8 3.9 %collective-permute-done.13.u2 = bf16[2,224,128]{2,1,0:T(8,128)(2,1)S(1)} collective-permute-done((bf16[2,224,128]{2,1,0:T(8,128)(2,1)S(1)}, bf16[2,224,128]{2,1,0:T(8,128)(2,1)S(1)}, u32[]{:S(2)}, u32[]{:S(2)}) %collective-permute-start.13) | collective-permute-done | bytes 114720 | tf_op jit(solution)/shard_map/ppermute | solution.py:27
  104.7 2.4 %back.2 = bf16[8,224,128]{2,1,0:T(8,128)(2,1)S(1)} custom-call(s32[4]{0:T(128)S(1)} %pad_add_fusion.at_ref, bf16[2,8,128,512]{3,2,1,0:T(8,128)(2,1)S(1)} %get-tuple-element.24.basis_ref, bf16[8,2,224,128]{3,2,1,0:T(8,128)(2,1)S(1)} %all-to-all-done.2.w_ref, bf16[2,224,128]{2,1,0:T(8,128)(2,1)S(1)} %get-tuple-element.32.u0, ...), custom_call_target="tpu_custom_call" | custom-call | flops 234881024 | bytes 3145728 | tf_op jit(solution)/shard_map/back/pallas_call | solution.py:253
  107.1 20.8 %all_to_all.30 = bf16[8,224,128]{2,1,0:T(8,128)(2,1)} all-to-all(bf16[8,224,128]{2,1,0:T(8,128)(2,1)S(1)} %back.2), channel_id=1, replica_groups=mesh['x'=4,'core'=2,'y'=4,'z'=8] {'z'}, dimensions={0} | all-to-all | bytes 917504 | tf_op jit(solution)/shard_map/all_to_all | solution.py:31
  133.9 2.4 %back.3 = bf16[8,224,128]{2,1,0:T(8,128)(2,1)S(1)} custom-call(s32[4]{0:T(128)S(1)} %pad_add_fusion.at_ref, bf16[2,8,128,512]{3,2,1,0:T(8,128)(2,1)S(1)} %get-tuple-element.24.basis_ref, bf16[8,2,224,128]{3,2,1,0:T(8,128)(2,1)S(1)} %all-to-all-done.2.w_ref, bf16[2,224,128]{2,1,0:T(8,128)(2,1)S(1)} %copy-done.9, bf16[2,224,128]{2,1,0:T(8,128)(2,1)S(1)} %copy-done.11, ...), custom_call_target="tpu_custom_call" | custom-call | flops 234881024 | bytes 3145728 | tf_op jit(solution)/shard_map/back/pallas_call | solution.py:253
  137.1 3.5 %all-to-all-start.4 = ((bf16[8,224,128]{2,1,0:T(8,128)(2,1)}), bf16[8,224,128]{2,1,0:T(8,128)(2,1)S(1)}, u32[]{:S(2)}, u32[]{:S(2)}) async-start(bf16[8,224,128]{2,1,0:T(8,128)(2,1)} %copy-done.2), calls=%async_computation.4 | async-start | bytes 917504 | tf_op jit(solution)/shard_map/all_to_all | solution.py:31
  140.6 1.7 collective-permute-start.17
  142.2 3.4 %collective-permute-start.23 = (bf16[128,1792]{1,0:T(8,128)(2,1)S(1)}, bf16[128,1792]{1,0:T(8,128)(2,1)S(1)}, u32[]{:S(2)}, u32[]{:S(2)}) collective-permute-start(bf16[128,1792]{1,0:T(8,128)(2,1)S(1)} %bitcast.15), channel_id=1, source_target_pairs={{0,32},{32,0},{1,33},{33,1},{2,34},{34,2},{3,35},{35,3},{4,36},{36... | collective-permute-start | bytes 1376264 | tf_op jit(solution)/shard_map/ppermute | solution.py:27
  145.6 4.0 %collective-permute-done.17.refs_1_ = bf16[128,1792]{1,0:T(8,128)(2,1)S(1)} collective-permute-done((bf16[128,1792]{1,0:T(8,128)(2,1)S(1)}, bf16[128,1792]{1,0:T(8,128)(2,1)S(1)}, u32[]{:S(2)}, u32[]{:S(2)}) %collective-permute-start.17) | collective-permute-done | bytes 458784 | tf_op jit(solution)/shard_map/ppermute | solution.py:27
  149.7 3.9 %collective-permute-start.22 = (bf16[128,1792]{1,0:T(8,128)(2,1)S(1)}, bf16[128,1792]{1,0:T(8,128)(2,1)}, u32[]{:S(2)}, u32[]{:S(2)}) collective-permute-start(bf16[128,1792]{1,0:T(8,128)(2,1)S(1)} %collective-permute-done.17.refs_1_), channel_id=1, source_target_pairs={{0,32},{32,0},{1,33},{33,1},{2,34},{34,2},{3,35},{35,3},{4,36},{36... | collective-permute-start | bytes 1376264 | tf_op jit(solution)/shard_map/ppermute | solution.py:27
  153.6 1.6 slice.21
  156.9 1.8 collective-permute-start.18
  158.9 6.5 %all-to-all-start.5 = ((f32[8,64,224]{2,1,0:T(8,128)}), f32[8,64,224]{2,1,0:T(8,128)S(1)}, u32[]{:S(2)}, u32[]{:S(2)}) async-start(f32[8,64,224]{2,1,0:T(8,128)} %copy-done.5), calls=%async_computation.5 | async-start | bytes 1048576 | tf_op jit(solution)/shard_map/all_to_all | solution.py:31
  166.2 2.7 %collective-permute-start.25 = (bf16[128,1792]{1,0:T(8,128)(2,1)S(1)}, bf16[128,1792]{1,0:T(8,128)(2,1)S(1)}, u32[]{:S(2)}, u32[]{:S(2)}) collective-permute-start(bf16[128,1792]{1,0:T(8,128)(2,1)S(1)} %bitcast.18), channel_id=1, source_target_pairs={{0,192},{64,0},{128,64},{192,128},{1,193},{65,1},{129,65},{193,129... | collective-permute-start | bytes 1376264 | tf_op jit(solution)/shard_map/ppermute | solution.py:27
  168.9 1.3 collective-permute-start.19
  171.3 1.5 place.6.refs_4_
  173.3 2.4 %place.7.refs_4_ = bf16[2,128,14336]{2,1,0:T(8,128)(2,1)} custom-call(s32[4]{0:T(128)S(1)} %pad_add_fusion.at_ref, bf16[128,1792]{1,0:T(8,128)(2,1)} %collective-permute-done.15.refs_0_, bf16[128,1792]{1,0:T(8,128)(2,1)S(1)} %collective-permute-done.17.refs_1_, ...), custom_call_target="tpu_custom_call", output_to_operand_aliasing={{}: (5, {})} | custom-call | flops 2000000000 | bytes 3670016 | tf_op jit(solution)/shard_map/place/pallas_call | solution.py:291
  175.8 2.0 %place.8.refs_2_ = bf16[2,128,14336]{2,1,0:T(8,128)(2,1)} custom-call(s32[4]{0:T(128)S(1)} %pad_add_fusion.at_ref, bf16[64,1792]{1,0:T(8,128)(2,1)} %collective-permute-done.16.refs_0_, bf16[64,1792]{1,0:T(8,128)(2,1)} %collective-permute-done.18.refs_1_, bf16[64,1792]{1,0:T(8,128)(2,1)S(1)} %collective-permute-done.19.refs_2_, ...), custom_call_target="tpu_custom_call", output_to_operand_aliasing={{}: (5, {})} | custom-call | flops 2000000000 | bytes 1835008 | tf_op jit(solution)/shard_map/place/pallas_call | solution.py:291
  178.8 1.6 collective-permute-start.26
  180.5 2.8 %collective-permute-start.30 = (bf16[64,1792]{1,0:T(8,128)(2,1)S(1)}, bf16[64,1792]{1,0:T(8,128)(2,1)S(1)}, u32[]{:S(2)}, u32[]{:S(2)}) collective-permute-start(bf16[64,1792]{1,0:T(8,128)(2,1)S(1)} %slice.19), channel_id=1, source_target_pairs={{0,192},{64,0},{128,64},{192,128},{1,193},{65,1},{129,65},{193,129... | collective-permute-start | bytes 688136 | tf_op jit(solution)/shard_map/ppermute | solution.py:27
  183.3 1.5 place.9.refs_4_
  184.8 1.8 place.10.refs_4_
  186.6 1.8 collective-permute-done.29.refs_0_
  188.4 1.4 collective-permute-start.31
  191.2 1.5 place.11
  (100 shorter events, 28.3 us)
Async XLA Ops:
  2.8 30.5 %copy-start.19 = (f32[2,16,1792]{2,1,0:T(8,128)S(1)}, f32[2,16,1792]{2,1,0:T(8,128)}, u32[]{:S(2)}) copy-start(f32[2,16,1792]{2,1,0:T(8,128)} %one_ref.1) | copy-start | bytes 688132
  2.8 30.5 %copy-start.20 = (f32[2,16,1792]{2,1,0:T(8,128)S(1)}, f32[2,16,1792]{2,1,0:T(8,128)}, u32[]{:S(2)}) copy-start(f32[2,16,1792]{2,1,0:T(8,128)} %two_ref.1) | copy-start | bytes 688132
  4.8 62.6 %copy-start.17 = (bf16[2,128,1792]{2,1,0:T(8,128)(2,1)S(1)}, bf16[2,128,1792]{2,1,0:T(8,128)(2,1)}, u32[]{:S(2)}) copy-start(bf16[2,128,1792]{2,1,0:T(8,128)(2,1)} %v_ref.3) | copy-start | bytes 2752516
  4.8 41.2 %all-to-all-start = ((bf16[8,2,288,128]{3,2,1,0:T(8,128)(2,1)}), bf16[8,2,288,128]{3,2,1,0:T(8,128)(2,1)S(1)}, u32[]{:S(2)}, u32[]{:S(2)}) async-start(bf16[8,2,288,128]{3,2,1,0:T(8,128)(2,1)} %get-tuple-element.23), calls=%async_computation | async-start | bytes 2359296 | tf_op jit(solution)/shard_map/all_to_all | solution.py:31
  13.9 2.5 %collective-permute-start.4 = (f32[8,224]{1,0:T(8,128)S(1)}, f32[8,224]{1,0:T(8,128)S(1)}, u32[]{:S(2)}, u32[]{:S(2)}) collective-permute-start(f32[8,224]{1,0:T(8,128)S(1)} %get-tuple-element.25), channel_id=1, source_target_pairs={{0,64},{64,0},{128,192},{192,128},{1,65},{65,1},{129,193},{193,129... | collective-permute-start | bytes 21512 | tf_op jit(solution)/shard_map/ppermute | solution.py:308
  16.4 4.0 %collective-permute-start.5 = (f32[8,224]{1,0:T(8,128)S(1)}, f32[8,224]{1,0:T(8,128)S(1)}, u32[]{:S(2)}, u32[]{:S(2)}) collective-permute-start(f32[8,224]{1,0:T(8,128)S(1)} %add.24), channel_id=1, source_target_pairs={{0,128},{64,192},{128,0},{192,64},{1,129},{65,193},{129,1},{193,65... | collective-permute-start | bytes 21512 | tf_op jit(solution)/shard_map/ppermute | solution.py:308
  20.4 2.8 %collective-permute-start.6 = (f32[8,224]{1,0:T(8,128)S(1)}, f32[8,224]{1,0:T(8,128)S(1)}, u32[]{:S(2)}, u32[]{:S(2)}) collective-permute-start(f32[8,224]{1,0:T(8,128)S(1)} %add.25), channel_id=1, source_target_pairs={{0,8},{8,0},{16,24},{24,16},{1,9},{9,1},{17,25},{25,17},{2,10},{10... | collective-permute-start | bytes 21512 | tf_op jit(solution)/shard_map/ppermute | solution.py:308
  23.2 4.3 %collective-permute-start.7 = (f32[8,224]{1,0:T(8,128)S(1)}, f32[8,224]{1,0:T(8,128)S(1)}, u32[]{:S(2)}, u32[]{:S(2)}) collective-permute-start(f32[8,224]{1,0:T(8,128)S(1)} %add.26), channel_id=1, source_target_pairs={{0,16},{8,24},{16,0},{24,8},{1,17},{9,25},{17,1},{25,9},{2,18},{10... | collective-permute-start | bytes 21512 | tf_op jit(solution)/shard_map/ppermute | solution.py:308
  27.5 5.8 %collective-permute-start.8 = (f32[8,224]{1,0:T(8,128)S(1)}, f32[8,224]{1,0:T(8,128)S(1)}, u32[]{:S(2)}, u32[]{:S(2)}) collective-permute-start(f32[8,224]{1,0:T(8,128)S(1)} %add.27), channel_id=1, source_target_pairs={{0,32},{32,0},{1,33},{33,1},{2,34},{34,2},{3,35},{35,3},{4,36},{36... | collective-permute-start | bytes 21512 | tf_op jit(solution)/shard_map/ppermute | solution.py:308
  45.9 29.8 %copy-start = (bf16[8,2,288,128]{3,2,1,0:T(8,128)(2,1)}, bf16[8,2,288,128]{3,2,1,0:T(8,128)(2,1)S(1)}, u32[]{:S(2)}) copy-start(bf16[8,2,288,128]{3,2,1,0:T(8,128)(2,1)S(1)} %all-to-all-done.g_ref) | copy-start | bytes 3538948
  45.9 23.2 %all-to-all-start.1 = ((f32[8,72,224]{2,1,0:T(8,128)}), f32[8,72,224]{2,1,0:T(8,128)S(1)}, u32[]{:S(2)}, u32[]{:S(2)}) async-start(f32[8,72,224]{2,1,0:T(8,128)} %pack_state.1), calls=%async_computation.1 | async-start | bytes 1179648 | tf_op jit(solution)/shard_map/all_to_all | solution.py:31
  49.6 8.7 %collective-permute-start = (bf16[8,2,64,128]{3,2,1,0:T(8,128)(2,1)S(1)}, bf16[8,2,64,128]{3,2,1,0:T(8,128)(2,1)S(1)}, u32[]{:S(2)}, u32[]{:S(2)}) collective-permute-start(bf16[8,2,64,128]{3,2,1,0:T(8,128)(2,1)S(1)} %get-tuple-element.44), channel_id=1, source_target_pairs={{0,64},{64,128},{128,192},{192,0},{1,65},{65,129},{129,193},{193,1... | collective-permute-start | bytes 786440 | tf_op jit(solution)/shard_map/ppermute | solution.py:27
  50.9 14.0 %collective-permute-start.1 = (bf16[8,2,64,128]{3,2,1,0:T(8,128)(2,1)S(1)}, bf16[8,2,64,128]{3,2,1,0:T(8,128)(2,1)S(1)}, u32[]{:S(2)}, u32[]{:S(2)}) collective-permute-start(bf16[8,2,64,128]{3,2,1,0:T(8,128)(2,1)S(1)} %get-tuple-element.44), channel_id=1, source_target_pairs={{0,128},{64,192},{128,0},{192,64},{1,129},{65,193},{129,1},{193,65... | collective-permute-start | bytes 786440 | tf_op jit(solution)/shard_map/ppermute | solution.py:27
  53.4 11.5 %collective-permute-start.2 = (bf16[8,2,64,128]{3,2,1,0:T(8,128)(2,1)S(1)}, bf16[8,2,64,128]{3,2,1,0:T(8,128)(2,1)S(1)}, u32[]{:S(2)}, u32[]{:S(2)}) collective-permute-start(bf16[8,2,64,128]{3,2,1,0:T(8,128)(2,1)S(1)} %get-tuple-element.44), channel_id=1, source_target_pairs={{0,192},{64,0},{128,64},{192,128},{1,193},{65,1},{129,65},{193,129... | collective-permute-start | bytes 786440 | tf_op jit(solution)/shard_map/ppermute | solution.py:27
  66.0 9.7 %collective-permute-start.3 = (bf16[4,8,2,64,128]{4,3,2,1,0:T(8,128)(2,1)}, bf16[4,8,2,64,128]{4,3,2,1,0:T(8,128)(2,1)}, u32[]{:S(2)}, u32[]{:S(2)}) collective-permute-start(bf16[4,8,2,64,128]{4,3,2,1,0:T(8,128)(2,1)} %pad_maximum_fusion.own_ref), channel_id=1, source_target_pairs={{0,32},{32,0},{1,33},{33,1},{2,34},{34,2},{3,35},{35,3},{4,36},{36... | collective-permute-start | bytes 3145736 | tf_op jit(solution)/shard_map/ppermute | solution.py:27
  69.1 6.6 %copy-start.3 = (f32[8,72,224]{2,1,0:T(8,128)}, f32[8,72,224]{2,1,0:T(8,128)S(1)}, u32[]{:S(2)}) copy-start(f32[8,72,224]{2,1,0:T(8,128)S(1)} %all-to-all-done.1.moments_ref) | copy-start | bytes 1548292
  69.1 35.6 %all-to-all-start.2 = ((bf16[8,2,224,128]{3,2,1,0:T(8,128)(2,1)}), bf16[8,2,224,128]{3,2,1,0:T(8,128)(2,1)S(1)}, u32[]{:S(2)}, u32[]{:S(2)}) async-start(bf16[8,2,224,128]{3,2,1,0:T(8,128)(2,1)} %pack.3), calls=%async_computation.2 | async-start | bytes 1835008 | tf_op jit(solution)/shard_map/all_to_all | solution.py:31
  79.9 8.5 %collective-permute-start.10 = (f32[2,224,128]{2,1,0:T(8,128)S(1)}, f32[2,224,128]{2,1,0:T(8,128)S(1)}, u32[]{:S(2)}, u32[]{:S(2)}) collective-permute-start(f32[2,224,128]{2,1,0:T(8,128)S(1)} %get-tuple-element.30), channel_id=1, source_target_pairs={{0,16},{8,24},{16,0},{24,8},{1,17},{9,25},{17,1},{25,9},{2,18},{10... | collective-permute-start | bytes 688136 | tf_op jit(solution)/shard_map/ppermute | solution.py:27
  83.0 10.8 %collective-permute-start.11 = (f32[2,224,128]{2,1,0:T(8,128)S(1)}, f32[2,224,128]{2,1,0:T(8,128)S(1)}, u32[]{:S(2)}, u32[]{:S(2)}) collective-permute-start(f32[2,224,128]{2,1,0:T(8,128)S(1)} %get-tuple-element.31), channel_id=1, source_target_pairs={{0,24},{8,0},{16,8},{24,16},{1,25},{9,1},{17,9},{25,17},{2,26},{10... | collective-permute-start | bytes 688136 | tf_op jit(solution)/shard_map/ppermute | solution.py:27
  83.7 10.1 %collective-permute-start.9 = (f32[2,224,128]{2,1,0:T(8,128)S(1)}, f32[2,224,128]{2,1,0:T(8,128)S(1)}, u32[]{:S(2)}, u32[]{:S(2)}) collective-permute-start(f32[2,224,128]{2,1,0:T(8,128)S(1)} %get-tuple-element.29), channel_id=1, source_target_pairs={{0,8},{8,16},{16,24},{24,0},{1,9},{9,17},{17,25},{25,1},{2,10},{10... | collective-permute-start | bytes 688136 | tf_op jit(solution)/shard_map/ppermute | solution.py:27
  95.3 9.4 %copy-start.5 = (f32[8,64,224]{2,1,0:T(8,128)}, f32[8,64,224]{2,1,0:T(8,128)S(1)}, u32[]{:S(2)}) copy-start(f32[8,64,224]{2,1,0:T(8,128)S(1)} %get-tuple-element.40) | copy-start | bytes 1376260
  95.3 32.6 %copy-start.8 = (bf16[2,224,128]{2,1,0:T(8,128)(2,1)}, bf16[2,224,128]{2,1,0:T(8,128)(2,1)S(1)}, u32[]{:S(2)}) copy-start(bf16[2,224,128]{2,1,0:T(8,128)(2,1)S(1)} %get-tuple-element.32.u0) | copy-start | bytes 344068
  95.3 5.5 %collective-permute-start.12 = (bf16[2,224,128]{2,1,0:T(8,128)(2,1)S(1)}, bf16[2,224,128]{2,1,0:T(8,128)(2,1)S(1)}, u32[]{:S(2)}, u32[]{:S(2)}) collective-permute-start(bf16[2,224,128]{2,1,0:T(8,128)(2,1)S(1)} %get-tuple-element.32.u0), channel_id=1, source_target_pairs={{0,8},{8,16},{16,24},{24,0},{1,9},{9,17},{17,25},{25,1},{2,10},{10... | collective-permute-start | bytes 344072 | tf_op jit(solution)/shard_map/ppermute | solution.py:27
  96.9 7.8 %collective-permute-start.13 = (bf16[2,224,128]{2,1,0:T(8,128)(2,1)S(1)}, bf16[2,224,128]{2,1,0:T(8,128)(2,1)S(1)}, u32[]{:S(2)}, u32[]{:S(2)}) collective-permute-start(bf16[2,224,128]{2,1,0:T(8,128)(2,1)S(1)} %get-tuple-element.32.u0), channel_id=1, source_target_pairs={{0,16},{8,24},{16,0},{24,8},{1,17},{9,25},{17,1},{25,9},{2,18},{10... | collective-permute-start | bytes 344072 | tf_op jit(solution)/shard_map/ppermute | solution.py:27
  99.5 5.2 %collective-permute-start.14 = (bf16[2,224,128]{2,1,0:T(8,128)(2,1)S(1)}, bf16[2,224,128]{2,1,0:T(8,128)(2,1)S(1)}, u32[]{:S(2)}, u32[]{:S(2)}) collective-permute-start(bf16[2,224,128]{2,1,0:T(8,128)(2,1)S(1)} %get-tuple-element.32.u0), channel_id=1, source_target_pairs={{0,24},{8,0},{16,8},{24,16},{1,25},{9,1},{17,9},{25,17},{2,26},{10... | collective-permute-start | bytes 344072 | tf_op jit(solution)/shard_map/ppermute | solution.py:27
  100.8 27.1 %copy-start.10 = (bf16[2,224,128]{2,1,0:T(8,128)(2,1)}, bf16[2,224,128]{2,1,0:T(8,128)(2,1)S(1)}, u32[]{:S(2)}) copy-start(bf16[2,224,128]{2,1,0:T(8,128)(2,1)S(1)} %collective-permute-done.12.u1) | copy-start | bytes 344068
  104.7 23.2 %copy-start.12 = (bf16[2,224,128]{2,1,0:T(8,128)(2,1)}, bf16[2,224,128]{2,1,0:T(8,128)(2,1)S(1)}, u32[]{:S(2)}) copy-start(bf16[2,224,128]{2,1,0:T(8,128)(2,1)S(1)} %collective-permute-done.13.u2) | copy-start | bytes 344068
  104.7 23.2 %copy-start.14 = (bf16[2,224,128]{2,1,0:T(8,128)(2,1)}, bf16[2,224,128]{2,1,0:T(8,128)(2,1)S(1)}, u32[]{:S(2)}) copy-start(bf16[2,224,128]{2,1,0:T(8,128)(2,1)S(1)} %collective-permute-done.14.u3) | copy-start | bytes 344068
  129.1 16.5 %collective-permute-start.15 = (bf16[128,1792]{1,0:T(8,128)(2,1)S(1)}, bf16[128,1792]{1,0:T(8,128)(2,1)}, u32[]{:S(2)}, u32[]{:S(2)}) collective-permute-start(bf16[128,1792]{1,0:T(8,128)(2,1)S(1)} %bitcast.13), channel_id=1, source_target_pairs={{0,64},{64,128},{128,192},{192,0},{1,65},{65,129},{129,193},{193,1... | collective-permute-start | bytes 1376264 | tf_op jit(solution)/shard_map/ppermute | solution.py:27
  137.1 21.6 %all-to-all-start.4 = ((bf16[8,224,128]{2,1,0:T(8,128)(2,1)}), bf16[8,224,128]{2,1,0:T(8,128)(2,1)S(1)}, u32[]{:S(2)}, u32[]{:S(2)}) async-start(bf16[8,224,128]{2,1,0:T(8,128)(2,1)} %copy-done.2), calls=%async_computation.4 | async-start | bytes 917504 | tf_op jit(solution)/shard_map/all_to_all | solution.py:31
  140.6 9.1 %collective-permute-start.17 = (bf16[128,1792]{1,0:T(8,128)(2,1)S(1)}, bf16[128,1792]{1,0:T(8,128)(2,1)S(1)}, u32[]{:S(2)}, u32[]{:S(2)}) collective-permute-start(bf16[128,1792]{1,0:T(8,128)(2,1)S(1)} %bitcast.14), channel_id=1, source_target_pairs={{0,192},{64,0},{128,64},{192,128},{1,193},{65,1},{129,65},{193,129... | collective-permute-start | bytes 1376264 | tf_op jit(solution)/shard_map/ppermute | solution.py:27
  142.2 23.2 %collective-permute-start.23 = (bf16[128,1792]{1,0:T(8,128)(2,1)S(1)}, bf16[128,1792]{1,0:T(8,128)(2,1)S(1)}, u32[]{:S(2)}, u32[]{:S(2)}) collective-permute-start(bf16[128,1792]{1,0:T(8,128)(2,1)S(1)} %bitcast.15), channel_id=1, source_target_pairs={{0,32},{32,0},{1,33},{33,1},{2,34},{34,2},{3,35},{35,3},{4,36},{36... | collective-permute-start | bytes 1376264 | tf_op jit(solution)/shard_map/ppermute | solution.py:27
  145.6 24.6 %collective-permute-start.21 = (bf16[128,1792]{1,0:T(8,128)(2,1)}, bf16[128,1792]{1,0:T(8,128)(2,1)S(1)}, u32[]{:S(2)}, u32[]{:S(2)}) collective-permute-start(bf16[128,1792]{1,0:T(8,128)(2,1)} %collective-permute-done.15.refs_0_), channel_id=1, source_target_pairs={{0,32},{32,0},{1,33},{33,1},{2,34},{34,2},{3,35},{35,3},{4,36},{36... | collective-permute-start | bytes 1376264 | tf_op jit(solution)/shard_map/ppermute | solution.py:27
  149.7 23.1 %collective-permute-start.22 = (bf16[128,1792]{1,0:T(8,128)(2,1)S(1)}, bf16[128,1792]{1,0:T(8,128)(2,1)}, u32[]{:S(2)}, u32[]{:S(2)}) collective-permute-start(bf16[128,1792]{1,0:T(8,128)(2,1)S(1)} %collective-permute-done.17.refs_1_), channel_id=1, source_target_pairs={{0,32},{32,0},{1,33},{33,1},{2,34},{34,2},{3,35},{35,3},{4,36},{36... | collective-permute-start | bytes 1376264 | tf_op jit(solution)/shard_map/ppermute | solution.py:27
  155.2 11.0 %collective-permute-start.16 = (bf16[64,1792]{1,0:T(8,128)(2,1)}, bf16[64,1792]{1,0:T(8,128)(2,1)}, u32[]{:S(2)}, u32[]{:S(2)}) collective-permute-start(bf16[64,1792]{1,0:T(8,128)(2,1)} %slice.21), channel_id=1, source_target_pairs={{0,64},{64,128},{128,192},{192,0},{1,65},{65,129},{129,193},{193,1... | collective-permute-start | bytes 688136 | tf_op jit(solution)/shard_map/ppermute | solution.py:27
  156.9 12.0 %collective-permute-start.18 = (bf16[64,1792]{1,0:T(8,128)(2,1)}, bf16[64,1792]{1,0:T(8,128)(2,1)}, u32[]{:S(2)}, u32[]{:S(2)}) collective-permute-start(bf16[64,1792]{1,0:T(8,128)(2,1)} %slice.22), channel_id=1, source_target_pairs={{0,192},{64,0},{128,64},{192,128},{1,193},{65,1},{129,65},{193,129... | collective-permute-start | bytes 688136 | tf_op jit(solution)/shard_map/ppermute | solution.py:27
  158.9 30.8 %all-to-all-start.5 = ((f32[8,64,224]{2,1,0:T(8,128)}), f32[8,64,224]{2,1,0:T(8,128)S(1)}, u32[]{:S(2)}, u32[]{:S(2)}) async-start(f32[8,64,224]{2,1,0:T(8,128)} %copy-done.5), calls=%async_computation.5 | async-start | bytes 1048576 | tf_op jit(solution)/shard_map/all_to_all | solution.py:31
  166.2 12.6 %collective-permute-start.24 = (bf16[128,1792]{1,0:T(8,128)(2,1)S(1)}, bf16[128,1792]{1,0:T(8,128)(2,1)S(1)}, u32[]{:S(2)}, u32[]{:S(2)}) collective-permute-start(bf16[128,1792]{1,0:T(8,128)(2,1)S(1)} %bitcast.17), channel_id=1, source_target_pairs={{0,64},{64,128},{128,192},{192,0},{1,65},{65,129},{129,193},{193,1... | collective-permute-start | bytes 1376264 | tf_op jit(solution)/shard_map/ppermute | solution.py:27
  166.2 12.6 %collective-permute-start.25 = (bf16[128,1792]{1,0:T(8,128)(2,1)S(1)}, bf16[128,1792]{1,0:T(8,128)(2,1)S(1)}, u32[]{:S(2)}, u32[]{:S(2)}) collective-permute-start(bf16[128,1792]{1,0:T(8,128)(2,1)S(1)} %bitcast.18), channel_id=1, source_target_pairs={{0,192},{64,0},{128,64},{192,128},{1,193},{65,1},{129,65},{193,129... | collective-permute-start | bytes 1376264 | tf_op jit(solution)/shard_map/ppermute | solution.py:27
  168.9 6.8 %collective-permute-start.19 = (bf16[64,1792]{1,0:T(8,128)(2,1)}, bf16[64,1792]{1,0:T(8,128)(2,1)S(1)}, u32[]{:S(2)}, u32[]{:S(2)}) collective-permute-start(bf16[64,1792]{1,0:T(8,128)(2,1)} %collective-permute-done.16.refs_0_), channel_id=1, source_target_pairs={{0,32},{32,0},{1,33},{33,1},{2,34},{34,2},{3,35},{35,3},{4,36},{36... | collective-permute-start | bytes 688136 | tf_op jit(solution)/shard_map/ppermute | solution.py:27
  170.2 5.6 %collective-permute-start.20 = (bf16[64,1792]{1,0:T(8,128)(2,1)}, bf16[64,1792]{1,0:T(8,128)(2,1)S(1)}, u32[]{:S(2)}, u32[]{:S(2)}) collective-permute-start(bf16[64,1792]{1,0:T(8,128)(2,1)} %collective-permute-done.18.refs_1_), channel_id=1, source_target_pairs={{0,32},{32,0},{1,33},{33,1},{2,34},{34,2},{3,35},{35,3},{4,36},{36... | collective-permute-start | bytes 688136 | tf_op jit(solution)/shard_map/ppermute | solution.py:27
  172.8 10.5 %collective-permute-start.28 = (bf16[128,1792]{1,0:T(8,128)(2,1)S(1)}, bf16[128,1792]{1,0:T(8,128)(2,1)S(1)}, u32[]{:S(2)}, u32[]{:S(2)}) collective-permute-start(bf16[128,1792]{1,0:T(8,128)(2,1)S(1)} %bitcast.19), channel_id=1, source_target_pairs={{0,32},{32,0},{1,33},{33,1},{2,34},{34,2},{3,35},{35,3},{4,36},{36... | collective-permute-start | bytes 1376264 | tf_op jit(solution)/shard_map/ppermute | solution.py:27
  178.8 6.0 %collective-permute-start.26 = (bf16[128,1792]{1,0:T(8,128)(2,1)S(1)}, bf16[128,1792]{1,0:T(8,128)(2,1)S(1)}, u32[]{:S(2)}, u32[]{:S(2)}) collective-permute-start(bf16[128,1792]{1,0:T(8,128)(2,1)S(1)} %collective-permute-done.24.refs_0_), channel_id=1, source_target_pairs={{0,32},{32,0},{1,33},{33,1},{2,34},{34,2},{3,35},{35,3},{4,36},{36... | collective-permute-start | bytes 1376264 | tf_op jit(solution)/shard_map/ppermute | solution.py:27
  180.4 4.4 %collective-permute-start.27 = (bf16[128,1792]{1,0:T(8,128)(2,1)S(1)}, bf16[128,1792]{1,0:T(8,128)(2,1)S(1)}, u32[]{:S(2)}, u32[]{:S(2)}) collective-permute-start(bf16[128,1792]{1,0:T(8,128)(2,1)S(1)} %collective-permute-done.25.refs_1_), channel_id=1, source_target_pairs={{0,32},{32,0},{1,33},{33,1},{2,34},{34,2},{3,35},{35,3},{4,36},{36... | collective-permute-start | bytes 1376264 | tf_op jit(solution)/shard_map/ppermute | solution.py:27
  180.4 8.0 %collective-permute-start.29 = (bf16[64,1792]{1,0:T(8,128)(2,1)S(1)}, bf16[64,1792]{1,0:T(8,128)(2,1)S(1)}, u32[]{:S(2)}, u32[]{:S(2)}) collective-permute-start(bf16[64,1792]{1,0:T(8,128)(2,1)S(1)} %slice.18), channel_id=1, source_target_pairs={{0,64},{64,128},{128,192},{192,0},{1,65},{65,129},{129,193},{193,1... | collective-permute-start | bytes 688136 | tf_op jit(solution)/shard_map/ppermute | solution.py:27
  180.5 7.9 %collective-permute-start.30 = (bf16[64,1792]{1,0:T(8,128)(2,1)S(1)}, bf16[64,1792]{1,0:T(8,128)(2,1)S(1)}, u32[]{:S(2)}, u32[]{:S(2)}) collective-permute-start(bf16[64,1792]{1,0:T(8,128)(2,1)S(1)} %slice.19), channel_id=1, source_target_pairs={{0,192},{64,0},{128,64},{192,128},{1,193},{65,1},{129,65},{193,129... | collective-permute-start | bytes 688136 | tf_op jit(solution)/shard_map/ppermute | solution.py:27
  188.4 2.5 %collective-permute-start.31 = (bf16[64,1792]{1,0:T(8,128)(2,1)S(1)}, bf16[64,1792]{1,0:T(8,128)(2,1)S(1)}, u32[]{:S(2)}, u32[]{:S(2)}) collective-permute-start(bf16[64,1792]{1,0:T(8,128)(2,1)S(1)} %collective-permute-done.29.refs_0_), channel_id=1, source_target_pairs={{0,32},{32,0},{1,33},{33,1},{2,34},{34,2},{3,35},{35,3},{4,36},{36... | collective-permute-start | bytes 688136 | tf_op jit(solution)/shard_map/ppermute | solution.py:27
  189.7 1.5 collective-permute-start.32
  (11 other events, 10.6 us)

commit v3 on v2

--- a/solution.py
+++ b/solution.py
@@ -39,77 +39,92 @@
     return lax.optimization_barrier((first, second))[1]
 
 
-def pack_kernel(extra, at_ref, v_ref, *refs):
-    out_ref = refs[-2] if extra else refs[-1]
-    nz = out_ref.shape[0]
-    cols = v_ref.shape[2] // nz
-    total = None
+def pack_kernel(v_ref, out_ref):
+    nz, _, cols, _ = out_ref.shape
     for m in range(MATS):
         turned = jnp.transpose(v_ref[m])
         for z in range(nz):
-            out_ref[z, m, :cols] = turned[z * cols : (z + 1) * cols]
-        if extra:
-            wide = v_ref[m].astype(F32)
-            squares = jnp.sum(wide * wide, axis=0, keepdims=True)
-            total = squares if total is None else total + squares
-    if extra:
-        basis_ref, tile_ref = refs[0], refs[-1]
-        tile_ref[...] = jnp.broadcast_to(jnp.sum(total, axis=1, keepdims=True), tile_ref.shape)
-        part = basis_ref.shape[1] // 8
-        start = pl.multiple_of((at_ref[0] * 2 + at_ref[1]) * part, part)
-        width = out_ref.shape[3]
-        for m in range(MATS):
-            piece = basis_ref[m, pl.ds(start, part)]
-            for k in range(piece.shape[1] // width):
-                low = cols + k * part
-                for z in range(nz):
-                    out_ref[z, m, low : low + part] = piece[:, k * width : (k + 1) * width]
-
-
-def pack(at, v, nz, basis=None):
+            out_ref[z, m] = turned[z * cols : (z + 1) * cols]
+
+
+def pack(v, nz):
     mats, rows, cols = v.shape
-    cols //= nz
-    extra = basis is not None
-    more = basis.shape[1] // 8 * (basis.shape[2] // rows) if extra else 0
-    shapes = [jax.ShapeDtypeStruct((nz, mats, cols + more, rows), BF16)]
-    if extra:
-        shapes.append(jax.ShapeDtypeStruct((8, cols), F32))
-    given = (basis,) if extra else ()
-    out = pl.pallas_call(
-        functools.partial(pack_kernel, extra),
-        out_shape=shapes,
-        in_specs=[SMEM] + [VMEM] * (1 + len(given)),
-        out_specs=[VMEM] * len(shapes),
+    return pl.pallas_call(
+        pack_kernel,
+        out_shape=jax.ShapeDtypeStruct((nz, mats, cols // nz, rows), BF16),
+        in_specs=[VMEM],
+        out_specs=VMEM,
         compiler_params=PARAMS,
         cost_estimate=cost(2e9, 2 * 2**20),
         name="pack",
-    )(at, v, *given)
-    return out if extra else out[0]
-
-
-def pack_state_kernel(one_ref, two_ref, tile_ref, out_ref):
-    nz, _, cols = out_ref.shape
+    )(v)
+
+
+def pieces_kernel(at_ref, v_ref, basis_ref, out_ref):
+    nz, size, width = out_ref.shape
+    part = basis_ref.shape[1] // 8
+    start = pl.multiple_of((at_ref[0] * 2 + at_ref[1]) * part, part)
+    total = None
+    for m in range(MATS):
+        wide = v_ref[m].astype(F32)
+        squares = jnp.sum(wide * wide, axis=0, keepdims=True)
+        total = squares if total is None else total + squares
+        piece = basis_ref[m, pl.ds(start, part)]
+        count = piece.shape[1] // width
+        for k in range(count):
+            low = (m * count + k) * part
+            for z in range(nz):
+                out_ref[z, low : low + part] = piece[:, k * width : (k + 1) * width]
+    total = jnp.sum(total, axis=1, keepdims=True)
+    high = total.astype(BF16).astype(F32)
+    middle = (total - high).astype(BF16).astype(F32)
+    low = total - high - middle
+    row = lax.broadcasted_iota(jnp.int32, (part, width), 0)
+    tile = jnp.where(row == 0, high, jnp.where(row == 1, middle, jnp.where(row == 2, low, 0.0)))
+    for z in range(nz):
+        out_ref[z, size - part :] = tile.astype(BF16)
+
+
+def pieces(at, v, basis, nz):
+    mats, rows, rank = basis.shape
+    part, width = rows // 8, 128
+    return pl.pallas_call(
+        pieces_kernel,
+        out_shape=jax.ShapeDtypeStruct((nz, mats * part * rank // width + part, width), BF16),
+        in_specs=[SMEM, VMEM, VMEM],
+        out_specs=VMEM,
+        compiler_params=PARAMS,
+        cost_estimate=cost(2e9, 2**20),
+        name="pieces",
+    )(at, v, basis)
+
+
+def pack_state_kernel(at_ref, one_ref, two_ref, *refs):
+    outs, held_ref = refs[:-1], refs[-1]
+    nz, _, cols = held_ref.shape
     ranks = one_ref.shape[1]
     for k, ref in enumerate((one_ref, two_ref)):
         for m in range(MATS):
             low = (k * MATS + m) * ranks
             for z in range(nz):
-                out_ref[z, low : low + ranks] = ref[m, :, z * cols : (z + 1) * cols]
-    for z in range(nz):
-        out_ref[z, 2 * MATS * ranks :] = tile_ref[...]
-
-
-def pack_state(one, two, tile, nz):
+                held_ref[z, low : low + ranks] = ref[m, :, z * cols : (z + 1) * cols]
+    for d in range(nz):
+        outs[d][...] = held_ref[lax.rem(at_ref[3] + d, nz)]
+
+
+def pack_state(at, one, two, nz):
     mats, ranks, cols = one.shape
+    size = (2 * mats * ranks, cols // nz)
     return pl.pallas_call(
         pack_state_kernel,
-        out_shape=jax.ShapeDtypeStruct((nz, 2 * mats * ranks + tile.shape[0], cols // nz), F32),
-        in_specs=[VMEM] * 3,
-        out_specs=VMEM,
+        out_shape=[jax.ShapeDtypeStruct(size, F32)] * nz,
+        in_specs=[SMEM, VMEM, VMEM],
+        out_specs=[VMEM] * nz,
+        scratch_shapes=[pltpu.VMEM((nz, *size), F32)],
         compiler_params=PARAMS,
         cost_estimate=cost(2e9, 2**20),
         name="pack_state",
-    )(one, two, tile)
+    )(at, one, two)
 
 
 def unpack_state_kernel(in_ref, one_ref, two_ref):
@@ -138,46 +153,56 @@
 def project_kernel(at_ref, g_ref, own_ref, peer_ref, basis_ref, *refs):
     outs, total_ref = refs[:-1], refs[-1]
     x, core, y = (at_ref[i] for i in range(3))
-    nx, nz, _, size, width = own_ref.shape
+    nx, nz, size, width = own_ref.shape
     rank = basis_ref.shape[3]
-    part = size * width // rank
-    cols = total_ref.shape[1]
+    part = basis_ref.shape[2] // (2 * nx)
+    count = rank // width
+    cols = g_ref.shape[2]
     ny = len(outs)
 
     def gather(z, _):
         for m in range(MATS):
             for xa in range(nx):
                 d = lax.rem(x - xa + nx, nx)
-                ours, theirs = own_ref[d, z, m], peer_ref[d, z, m]
-                pair = (jnp.where(core == 0, ours, theirs), jnp.where(core == 0, theirs, ours))
-                for c in range(2):
-                    low = (2 * xa + c) * part
-                    for k in range(rank // width):
-                        basis_ref[m, z, low : low + part, k * width : (k + 1) * width] = pair[c][
-                            k * part : (k + 1) * part
-                        ]
+                for k in range(count):
+                    low = (m * count + k) * part
+                    ours, theirs = own_ref[d, z, low : low + part], peer_ref[d, z, low : low + part]
+                    at = 2 * xa * part
+                    lanes = slice(k * width, (k + 1) * width)
+                    basis_ref[m, z, at : at + part, lanes] = jnp.where(core == 0, ours, theirs)
+                    basis_ref[m, z, at + part : at + 2 * part, lanes] = jnp.where(
+                        core == 0, theirs, ours
+                    )
         return 0
 
     lax.fori_loop(0, nz, gather, 0)
 
     def multiply(m, _):
-        left = jnp.concatenate([g_ref[z, m, :cols] for z in range(nz)], axis=1)
+        left = jnp.concatenate([g_ref[z, m] for z in range(nz)], axis=1)
         right = basis_ref[m].reshape(left.shape[1], -1)
         total_ref[m] = jnp.dot(left, right, preferred_element_type=F32)
         return 0
 
     lax.fori_loop(0, MATS, multiply, 0)
+    squares = jnp.zeros((part, width), F32)
+    for ref in (own_ref, peer_ref):
+        for d in range(nx):
+            for z in range(nz):
+                squares = squares + ref[d, z, size - part :].astype(F32)
+    squares = jnp.sum(squares, axis=0, keepdims=True)
     for d in range(ny):
         start = pl.multiple_of(lax.rem(y + d, ny) * width, width)
-        outs[d][...] = total_ref[:, :, pl.ds(start, width)]
-
-
-def project(at, g, own, peer, cols, rank, parts):
-    nz, mats, _, rows = g.shape
+        outs[d][:, :cols] = total_ref[:, :, pl.ds(start, width)]
+        for m in range(MATS):
+            outs[d][m, cols:] = jnp.broadcast_to(squares, (8, width))
+
+
+def project(at, g, own, peer, rank, parts):
+    nz, mats, cols, rows = g.shape
     basis, *out = pl.pallas_call(
         project_kernel,
         out_shape=[jax.ShapeDtypeStruct((mats, nz, rows, rank), BF16)]
-        + [jax.ShapeDtypeStruct((mats, cols, rank // parts), F32)] * parts,
+        + [jax.ShapeDtypeStruct((mats, cols + 8, rank // parts), F32)] * parts,
         in_specs=[SMEM] + [VMEM] * 3,
         out_specs=[VMEM] * (1 + parts),
         scratch_shapes=[pltpu.VMEM((mats, cols, rank), F32)],
@@ -188,23 +213,24 @@
     return basis, out
 
 
-def moments_kernel(moments_ref, sum_ref, new_ref, update_ref):
-    nz, _, cols = moments_ref.shape
-    kinds = 2 * MATS
-    ranks = new_ref.shape[1] // kinds
+def moments_kernel(at_ref, sum_ref, *refs):
+    held, new_ref, update_ref, held_ref = refs[:-3], refs[-3], refs[-2], refs[-1]
+    nz, kinds, cols = held_ref.shape
+    ranks = kinds // (2 * MATS)
+    for d in range(nz):
+        held_ref[lax.rem(at_ref[3] - d + nz, nz)] = held[d][...]
     limit = 1.0 * math.sqrt(MATS * D * FF)
-    total = jnp.sum(moments_ref[:, kinds * ranks :], axis=0)
-    scale = limit / jnp.maximum(jnp.sqrt(total[0:1, 0:1]), limit)
+    scale = limit / jnp.maximum(jnp.sqrt(sum_ref[0, cols : cols + 1, 0:1]), limit)
     first_bias_correction = 1.0 - 0.9**STEP
     second_fix = 1.0 - 0.999**STEP
     spare = 256 - cols
     for m in range(MATS):
         one, two = (slice(k * ranks, (k + 1) * ranks) for k in (m, MATS + m))
-        summed = sum_ref[m]
+        summed = sum_ref[m, :cols]
         padded = jnp.concatenate([summed, jnp.zeros((spare, summed.shape[1]), F32)], axis=0)
         scaled = scale * jnp.transpose(padded)[:, :cols]
-        first = 0.9 * moments_ref[:, one].reshape(nz * ranks, cols) + 0.1 * scaled
-        second = 0.999 * moments_ref[:, two].reshape(nz * ranks, cols) + 0.001 * scaled * scaled
+        first = 0.9 * held_ref[:, one].reshape(nz * ranks, cols) + 0.1 * scaled
+        second = 0.999 * held_ref[:, two].reshape(nz * ranks, cols) + 0.001 * scaled * scaled
         new_ref[:, one] = first.reshape(nz, ranks, cols)
         new_ref[:, two] = second.reshape(nz, ranks, cols)
         update = first / first_bias_correction / (jnp.sqrt(second / second_fix) + 1e-08)
@@ -212,20 +238,23 @@
         update_ref[m] = jnp.transpose(wide)[:cols].astype(BF16)
 
 
-def moments(held, ranks, summed):
-    nz, _, cols = held.shape
+def moments(at, summed, held):
+    nz = len(held)
+    kinds, cols = held[0].shape
+    ranks = kinds // (2 * MATS)
     return pl.pallas_call(
         moments_kernel,
         out_shape=[
-            jax.ShapeDtypeStruct((nz, 2 * MATS * ranks, cols), F32),
+            jax.ShapeDtypeStruct((nz, kinds, cols), F32),
             jax.ShapeDtypeStruct((MATS, cols, nz * ranks), BF16),
         ],
-        in_specs=[VMEM] * 2,
+        in_specs=[SMEM] + [VMEM] * (1 + nz),
         out_specs=[VMEM] * 2,
+        scratch_shapes=[pltpu.VMEM((nz, kinds, cols), F32)],
         compiler_params=PARAMS,
         cost_estimate=cost(2e9, 2 * 2**20),
         name="moments",
-    )(held, summed)
+    )(at, summed, *held)
 
 
 def back_kernel(m, at_ref, basis_ref, w_ref, u0, u1, u2, u3, out_ref, whole_ref):
@@ -301,41 +330,28 @@
     )(at, *blocks, *given)
 
 
-def sum_over(tile, axis):
-    n = lax.axis_size(axis)
-    step = 1
-    while step < n:
-        tile = tile + lax.ppermute(tile, axis, [(i, i ^ step) for i in range(n)])
-        step *= 2
-    return tile
-
-
 def step(grads, basis, moment1, moment2, weights):
     x, core = lax.axis_index("x"), lax.axis_index("core")
     y, z = lax.axis_index("y"), lax.axis_index("z")
     nx, nc, ny, nz = (lax.axis_size(a) for a in ("x", "core", "y", "z"))
     mats, rows, cols = grads.shape
     rank = basis.shape[2]
-    ranks = rank // (ny * nz)
     at = jnp.stack([x, core, y, z])
 
-    sent, tile = pack(at, grads, nz, basis)
+    held = exchange(pieces(at, grads, basis, nz), "z")
+    sent = pack(grads, nz)
     mine = exchange(sent, "z")
-    for axis in ("x", "y", "core"):
-        tile = sum_over(tile, axis)
-    state = pack_state(moment1, moment2, tile, nz)
-    w = pack(at, weights, nz)
-
-    held = mine[:, :, cols // nz :]
+    w = pack(weights, nz)
+    state = pack_state(at, moment1, moment2, nz)
     own = jnp.stack([held] + [shift(held, "x", k) for k in range(1, nx)])
     peer = shift(own, "core", 1)
-    state = exchange(before(mine, state), "z")
-    w = exchange(before(state, w), "z")
-
-    gathered, parts = project(at, mine, own, peer, cols // nz, rank, ny)
+    state = [state[0]] + [shift(state[k], "z", k) for k in range(1, nz)]
+    w = exchange(before(mine, w), "z")
+
+    gathered, parts = project(at, mine, own, peer, rank, ny)
     parts = [parts[0]] + [shift(parts[k], "y", k) for k in range(1, ny)]
     summed = (parts[0] + parts[1]) + (parts[2] + parts[3])
-    news, update = moments(state, ranks, summed)
+    news, update = moments(at, summed, state)
     updates = [update] + [shift(update, "y", k) for k in range(1, ny)]
     fresh = [exchange(back(m, at, gathered, w, updates), "z") for m in range(mats)]
     news = unpack_state(exchange(before(fresh[-1], news), "z"))

time: 194 us -> 194 us (level)
  blocking collectives: 20.8 us -> 16.7 us
  waiting for transfers between devices: 49.2 us -> 51.5 us
    ppermute x28 -> x35, starting transfers between devices: 39.2 us -> 56.3 us  [shift(): return lax.ppermute(v, axis, [(i, (i + k) % n) for i in range(n)])]
    ppermute x5 -> x0, starting transfers between devices: 13.1 us -> none  [sum_over(): tile = tile + lax.ppermute(tile, axis, [(i, i ^ step) for i in range(n)])]
    ppermute x5 -> x0, waiting for transfers between devices: 6.27 us -> none  [sum_over(): tile = tile + lax.ppermute(tile, axis, [(i, i ^ step) for i in range(n)])]
    ppermute x28 -> x35, waiting for transfers between devices: 31.4 us -> 36.3 us  [shift(): return lax.ppermute(v, axis, [(i, (i + k) % n) for i in range(n)])]
    all_to_all x1, blocking collectives: 20.8 us -> 16.7 us  [exchange(): return lax.all_to_all(v, axis, split_axis=0, concat_axis=0, tiled=True)]
    all_to_all x5, waiting for transfers between devices: 11.6 us -> 15.2 us  [exchange(): return lax.all_to_all(v, axis, split_axis=0, concat_axis=0, tiled=True)]
    all_to_all x5, starting transfers between devices: 29.2 us -> 26.4 us  [exchange(): return lax.all_to_all(v, axis, split_axis=0, concat_axis=0, tiled=True)]
    unnamed x42 -> x48, local copies, waits for them, and re-layouts: 10.6 us -> 12.5 us
  transfers between devices with their start and end apart: 38 -> 40, of which waited for: 18 -> 15; matrix products, arithmetic and copies ran while one was open for 2% -> 1% of each run, Pallas kernels for 10% -> 10%
where the time goes in v3:
time: 194 us; the launch traced here: 193 us
  starting transfers between devices  82.6 us (43%)
  waiting for transfers between devices  51.5 us (27%)
  Pallas kernels  24.4 us (13%)
  blocking collectives  16.7 us (9%)
  local copies, waits for them, and re-layouts  16.3 us (8%)
    ppermute x35, starting transfers between devices, shift(): return lax.ppermute(v, axis, [(i, (i + k) % n) for i in range(n)])  56.3 us
    ppermute x35, waiting for transfers between devices, shift(): return lax.ppermute(v, axis, [(i, (i + k) % n) for i in range(n)])  36.3 us
    all_to_all x5, starting transfers between devices, exchange(): return lax.all_to_all(v, axis, split_axis=0, concat_axis=0, tiled=True)  26.4 us
    all_to_all x1, blocking collectives, exchange(): return lax.all_to_all(v, axis, split_axis=0, concat_axis=0, tiled=True)  16.7 us
    all_to_all x5, waiting for transfers between devices, exchange(): return lax.all_to_all(v, axis, split_axis=0, concat_axis=0, tiled=True)  15.2 us
    unnamed x48, local copies, waits for them, and re-layouts  12.5 us
    pallas_call x6, Pallas kernels, place(): pl.pallas_call(functools.partial(place_kernel, m, spots), out_shape=jax.S...  10.7 us
    pallas_call x2, Pallas kernels, back(): pl.pallas_call(functools.partial(back_kernel, m), out_shape=jax.ShapeDtyp...  4.76 us
  transfers between devices with their start and end apart: 40, of which 15 were waited for; matrix products, arithmetic and copies ran while one was open for 1% of the time, Pallas kernels for 10%

profile of v3, /device:TPU:1, one launch (start us, length us, event | category | flops | bytes accessed | tf_op | source)
XLA Modules:
  0.0 192.9 jit_solution(5338054994245791724)
XLA Ops:
  2.8 1.4 pieces.1
  4.3 9.0 %all-to-all-start.1 = ((bf16[8,144,128]{2,1,0:T(8,128)(2,1)}), bf16[8,144,128]{2,1,0:T(8,128)(2,1)S(1)}, u32[]{:S(2)}, u32[]{:S(2)}) async-start(bf16[8,144,128]{2,1,0:T(8,128)(2,1)} %pieces.1), calls=%async_computation.1 | async-start | bytes 589824 | tf_op jit(solution)/shard_map/all_to_all | solution.py:31
  14.5 10.0 %all-to-all-done.1 = bf16[8,144,128]{2,1,0:T(8,128)(2,1)S(1)} async-done(((bf16[8,144,128]{2,1,0:T(8,128)(2,1)}), bf16[8,144,128]{2,1,0:T(8,128)(2,1)S(1)}, u32[]{:S(2)}, u32[]{:S(2)}) %all-to-all-start.1) | async-done | bytes 294944 | tf_op jit(solution)/shard_map/all_to_all | solution.py:31
  24.5 3.6 %all-to-all-start = ((bf16[8,2,224,128]{3,2,1,0:T(8,128)(2,1)}), bf16[8,2,224,128]{3,2,1,0:T(8,128)(2,1)S(1)}, u32[]{:S(2)}, u32[]{:S(2)}) async-start(bf16[8,2,224,128]{3,2,1,0:T(8,128)(2,1)} %pack.2), calls=%async_computation | async-start | bytes 1835008 | tf_op jit(solution)/shard_map/all_to_all | solution.py:31
  28.1 1.3 collective-permute-start
  29.4 2.5 %collective-permute-start.1 = (bf16[8,144,128]{2,1,0:T(8,128)(2,1)S(1)}, bf16[8,144,128]{2,1,0:T(8,128)(2,1)S(1)}, u32[]{:S(2)}, u32[]{:S(2)}) collective-permute-start(bf16[8,144,128]{2,1,0:T(8,128)(2,1)S(1)} %all-to-all-done.1), channel_id=1, source_target_pairs={{0,128},{64,192},{128,0},{192,64},{1,129},{65,193},{129,1},{193,65... | collective-permute-start | bytes 884744 | tf_op jit(solution)/shard_map/ppermute | solution.py:27
  33.0 2.7 %collective-permute-done = bf16[8,144,128]{2,1,0:T(8,128)(2,1)S(1)} collective-permute-done((bf16[8,144,128]{2,1,0:T(8,128)(2,1)S(1)}, bf16[8,144,128]{2,1,0:T(8,128)(2,1)S(1)}, u32[]{:S(2)}, u32[]{:S(2)}) %collective-permute-start) | collective-permute-done | bytes 294944 | tf_op jit(solution)/shard_map/ppermute | solution.py:27
  35.7 7.3 %collective-permute-done.1 = bf16[8,144,128]{2,1,0:T(8,128)(2,1)S(1)} collective-permute-done((bf16[8,144,128]{2,1,0:T(8,128)(2,1)S(1)}, bf16[8,144,128]{2,1,0:T(8,128)(2,1)S(1)}, u32[]{:S(2)}, u32[]{:S(2)}) %collective-permute-start.1) | collective-permute-done | bytes 294944 | tf_op jit(solution)/shard_map/ppermute | solution.py:27
  43.5 2.8 %collective-permute-start.3 = (bf16[4,8,144,128]{3,2,1,0:T(8,128)(2,1)S(1)}, bf16[4,8,144,128]{3,2,1,0:T(8,128)(2,1)}, u32[]{:S(2)}, u32[]{:S(2)}) collective-permute-start(bf16[4,8,144,128]{3,2,1,0:T(8,128)(2,1)S(1)} %pad_maximum_fusion.own_ref), channel_id=1, source_target_pairs={{0,32},{32,0},{1,33},{33,1},{2,34},{34,2},{3,35},{35,3},{4,36},{36... | collective-permute-start | bytes 3538952 | tf_op jit(solution)/shard_map/ppermute | solution.py:27
  47.6 5.2 %all-to-all-done.g_ref = bf16[8,2,224,128]{3,2,1,0:T(8,128)(2,1)S(1)} async-done(((bf16[8,2,224,128]{3,2,1,0:T(8,128)(2,1)}), bf16[8,2,224,128]{3,2,1,0:T(8,128)(2,1)S(1)}, u32[]{:S(2)}, u32[]{:S(2)}) %all-to-all-start) | async-done | bytes 917536 | tf_op jit(solution)/shard_map/all_to_all | solution.py:31
  52.8 3.6 %all-to-all-start.2 = ((bf16[8,2,224,128]{3,2,1,0:T(8,128)(2,1)}), bf16[8,2,224,128]{3,2,1,0:T(8,128)(2,1)S(1)}, u32[]{:S(2)}, u32[]{:S(2)}) async-start(bf16[8,2,224,128]{3,2,1,0:T(8,128)(2,1)} %copy-done.5), calls=%async_computation.2 | async-start | bytes 1835008 | tf_op jit(solution)/shard_map/all_to_all | solution.py:31
  56.4 1.3 copy-done.1
  58.8 2.8 %project.1 = (bf16[2,8,128,512]{3,2,1,0:T(8,128)(2,1)S(1)}, f32[2,232,128]{2,1,0:T(8,128)S(1)}, f32[2,232,128]{2,1,0:T(8,128)S(1)}, f32[2,232,128]{2,1,0:T(8,128)S(1)}, f32[2,232,128]{2,1,0:T(8,128)S(1)}) custom-call(s32[4]{0:T(128)S(1)} %pad_add_fusion.at_ref, bf16[8,2,224,128]{3,2,1,0:T(8,128)(2,1)S(1)} %copy-done.3, ...), custom_call_target="tpu_custom_call" | custom-call | flops 469762048 | bytes 4194304 | tf_op jit(solution)/shard_map/project/pallas_call | solution.py:202
  61.6 1.4 collective-permute-start.4
  62.9 2.6 %collective-permute-start.5 = (f32[2,232,128]{2,1,0:T(8,128)S(1)}, f32[2,232,128]{2,1,0:T(8,128)S(1)}, u32[]{:S(2)}, u32[]{:S(2)}) collective-permute-start(f32[2,232,128]{2,1,0:T(8,128)S(1)} %get-tuple-element.32), channel_id=1, source_target_pairs={{0,16},{8,24},{16,0},{24,8},{1,17},{9,25},{17,1},{25,9},{2,18},{10... | collective-permute-start | bytes 712712 | tf_op jit(solution)/shard_map/ppermute | solution.py:27
  67.4 5.4 %collective-permute-start.10 = (f32[64,224]{1,0:T(8,128)S(1)}, f32[64,224]{1,0:T(8,128)S(1)}, u32[]{:S(2)}, u32[]{:S(2)}) collective-permute-start(f32[64,224]{1,0:T(8,128)S(1)} %get-tuple-element.38), channel_id=1, source_target_pairs={{0,4},{1,5},{2,6},{3,7},{4,0},{5,1},{6,2},{7,3},{8,12},{9,13},{10,... | collective-permute-start | bytes 172040 | tf_op jit(solution)/shard_map/ppermute | solution.py:27
  73.0 11.2 %collective-permute-done.10.refs_4_ = f32[64,224]{1,0:T(8,128)S(1)} collective-permute-done((f32[64,224]{1,0:T(8,128)S(1)}, f32[64,224]{1,0:T(8,128)S(1)}, u32[]{:S(2)}, u32[]{:S(2)}) %collective-permute-start.10) | collective-permute-done | bytes 57376 | tf_op jit(solution)/shard_map/ppermute | solution.py:27
  84.2 2.5 %collective-permute-start.13 = (f32[64,224]{1,0:T(8,128)S(1)}, f32[64,224]{1,0:T(8,128)S(1)}, u32[]{:S(2)}, u32[]{:S(2)}) collective-permute-start(f32[64,224]{1,0:T(8,128)S(1)} %get-tuple-element.41), channel_id=1, source_target_pairs={{0,7},{1,0},{2,1},{3,2},{4,3},{5,4},{6,5},{7,6},{8,15},{9,8},{10,9... | collective-permute-start | bytes 172040 | tf_op jit(solution)/shard_map/ppermute | solution.py:27
  86.8 2.8 %collective-permute-start.7 = (f32[64,224]{1,0:T(8,128)S(1)}, f32[64,224]{1,0:T(8,128)S(1)}, u32[]{:S(2)}, u32[]{:S(2)}) collective-permute-start(f32[64,224]{1,0:T(8,128)S(1)} %get-tuple-element.35), channel_id=1, source_target_pairs={{0,1},{1,2},{2,3},{3,4},{4,5},{5,6},{6,7},{7,0},{8,9},{9,10},{10,1... | collective-permute-start | bytes 172040 | tf_op jit(solution)/shard_map/ppermute | solution.py:27
  89.6 1.3 collective-permute-start.8
  91.5 3.8 %collective-permute-done.8.refs_2_ = f32[64,224]{1,0:T(8,128)S(1)} collective-permute-done((f32[64,224]{1,0:T(8,128)S(1)}, f32[64,224]{1,0:T(8,128)S(1)}, u32[]{:S(2)}, u32[]{:S(2)}) %collective-permute-start.8) | collective-permute-done | bytes 57376 | tf_op jit(solution)/shard_map/ppermute | solution.py:27
  95.3 3.9 %collective-permute-done.9.refs_3_ = f32[64,224]{1,0:T(8,128)S(1)} collective-permute-done((f32[64,224]{1,0:T(8,128)S(1)}, f32[64,224]{1,0:T(8,128)S(1)}, u32[]{:S(2)}, u32[]{:S(2)}) %collective-permute-start.9) | collective-permute-done | bytes 57376 | tf_op jit(solution)/shard_map/ppermute | solution.py:27
  99.2 1.6 moments.1
  100.8 2.7 %collective-permute-start.16 = (bf16[2,224,128]{2,1,0:T(8,128)(2,1)S(1)}, bf16[2,224,128]{2,1,0:T(8,128)(2,1)S(1)}, u32[]{:S(2)}, u32[]{:S(2)}) collective-permute-start(bf16[2,224,128]{2,1,0:T(8,128)(2,1)S(1)} %get-tuple-element.42.u0), channel_id=1, source_target_pairs={{0,24},{8,0},{16,8},{24,16},{1,25},{9,1},{17,9},{25,17},{2,26},{10... | collective-permute-start | bytes 344072 | tf_op jit(solution)/shard_map/ppermute | solution.py:27
  103.4 3.4 %collective-permute-done.14.u1 = bf16[2,224,128]{2,1,0:T(8,128)(2,1)S(1)} collective-permute-done((bf16[2,224,128]{2,1,0:T(8,128)(2,1)S(1)}, bf16[2,224,128]{2,1,0:T(8,128)(2,1)S(1)}, u32[]{:S(2)}, u32[]{:S(2)}) %collective-permute-start.14) | collective-permute-done | bytes 114720 | tf_op jit(solution)/shard_map/ppermute | solution.py:27
  107.5 2.4 %back.2 = bf16[8,224,128]{2,1,0:T(8,128)(2,1)S(1)} custom-call(s32[4]{0:T(128)S(1)} %pad_add_fusion.at_ref, bf16[2,8,128,512]{3,2,1,0:T(8,128)(2,1)S(1)} %get-tuple-element.28.basis_ref, bf16[8,2,224,128]{3,2,1,0:T(8,128)(2,1)S(1)} %all-to-all-done.2.w_ref, bf16[2,224,128]{2,1,0:T(8,128)(2,1)S(1)} %get-tuple-element.42.u0, ...), custom_call_target="tpu_custom_call" | custom-call | flops 234881024 | bytes 3145728 | tf_op jit(solution)/shard_map/back/pallas_call | solution.py:282
  109.9 16.7 %all_to_all.30 = bf16[8,224,128]{2,1,0:T(8,128)(2,1)} all-to-all(bf16[8,224,128]{2,1,0:T(8,128)(2,1)S(1)} %back.2), channel_id=1, replica_groups=mesh['x'=4,'core'=2,'y'=4,'z'=8] {'z'}, dimensions={0} | all-to-all | bytes 917504 | tf_op jit(solution)/shard_map/all_to_all | solution.py:31
  127.8 1.4 collective-permute-start.17
  132.7 2.4 %back.3 = bf16[8,224,128]{2,1,0:T(8,128)(2,1)S(1)} custom-call(s32[4]{0:T(128)S(1)} %pad_add_fusion.at_ref, bf16[2,8,128,512]{3,2,1,0:T(8,128)(2,1)S(1)} %get-tuple-element.28.basis_ref, bf16[8,2,224,128]{3,2,1,0:T(8,128)(2,1)S(1)} %all-to-all-done.2.w_ref, bf16[2,224,128]{2,1,0:T(8,128)(2,1)S(1)} %copy-done.11, bf16[2,224,128]{2,1,0:T(8,128)(2,1)S(1)} %copy-done.13, ...), custom_call_target="tpu_custom_call" | custom-call | flops 234881024 | bytes 3145728 | tf_op jit(solution)/shard_map/back/pallas_call | solution.py:282
  135.9 3.5 %all-to-all-start.4 = ((bf16[8,224,128]{2,1,0:T(8,128)(2,1)}), bf16[8,224,128]{2,1,0:T(8,128)(2,1)S(1)}, u32[]{:S(2)}, u32[]{:S(2)}) async-start(bf16[8,224,128]{2,1,0:T(8,128)(2,1)} %copy-done.4), calls=%async_computation.4 | async-start | bytes 917504 | tf_op jit(solution)/shard_map/all_to_all | solution.py:31
  139.4 1.4 collective-permute-start.19
  140.8 5.9 %collective-permute-start.25 = (bf16[128,1792]{1,0:T(8,128)(2,1)S(1)}, bf16[128,1792]{1,0:T(8,128)(2,1)S(1)}, u32[]{:S(2)}, u32[]{:S(2)}) collective-permute-start(bf16[128,1792]{1,0:T(8,128)(2,1)S(1)} %bitcast.14), channel_id=1, source_target_pairs={{0,32},{32,0},{1,33},{33,1},{2,34},{34,2},{3,35},{35,3},{4,36},{36... | collective-permute-start | bytes 1376264 | tf_op jit(solution)/shard_map/ppermute | solution.py:27
  146.8 6.7 %collective-permute-start.24 = (bf16[128,1792]{1,0:T(8,128)(2,1)S(1)}, bf16[128,1792]{1,0:T(8,128)(2,1)}, u32[]{:S(2)}, u32[]{:S(2)}) collective-permute-start(bf16[128,1792]{1,0:T(8,128)(2,1)S(1)} %collective-permute-done.19.refs_1_), channel_id=1, source_target_pairs={{0,32},{32,0},{1,33},{33,1},{2,34},{34,2},{3,35},{35,3},{4,36},{36... | collective-permute-start | bytes 1376264 | tf_op jit(solution)/shard_map/ppermute | solution.py:27
  153.5 1.6 slice.16
  157.0 1.5 collective-permute-start.20
  158.7 6.8 %all-to-all-start.5 = ((f32[8,64,224]{2,1,0:T(8,128)}), f32[8,64,224]{2,1,0:T(8,128)S(1)}, u32[]{:S(2)}, u32[]{:S(2)}) async-start(f32[8,64,224]{2,1,0:T(8,128)} %get-tuple-element.50), calls=%async_computation.5 | async-start | bytes 1048576 | tf_op jit(solution)/shard_map/all_to_all | solution.py:31
  166.3 2.7 %collective-permute-start.27 = (bf16[128,1792]{1,0:T(8,128)(2,1)S(1)}, bf16[128,1792]{1,0:T(8,128)(2,1)S(1)}, u32[]{:S(2)}, u32[]{:S(2)}) collective-permute-start(bf16[128,1792]{1,0:T(8,128)(2,1)S(1)} %bitcast.17), channel_id=1, source_target_pairs={{0,192},{64,0},{128,64},{192,128},{1,193},{65,1},{129,65},{193,129... | collective-permute-start | bytes 1376264 | tf_op jit(solution)/shard_map/ppermute | solution.py:27
  168.9 1.4 collective-permute-start.21
  172.2 1.5 place.6.refs_4_
  174.3 2.4 %place.7.refs_4_ = bf16[2,128,14336]{2,1,0:T(8,128)(2,1)} custom-call(s32[4]{0:T(128)S(1)} %pad_add_fusion.at_ref, bf16[128,1792]{1,0:T(8,128)(2,1)} %collective-permute-done.17.refs_0_, bf16[128,1792]{1,0:T(8,128)(2,1)S(1)} %collective-permute-done.19.refs_1_, bf16[128,1792]{1,0:T(8,128)(2,1)S(1)} %copy-done.7, ...), custom_call_target="tpu_custom_call", output_to_operand_aliasing={{}: (5, {})} | custom-call | flops 2000000000 | bytes 3670016 | tf_op jit(solution)/shard_map/place/pallas_call | solution.py:320
  176.7 2.0 %place.8.refs_2_ = bf16[2,128,14336]{2,1,0:T(8,128)(2,1)} custom-call(s32[4]{0:T(128)S(1)} %pad_add_fusion.at_ref, bf16[64,1792]{1,0:T(8,128)(2,1)} %collective-permute-done.18.refs_0_, bf16[64,1792]{1,0:T(8,128)(2,1)} %collective-permute-done.20.refs_1_, bf16[64,1792]{1,0:T(8,128)(2,1)S(1)} %collective-permute-done.21.refs_2_, ...), custom_call_target="tpu_custom_call", output_to_operand_aliasing={{}: (5, {})} | custom-call | flops 2000000000 | bytes 1835008 | tf_op jit(solution)/shard_map/place/pallas_call | solution.py:320
  178.8 1.6 collective-permute-start.28
  180.6 2.8 %collective-permute-start.32 = (bf16[64,1792]{1,0:T(8,128)(2,1)S(1)}, bf16[64,1792]{1,0:T(8,128)(2,1)S(1)}, u32[]{:S(2)}, u32[]{:S(2)}) collective-permute-start(bf16[64,1792]{1,0:T(8,128)(2,1)S(1)} %slice.15), channel_id=1, source_target_pairs={{0,192},{64,0},{128,64},{192,128},{1,193},{65,1},{129,65},{193,129... | collective-permute-start | bytes 688136 | tf_op jit(solution)/shard_map/ppermute | solution.py:27
  183.3 1.5 place.9.refs_4_
  184.8 1.8 place.10.refs_4_
  186.6 1.8 collective-permute-done.31.refs_0_
  188.4 1.4 collective-permute-start.33
  191.3 1.5 place.11
  (105 shorter events, 23.5 us)
Async XLA Ops:
  2.8 10.4 %copy-start.19 = (bf16[2,128,1792]{2,1,0:T(8,128)(2,1)S(1)}, bf16[2,128,1792]{2,1,0:T(8,128)(2,1)}, u32[]{:S(2)}) copy-start(bf16[2,128,1792]{2,1,0:T(8,128)(2,1)} %v_ref.4) | copy-start | bytes 2752516
  4.3 20.3 %all-to-all-start.1 = ((bf16[8,144,128]{2,1,0:T(8,128)(2,1)}), bf16[8,144,128]{2,1,0:T(8,128)(2,1)S(1)}, u32[]{:S(2)}, u32[]{:S(2)}) async-start(bf16[8,144,128]{2,1,0:T(8,128)(2,1)} %pieces.1), calls=%async_computation.1 | async-start | bytes 589824 | tf_op jit(solution)/shard_map/all_to_all | solution.py:31
  24.5 28.2 %all-to-all-start = ((bf16[8,2,224,128]{3,2,1,0:T(8,128)(2,1)}), bf16[8,2,224,128]{3,2,1,0:T(8,128)(2,1)S(1)}, u32[]{:S(2)}, u32[]{:S(2)}) async-start(bf16[8,2,224,128]{3,2,1,0:T(8,128)(2,1)} %pack.2), calls=%async_computation | async-start | bytes 1835008 | tf_op jit(solution)/shard_map/all_to_all | solution.py:31
  28.1 7.6 %collective-permute-start = (bf16[8,144,128]{2,1,0:T(8,128)(2,1)S(1)}, bf16[8,144,128]{2,1,0:T(8,128)(2,1)S(1)}, u32[]{:S(2)}, u32[]{:S(2)}) collective-permute-start(bf16[8,144,128]{2,1,0:T(8,128)(2,1)S(1)} %all-to-all-done.1), channel_id=1, source_target_pairs={{0,64},{64,128},{128,192},{192,0},{1,65},{65,129},{129,193},{193,1... | collective-permute-start | bytes 884744 | tf_op jit(solution)/shard_map/ppermute | solution.py:27
  29.4 13.6 %collective-permute-start.1 = (bf16[8,144,128]{2,1,0:T(8,128)(2,1)S(1)}, bf16[8,144,128]{2,1,0:T(8,128)(2,1)S(1)}, u32[]{:S(2)}, u32[]{:S(2)}) collective-permute-start(bf16[8,144,128]{2,1,0:T(8,128)(2,1)S(1)} %all-to-all-done.1), channel_id=1, source_target_pairs={{0,128},{64,192},{128,0},{192,64},{1,129},{65,193},{129,1},{193,65... | collective-permute-start | bytes 884744 | tf_op jit(solution)/shard_map/ppermute | solution.py:27
  31.8 11.5 %collective-permute-start.2 = (bf16[8,144,128]{2,1,0:T(8,128)(2,1)S(1)}, bf16[8,144,128]{2,1,0:T(8,128)(2,1)S(1)}, u32[]{:S(2)}, u32[]{:S(2)}) collective-permute-start(bf16[8,144,128]{2,1,0:T(8,128)(2,1)S(1)} %all-to-all-done.1), channel_id=1, source_target_pairs={{0,192},{64,0},{128,64},{192,128},{1,193},{65,1},{129,65},{193,129... | collective-permute-start | bytes 884744 | tf_op jit(solution)/shard_map/ppermute | solution.py:27
  43.5 3.1 %copy-start = (bf16[4,8,144,128]{3,2,1,0:T(8,128)(2,1)}, bf16[4,8,144,128]{3,2,1,0:T(8,128)(2,1)S(1)}, u32[]{:S(2)}) copy-start(bf16[4,8,144,128]{3,2,1,0:T(8,128)(2,1)S(1)} %pad_maximum_fusion.own_ref) | copy-start | bytes 3538948
  43.5 12.8 %collective-permute-start.3 = (bf16[4,8,144,128]{3,2,1,0:T(8,128)(2,1)S(1)}, bf16[4,8,144,128]{3,2,1,0:T(8,128)(2,1)}, u32[]{:S(2)}, u32[]{:S(2)}) collective-permute-start(bf16[4,8,144,128]{3,2,1,0:T(8,128)(2,1)S(1)} %pad_maximum_fusion.own_ref), channel_id=1, source_target_pairs={{0,32},{32,0},{1,33},{33,1},{2,34},{34,2},{3,35},{35,3},{4,36},{36... | collective-permute-start | bytes 3538952 | tf_op jit(solution)/shard_map/ppermute | solution.py:27
  52.8 3.6 %copy-start.2 = (bf16[8,2,224,128]{3,2,1,0:T(8,128)(2,1)}, bf16[8,2,224,128]{3,2,1,0:T(8,128)(2,1)S(1)}, u32[]{:S(2)}) copy-start(bf16[8,2,224,128]{3,2,1,0:T(8,128)(2,1)S(1)} %all-to-all-done.g_ref) | copy-start | bytes 2752516
  52.8 54.7 %all-to-all-start.2 = ((bf16[8,2,224,128]{3,2,1,0:T(8,128)(2,1)}), bf16[8,2,224,128]{3,2,1,0:T(8,128)(2,1)S(1)}, u32[]{:S(2)}, u32[]{:S(2)}) async-start(bf16[8,2,224,128]{3,2,1,0:T(8,128)(2,1)} %copy-done.5), calls=%async_computation.2 | async-start | bytes 1835008 | tf_op jit(solution)/shard_map/all_to_all | solution.py:31
  58.8 7.8 %copy-start.22 = (f32[2,16,1792]{2,1,0:T(8,128)S(1)}, f32[2,16,1792]{2,1,0:T(8,128)}, u32[]{:S(2)}) copy-start(f32[2,16,1792]{2,1,0:T(8,128)} %one_ref.1) | copy-start | bytes 688132
  58.8 7.8 %copy-start.23 = (f32[2,16,1792]{2,1,0:T(8,128)S(1)}, f32[2,16,1792]{2,1,0:T(8,128)}, u32[]{:S(2)}) copy-start(f32[2,16,1792]{2,1,0:T(8,128)} %two_ref.1) | copy-start | bytes 688132
  61.6 25.2 %collective-permute-start.4 = (f32[2,232,128]{2,1,0:T(8,128)S(1)}, f32[2,232,128]{2,1,0:T(8,128)S(1)}, u32[]{:S(2)}, u32[]{:S(2)}) collective-permute-start(f32[2,232,128]{2,1,0:T(8,128)S(1)} %get-tuple-element.31), channel_id=1, source_target_pairs={{0,8},{8,16},{16,24},{24,0},{1,9},{9,17},{17,25},{25,1},{2,10},{10... | collective-permute-start | bytes 712712 | tf_op jit(solution)/shard_map/ppermute | solution.py:27
  62.9 26.7 %collective-permute-start.5 = (f32[2,232,128]{2,1,0:T(8,128)S(1)}, f32[2,232,128]{2,1,0:T(8,128)S(1)}, u32[]{:S(2)}, u32[]{:S(2)}) collective-permute-start(f32[2,232,128]{2,1,0:T(8,128)S(1)} %get-tuple-element.32), channel_id=1, source_target_pairs={{0,16},{8,24},{16,0},{24,8},{1,17},{9,25},{17,1},{25,9},{2,18},{10... | collective-permute-start | bytes 712712 | tf_op jit(solution)/shard_map/ppermute | solution.py:27
  65.6 25.3 %collective-permute-start.6 = (f32[2,232,128]{2,1,0:T(8,128)S(1)}, f32[2,232,128]{2,1,0:T(8,128)S(1)}, u32[]{:S(2)}, u32[]{:S(2)}) collective-permute-start(f32[2,232,128]{2,1,0:T(8,128)S(1)} %get-tuple-element.33), channel_id=1, source_target_pairs={{0,24},{8,0},{16,8},{24,16},{1,25},{9,1},{17,9},{25,17},{2,26},{10... | collective-permute-start | bytes 712712 | tf_op jit(solution)/shard_map/ppermute | solution.py:27
  67.4 16.8 %collective-permute-start.10 = (f32[64,224]{1,0:T(8,128)S(1)}, f32[64,224]{1,0:T(8,128)S(1)}, u32[]{:S(2)}, u32[]{:S(2)}) collective-permute-start(f32[64,224]{1,0:T(8,128)S(1)} %get-tuple-element.38), channel_id=1, source_target_pairs={{0,4},{1,5},{2,6},{3,7},{4,0},{5,1},{6,2},{7,3},{8,12},{9,13},{10,... | collective-permute-start | bytes 172040 | tf_op jit(solution)/shard_map/ppermute | solution.py:27
  72.8 11.5 %collective-permute-start.11 = (f32[64,224]{1,0:T(8,128)S(1)}, f32[64,224]{1,0:T(8,128)S(1)}, u32[]{:S(2)}, u32[]{:S(2)}) collective-permute-start(f32[64,224]{1,0:T(8,128)S(1)} %get-tuple-element.39), channel_id=1, source_target_pairs={{0,5},{1,6},{2,7},{3,0},{4,1},{5,2},{6,3},{7,4},{8,13},{9,14},{10,... | collective-permute-start | bytes 172040 | tf_op jit(solution)/shard_map/ppermute | solution.py:27
  84.2 6.7 %collective-permute-start.12 = (f32[64,224]{1,0:T(8,128)S(1)}, f32[64,224]{1,0:T(8,128)S(1)}, u32[]{:S(2)}, u32[]{:S(2)}) collective-permute-start(f32[64,224]{1,0:T(8,128)S(1)} %get-tuple-element.40), channel_id=1, source_target_pairs={{0,6},{1,7},{2,0},{3,1},{4,2},{5,3},{6,4},{7,5},{8,14},{9,15},{10,... | collective-permute-start | bytes 172040 | tf_op jit(solution)/shard_map/ppermute | solution.py:27
  84.2 7.3 %collective-permute-start.13 = (f32[64,224]{1,0:T(8,128)S(1)}, f32[64,224]{1,0:T(8,128)S(1)}, u32[]{:S(2)}, u32[]{:S(2)}) collective-permute-start(f32[64,224]{1,0:T(8,128)S(1)} %get-tuple-element.41), channel_id=1, source_target_pairs={{0,7},{1,0},{2,1},{3,2},{4,3},{5,4},{6,5},{7,6},{8,15},{9,8},{10,9... | collective-permute-start | bytes 172040 | tf_op jit(solution)/shard_map/ppermute | solution.py:27
  86.8 4.7 %collective-permute-start.7 = (f32[64,224]{1,0:T(8,128)S(1)}, f32[64,224]{1,0:T(8,128)S(1)}, u32[]{:S(2)}, u32[]{:S(2)}) collective-permute-start(f32[64,224]{1,0:T(8,128)S(1)} %get-tuple-element.35), channel_id=1, source_target_pairs={{0,1},{1,2},{2,3},{3,4},{4,5},{5,6},{6,7},{7,0},{8,9},{9,10},{10,1... | collective-permute-start | bytes 172040 | tf_op jit(solution)/shard_map/ppermute | solution.py:27
  89.6 5.7 %collective-permute-start.8 = (f32[64,224]{1,0:T(8,128)S(1)}, f32[64,224]{1,0:T(8,128)S(1)}, u32[]{:S(2)}, u32[]{:S(2)}) collective-permute-start(f32[64,224]{1,0:T(8,128)S(1)} %get-tuple-element.36), channel_id=1, source_target_pairs={{0,2},{1,3},{2,4},{3,5},{4,6},{5,7},{6,0},{7,1},{8,10},{9,11},{10,... | collective-permute-start | bytes 172040 | tf_op jit(solution)/shard_map/ppermute | solution.py:27
  90.9 8.3 %collective-permute-start.9 = (f32[64,224]{1,0:T(8,128)S(1)}, f32[64,224]{1,0:T(8,128)S(1)}, u32[]{:S(2)}, u32[]{:S(2)}) collective-permute-start(f32[64,224]{1,0:T(8,128)S(1)} %get-tuple-element.37), channel_id=1, source_target_pairs={{0,3},{1,4},{2,5},{3,6},{4,7},{5,0},{6,1},{7,2},{8,11},{9,12},{10,... | collective-permute-start | bytes 172040 | tf_op jit(solution)/shard_map/ppermute | solution.py:27
  100.7 9.1 %copy-start.10 = (bf16[2,224,128]{2,1,0:T(8,128)(2,1)}, bf16[2,224,128]{2,1,0:T(8,128)(2,1)S(1)}, u32[]{:S(2)}) copy-start(bf16[2,224,128]{2,1,0:T(8,128)(2,1)S(1)} %get-tuple-element.42.u0) | copy-start | bytes 344068
  100.7 6.1 %collective-permute-start.14 = (bf16[2,224,128]{2,1,0:T(8,128)(2,1)S(1)}, bf16[2,224,128]{2,1,0:T(8,128)(2,1)S(1)}, u32[]{:S(2)}, u32[]{:S(2)}) collective-permute-start(bf16[2,224,128]{2,1,0:T(8,128)(2,1)S(1)} %get-tuple-element.42.u0), channel_id=1, source_target_pairs={{0,8},{8,16},{16,24},{24,0},{1,9},{9,17},{17,25},{25,1},{2,10},{10... | collective-permute-start | bytes 344072 | tf_op jit(solution)/shard_map/ppermute | solution.py:27
  100.7 6.1 %collective-permute-start.15 = (bf16[2,224,128]{2,1,0:T(8,128)(2,1)S(1)}, bf16[2,224,128]{2,1,0:T(8,128)(2,1)S(1)}, u32[]{:S(2)}, u32[]{:S(2)}) collective-permute-start(bf16[2,224,128]{2,1,0:T(8,128)(2,1)S(1)} %get-tuple-element.42.u0), channel_id=1, source_target_pairs={{0,16},{8,24},{16,0},{24,8},{1,17},{9,25},{17,1},{25,9},{2,18},{10... | collective-permute-start | bytes 344072 | tf_op jit(solution)/shard_map/ppermute | solution.py:27
  100.8 6.7 %collective-permute-start.16 = (bf16[2,224,128]{2,1,0:T(8,128)(2,1)S(1)}, bf16[2,224,128]{2,1,0:T(8,128)(2,1)S(1)}, u32[]{:S(2)}, u32[]{:S(2)}) collective-permute-start(bf16[2,224,128]{2,1,0:T(8,128)(2,1)S(1)} %get-tuple-element.42.u0), channel_id=1, source_target_pairs={{0,24},{8,0},{16,8},{24,16},{1,25},{9,1},{17,9},{25,17},{2,26},{10... | collective-permute-start | bytes 344072 | tf_op jit(solution)/shard_map/ppermute | solution.py:27
  106.8 3.0 %copy-start.12 = (bf16[2,224,128]{2,1,0:T(8,128)(2,1)}, bf16[2,224,128]{2,1,0:T(8,128)(2,1)S(1)}, u32[]{:S(2)}) copy-start(bf16[2,224,128]{2,1,0:T(8,128)(2,1)S(1)} %collective-permute-done.14.u1) | copy-start | bytes 344068
  106.8 3.0 %copy-start.14 = (bf16[2,224,128]{2,1,0:T(8,128)(2,1)}, bf16[2,224,128]{2,1,0:T(8,128)(2,1)S(1)}, u32[]{:S(2)}) copy-start(bf16[2,224,128]{2,1,0:T(8,128)(2,1)S(1)} %collective-permute-done.15.u2) | copy-start | bytes 344068
  127.8 18.9 %collective-permute-start.17 = (bf16[128,1792]{1,0:T(8,128)(2,1)S(1)}, bf16[128,1792]{1,0:T(8,128)(2,1)}, u32[]{:S(2)}, u32[]{:S(2)}) collective-permute-start(bf16[128,1792]{1,0:T(8,128)(2,1)S(1)} %bitcast.12), channel_id=1, source_target_pairs={{0,64},{64,128},{128,192},{192,0},{1,65},{65,129},{129,193},{193,1... | collective-permute-start | bytes 1376264 | tf_op jit(solution)/shard_map/ppermute | solution.py:27
  135.9 22.6 %all-to-all-start.4 = ((bf16[8,224,128]{2,1,0:T(8,128)(2,1)}), bf16[8,224,128]{2,1,0:T(8,128)(2,1)S(1)}, u32[]{:S(2)}, u32[]{:S(2)}) async-start(bf16[8,224,128]{2,1,0:T(8,128)(2,1)} %copy-done.4), calls=%async_computation.4 | async-start | bytes 917504 | tf_op jit(solution)/shard_map/all_to_all | solution.py:31
  139.4 7.4 %collective-permute-start.19 = (bf16[128,1792]{1,0:T(8,128)(2,1)S(1)}, bf16[128,1792]{1,0:T(8,128)(2,1)S(1)}, u32[]{:S(2)}, u32[]{:S(2)}) collective-permute-start(bf16[128,1792]{1,0:T(8,128)(2,1)S(1)} %bitcast.13), channel_id=1, source_target_pairs={{0,192},{64,0},{128,64},{192,128},{1,193},{65,1},{129,65},{193,129... | collective-permute-start | bytes 1376264 | tf_op jit(solution)/shard_map/ppermute | solution.py:27
  140.8 24.6 %collective-permute-start.25 = (bf16[128,1792]{1,0:T(8,128)(2,1)S(1)}, bf16[128,1792]{1,0:T(8,128)(2,1)S(1)}, u32[]{:S(2)}, u32[]{:S(2)}) collective-permute-start(bf16[128,1792]{1,0:T(8,128)(2,1)S(1)} %bitcast.14), channel_id=1, source_target_pairs={{0,32},{32,0},{1,33},{33,1},{2,34},{34,2},{3,35},{35,3},{4,36},{36... | collective-permute-start | bytes 1376264 | tf_op jit(solution)/shard_map/ppermute | solution.py:27
  146.7 23.6 %collective-permute-start.23 = (bf16[128,1792]{1,0:T(8,128)(2,1)}, bf16[128,1792]{1,0:T(8,128)(2,1)S(1)}, u32[]{:S(2)}, u32[]{:S(2)}) collective-permute-start(bf16[128,1792]{1,0:T(8,128)(2,1)} %collective-permute-done.17.refs_0_), channel_id=1, source_target_pairs={{0,32},{32,0},{1,33},{33,1},{2,34},{34,2},{3,35},{35,3},{4,36},{36... | collective-permute-start | bytes 1376264 | tf_op jit(solution)/shard_map/ppermute | solution.py:27
  146.8 26.9 %collective-permute-start.24 = (bf16[128,1792]{1,0:T(8,128)(2,1)S(1)}, bf16[128,1792]{1,0:T(8,128)(2,1)}, u32[]{:S(2)}, u32[]{:S(2)}) collective-permute-start(bf16[128,1792]{1,0:T(8,128)(2,1)S(1)} %collective-permute-done.19.refs_1_), channel_id=1, source_target_pairs={{0,32},{32,0},{1,33},{33,1},{2,34},{34,2},{3,35},{35,3},{4,36},{36... | collective-permute-start | bytes 1376264 | tf_op jit(solution)/shard_map/ppermute | solution.py:27
  155.1 11.2 %collective-permute-start.18 = (bf16[64,1792]{1,0:T(8,128)(2,1)}, bf16[64,1792]{1,0:T(8,128)(2,1)}, u32[]{:S(2)}, u32[]{:S(2)}) collective-permute-start(bf16[64,1792]{1,0:T(8,128)(2,1)} %slice.16), channel_id=1, source_target_pairs={{0,64},{64,128},{128,192},{192,0},{1,65},{65,129},{129,193},{193,1... | collective-permute-start | bytes 688136 | tf_op jit(solution)/shard_map/ppermute | solution.py:27
  157.0 11.9 %collective-permute-start.20 = (bf16[64,1792]{1,0:T(8,128)(2,1)}, bf16[64,1792]{1,0:T(8,128)(2,1)}, u32[]{:S(2)}, u32[]{:S(2)}) collective-permute-start(bf16[64,1792]{1,0:T(8,128)(2,1)} %slice.17), channel_id=1, source_target_pairs={{0,192},{64,0},{128,64},{192,128},{1,193},{65,1},{129,65},{193,129... | collective-permute-start | bytes 688136 | tf_op jit(solution)/shard_map/ppermute | solution.py:27
  158.7 31.1 %all-to-all-start.5 = ((f32[8,64,224]{2,1,0:T(8,128)}), f32[8,64,224]{2,1,0:T(8,128)S(1)}, u32[]{:S(2)}, u32[]{:S(2)}) async-start(f32[8,64,224]{2,1,0:T(8,128)} %get-tuple-element.50), calls=%async_computation.5 | async-start | bytes 1048576 | tf_op jit(solution)/shard_map/all_to_all | solution.py:31
  166.3 12.5 %collective-permute-start.26 = (bf16[128,1792]{1,0:T(8,128)(2,1)S(1)}, bf16[128,1792]{1,0:T(8,128)(2,1)S(1)}, u32[]{:S(2)}, u32[]{:S(2)}) collective-permute-start(bf16[128,1792]{1,0:T(8,128)(2,1)S(1)} %bitcast.16), channel_id=1, source_target_pairs={{0,64},{64,128},{128,192},{192,0},{1,65},{65,129},{129,193},{193,1... | collective-permute-start | bytes 1376264 | tf_op jit(solution)/shard_map/ppermute | solution.py:27
  166.3 12.5 %collective-permute-start.27 = (bf16[128,1792]{1,0:T(8,128)(2,1)S(1)}, bf16[128,1792]{1,0:T(8,128)(2,1)S(1)}, u32[]{:S(2)}, u32[]{:S(2)}) collective-permute-start(bf16[128,1792]{1,0:T(8,128)(2,1)S(1)} %bitcast.17), channel_id=1, source_target_pairs={{0,192},{64,0},{128,64},{192,128},{1,193},{65,1},{129,65},{193,129... | collective-permute-start | bytes 1376264 | tf_op jit(solution)/shard_map/ppermute | solution.py:27
  168.9 7.8 %collective-permute-start.21 = (bf16[64,1792]{1,0:T(8,128)(2,1)}, bf16[64,1792]{1,0:T(8,128)(2,1)S(1)}, u32[]{:S(2)}, u32[]{:S(2)}) collective-permute-start(bf16[64,1792]{1,0:T(8,128)(2,1)} %collective-permute-done.18.refs_0_), channel_id=1, source_target_pairs={{0,32},{32,0},{1,33},{33,1},{2,34},{34,2},{3,35},{35,3},{4,36},{36... | collective-permute-start | bytes 688136 | tf_op jit(solution)/shard_map/ppermute | solution.py:27
  171.1 5.6 %collective-permute-start.22 = (bf16[64,1792]{1,0:T(8,128)(2,1)}, bf16[64,1792]{1,0:T(8,128)(2,1)S(1)}, u32[]{:S(2)}, u32[]{:S(2)}) collective-permute-start(bf16[64,1792]{1,0:T(8,128)(2,1)} %collective-permute-done.20.refs_1_), channel_id=1, source_target_pairs={{0,32},{32,0},{1,33},{33,1},{2,34},{34,2},{3,35},{35,3},{4,36},{36... | collective-permute-start | bytes 688136 | tf_op jit(solution)/shard_map/ppermute | solution.py:27
  173.7 9.6 %collective-permute-start.30 = (bf16[128,1792]{1,0:T(8,128)(2,1)S(1)}, bf16[128,1792]{1,0:T(8,128)(2,1)S(1)}, u32[]{:S(2)}, u32[]{:S(2)}) collective-permute-start(bf16[128,1792]{1,0:T(8,128)(2,1)S(1)} %bitcast.18), channel_id=1, source_target_pairs={{0,32},{32,0},{1,33},{33,1},{2,34},{34,2},{3,35},{35,3},{4,36},{36... | collective-permute-start | bytes 1376264 | tf_op jit(solution)/shard_map/ppermute | solution.py:27
  178.8 6.0 %collective-permute-start.28 = (bf16[128,1792]{1,0:T(8,128)(2,1)S(1)}, bf16[128,1792]{1,0:T(8,128)(2,1)S(1)}, u32[]{:S(2)}, u32[]{:S(2)}) collective-permute-start(bf16[128,1792]{1,0:T(8,128)(2,1)S(1)} %collective-permute-done.26.refs_0_), channel_id=1, source_target_pairs={{0,32},{32,0},{1,33},{33,1},{2,34},{34,2},{3,35},{35,3},{4,36},{36... | collective-permute-start | bytes 1376264 | tf_op jit(solution)/shard_map/ppermute | solution.py:27
  180.4 4.4 %collective-permute-start.29 = (bf16[128,1792]{1,0:T(8,128)(2,1)S(1)}, bf16[128,1792]{1,0:T(8,128)(2,1)S(1)}, u32[]{:S(2)}, u32[]{:S(2)}) collective-permute-start(bf16[128,1792]{1,0:T(8,128)(2,1)S(1)} %collective-permute-done.27.refs_1_), channel_id=1, source_target_pairs={{0,32},{32,0},{1,33},{33,1},{2,34},{34,2},{3,35},{35,3},{4,36},{36... | collective-permute-start | bytes 1376264 | tf_op jit(solution)/shard_map/ppermute | solution.py:27
  180.5 8.0 %collective-permute-start.31 = (bf16[64,1792]{1,0:T(8,128)(2,1)S(1)}, bf16[64,1792]{1,0:T(8,128)(2,1)S(1)}, u32[]{:S(2)}, u32[]{:S(2)}) collective-permute-start(bf16[64,1792]{1,0:T(8,128)(2,1)S(1)} %slice.14), channel_id=1, source_target_pairs={{0,64},{64,128},{128,192},{192,0},{1,65},{65,129},{129,193},{193,1... | collective-permute-start | bytes 688136 | tf_op jit(solution)/shard_map/ppermute | solution.py:27
  180.6 7.9 %collective-permute-start.32 = (bf16[64,1792]{1,0:T(8,128)(2,1)S(1)}, bf16[64,1792]{1,0:T(8,128)(2,1)S(1)}, u32[]{:S(2)}, u32[]{:S(2)}) collective-permute-start(bf16[64,1792]{1,0:T(8,128)(2,1)S(1)} %slice.15), channel_id=1, source_target_pairs={{0,192},{64,0},{128,64},{192,128},{1,193},{65,1},{129,65},{193,129... | collective-permute-start | bytes 688136 | tf_op jit(solution)/shard_map/ppermute | solution.py:27
  188.4 2.5 %collective-permute-start.33 = (bf16[64,1792]{1,0:T(8,128)(2,1)S(1)}, bf16[64,1792]{1,0:T(8,128)(2,1)S(1)}, u32[]{:S(2)}, u32[]{:S(2)}) collective-permute-start(bf16[64,1792]{1,0:T(8,128)(2,1)S(1)} %collective-permute-done.31.refs_0_), channel_id=1, source_target_pairs={{0,32},{32,0},{1,33},{33,1},{2,34},{34,2},{3,35},{35,3},{4,36},{36... | collective-permute-start | bytes 688136 | tf_op jit(solution)/shard_map/ppermute | solution.py:27
  189.8 1.5 collective-permute-start.34
  (16 other events, 20.0 us)
